TPU v7x, 32 devices: a whole 2x2x4 slice. The times are simulated.
32 devices in a mesh: dp: 8 (over y, x, core), mp: 4 (over z).
Axes of the slice: x: 2, y: 2, z: 4, core: 2. Of those that a mesh axis runs over, the one named last changes fastest.
Arguments:
- hidden: bfloat16 [8192, 2048], P('dp'), may hold values from -6 to 6
- cotangent: bfloat16 [8192, 2048], P('dp'), may hold values from -6 to 6
- lengths: int32 [16], P('dp'), may hold values from 64 to 512, as said below
- input_gain: bfloat16 [2048], P('dp'), may hold values from 0.5 to 1.5
- input_shift: bfloat16 [2048], P('dp'), may hold values from -1.25 to 1.25
- triple_weight: bfloat16 [2048, 3, 2048], P('dp', None, 'mp'), may hold values from -0.125 to 0.125
- triple_bias: bfloat16 [2, 2048], P(None, 'mp'), may hold values from -1.25 to 1.25
- merge_weight: bfloat16 [2048, 2048], P('mp', 'dp'), may hold values from -0.5 to 0.5
- merge_bias: bfloat16 [2048], P('dp'), may hold values from -1.25 to 1.25
- middle_gain: bfloat16 [2048], P('dp'), may hold values from 0.5 to 1.5
- middle_shift: bfloat16 [2048], P('dp'), may hold values from -1.25 to 1.25
- expand_weight: bfloat16 [2048, 8192], P('dp', 'mp'), may hold values from -0.125 to 0.125
- expand_bias: bfloat16 [8192], P('mp'), may hold values from -1.25 to 1.25
- reduce_weight: bfloat16 [8192, 2048], P('mp', 'dp'), may hold values from -0.0625 to 0.0625
- reduce_bias: bfloat16 [2048], P('dp'), may hold values from -1.25 to 1.25
Outputs:
- layer_output: bfloat16 [8192, 2048], P('dp')
- hidden_grad: bfloat16 [8192, 2048], P('dp')
- input_gain_grad: float32 [2048], P('dp')
- input_shift_grad: float32 [2048], P('dp')
- triple_weight_grad: float32 [2048, 3, 2048], P('dp', None, 'mp')
- triple_bias_grad: float32 [2, 2048], P(None, 'mp')
- merge_weight_grad: float32 [2048, 2048], P('mp', 'dp')
- merge_bias_grad: float32 [2048], P('dp')
- middle_gain_grad: float32 [2048], P('dp')
- middle_shift_grad: float32 [2048], P('dp')
- expand_weight_grad: float32 [2048, 8192], P('dp', 'mp')
- expand_bias_grad: float32 [8192], P('mp')
- reduce_weight_grad: float32 [8192, 2048], P('mp', 'dp')
- reduce_bias_grad: float32 [2048], P('dp')
- branch_rms: float32 [3], replicated
Inputs may be any that keep to these rules, and one draw needn't show every extreme that they name: `lengths`: each slot's valid tokens stand at its start; in every draw some slot is full (512 valid tokens).
All inputs are finite; a program needn't handle non-finite values.
Results may differ from a plain program's by a relative error of at most 0.023.
Values may be sent and summed in bfloat16 or wider, within the bound.
A program may use at most 256 MiB of HBM per device.

v0:
```python
import jax
import jax.numpy as jnp
from jax import lax
from jax.sharding import PartitionSpec as P

HEADS = 32
HEAD_DIM = 64
SLOT = 512
MICRO = 2


def layer_norm(values, gain_vec, shift_vec):
    center = values - jnp.mean(values, axis=-1, keepdims=True)
    spread = jnp.mean(center * center, axis=-1, keepdims=True)
    return center * lax.rsqrt(spread + 1e-05) * gain_vec + shift_vec


def gelu_exact(values):
    return jax.nn.gelu(values, approximate=False)


def attention_scores(query_low, key_low, slopes, length):
    raw_scores = jnp.einsum("qhe,khe->hqk", query_low, key_low, preferred_element_type=jnp.float32)
    places = jnp.arange(query_low.shape[0], dtype=jnp.int32)
    key_place = places.astype(jnp.float32)
    scores = (raw_scores + slopes[:, None, None] * key_place[None, None, :]) * 0.125
    allowed = (places[None, :] <= places[:, None]) & (places[None, :] < length)
    return jnp.where(allowed[None], scores, -1000000000.0)


def local(
    hidden,
    cotangent,
    lengths,
    input_gain,
    input_shift,
    triple_weight,
    triple_bias,
    merge_weight,
    merge_bias,
    middle_gain,
    middle_shift,
    expand_weight,
    expand_bias,
    reduce_weight,
    reduce_bias,
):
    slot = SLOT
    width = hidden.shape[1]
    head_cols = triple_weight.shape[2]
    unit_cols = expand_weight.shape[1]
    local_heads = head_cols // HEAD_DIM
    head_start = lax.axis_index("mp") * local_heads
    slopes = 2.0 ** (
        -8.0
        * (head_start + jnp.arange(local_heads, dtype=jnp.int32) + 1).astype(jnp.float32)
        / HEADS
    )
    bias_pair = triple_bias.astype(jnp.float32)
    unit_shift = expand_bias.astype(jnp.float32)
    attention_kept = (
        lax.all_gather(input_gain, "dp", axis=0, tiled=True),
        lax.all_gather(input_shift, "dp", axis=0, tiled=True),
        lax.all_gather(triple_weight, "dp", axis=0, tiled=True),
        lax.all_gather(merge_weight, "dp", axis=1, tiled=True),
        lax.all_gather(merge_bias, "dp", axis=0, tiled=True),
    )
    feed_kept = (
        lax.all_gather(middle_gain, "dp", axis=0, tiled=True),
        lax.all_gather(middle_shift, "dp", axis=0, tiled=True),
        lax.all_gather(expand_weight, "dp", axis=0, tiled=True),
        lax.all_gather(reduce_weight, "dp", axis=1, tiled=True),
        lax.all_gather(reduce_bias, "dp", axis=0, tiled=True),
    )
    acc_triple = jnp.zeros((width, 3, head_cols), jnp.float32)
    acc_merge = jnp.zeros((head_cols, width), jnp.float32)
    acc_expand = jnp.zeros((width, unit_cols), jnp.float32)
    acc_reduce = jnp.zeros((unit_cols, width), jnp.float32)
    acc_gain_one = jnp.zeros((width,), jnp.float32)
    acc_shift_one = jnp.zeros((width,), jnp.float32)
    acc_merge_bias = jnp.zeros((width,), jnp.float32)
    acc_gain_two = jnp.zeros((width,), jnp.float32)
    acc_shift_two = jnp.zeros((width,), jnp.float32)
    acc_reduce_bias = jnp.zeros((width,), jnp.float32)
    acc_pair_bias = jnp.zeros((2, head_cols), jnp.float32)
    acc_unit_bias = jnp.zeros((unit_cols,), jnp.float32)
    square_sums = jnp.zeros((4,), jnp.float32)
    output_parts = []
    grad_parts = []
    for batch_index in range(MICRO):
        start = batch_index * slot
        token_rows = hidden[start : start + slot].astype(jnp.float32)
        length = lengths[batch_index]
        valid_rows = (jnp.arange(slot, dtype=jnp.int32) < length)[:, None]
        gain_one, shift_one, triple_full, merge_full, merge_shift = attention_kept
        gain_two, shift_two, expand_full, reduce_full, reduce_shift = feed_kept
        gain_one = gain_one.astype(jnp.float32)
        shift_one = shift_one.astype(jnp.float32)
        gain_two = gain_two.astype(jnp.float32)
        shift_two = shift_two.astype(jnp.float32)
        norm_in = layer_norm(token_rows, gain_one, shift_one).astype(jnp.bfloat16)
        triple = jnp.einsum("td,dcf->tcf", norm_in, triple_full, preferred_element_type=jnp.float32)
        query_low = (
            (triple[:, 0] + bias_pair[0]).astype(jnp.bfloat16).reshape(slot, local_heads, HEAD_DIM)
        )
        key_low = triple[:, 1].astype(jnp.bfloat16).reshape(slot, local_heads, HEAD_DIM)
        value_low = (
            (triple[:, 2] + bias_pair[1]).astype(jnp.bfloat16).reshape(slot, local_heads, HEAD_DIM)
        )
        scores = attention_scores(query_low, key_low, slopes, length)
        log_total = jax.nn.logsumexp(scores, axis=-1)
        attention_weights = jnp.exp(scores - log_total[..., None]).astype(jnp.bfloat16)
        mixed_heads = jnp.einsum(
            "hqk,khe->qhe", attention_weights, value_low, preferred_element_type=jnp.float32
        )
        mixed_heads = mixed_heads.reshape(slot, head_cols).astype(jnp.bfloat16)
        attention_part = jnp.dot(mixed_heads, merge_full, preferred_element_type=jnp.float32)
        attention_branch = lax.psum(attention_part.astype(jnp.bfloat16), "mp").astype(
            jnp.float32
        ) + merge_shift.astype(jnp.float32)
        residual = token_rows + attention_branch
        norm_mid = layer_norm(residual, gain_two, shift_two).astype(jnp.bfloat16)
        token_count = length.astype(jnp.float32)
        expand_pre = jnp.dot(norm_mid, expand_full, preferred_element_type=jnp.float32) + unit_shift
        activation = gelu_exact(expand_pre).astype(jnp.bfloat16)
        feed_part = jnp.dot(activation, reduce_full, preferred_element_type=jnp.float32)
        feed_branch = lax.psum(feed_part.astype(jnp.bfloat16), "mp").astype(
            jnp.float32
        ) + reduce_shift.astype(jnp.float32)
        result = residual + feed_branch
        output_parts.append(jnp.where(valid_rows, result, 0.0).astype(jnp.bfloat16))
        square_sums = square_sums + jnp.stack(
            [
                jnp.sum(jnp.where(valid_rows, result * result, 0.0)),
                jnp.sum(jnp.where(valid_rows, attention_branch * attention_branch, 0.0)),
                jnp.sum(jnp.where(valid_rows, feed_branch * feed_branch, 0.0)),
                token_count,
            ]
        )
        grad_out = jnp.where(valid_rows, cotangent[start : start + slot].astype(jnp.float32), 0.0)
        grad_feed = grad_out.astype(jnp.bfloat16)
        acc_reduce_bias = acc_reduce_bias + jnp.sum(grad_out, axis=0)
        acc_reduce = acc_reduce + jnp.dot(
            activation.T, grad_feed, preferred_element_type=jnp.float32
        )
        grad_act = jnp.dot(grad_feed, reduce_full.T, preferred_element_type=jnp.float32)
        gelu_value, gelu_back = jax.vjp(gelu_exact, expand_pre)
        grad_pre = gelu_back(grad_act)[0].astype(jnp.bfloat16)
        acc_unit_bias = acc_unit_bias + jnp.sum(grad_pre, axis=0, dtype=jnp.float32)
        acc_expand = acc_expand + jnp.dot(norm_mid.T, grad_pre, preferred_element_type=jnp.float32)
        mid_part = jnp.dot(grad_pre, expand_full.T, preferred_element_type=jnp.float32)
        grad_mid = lax.psum(mid_part.astype(jnp.bfloat16), "mp").astype(jnp.float32)
        norm_value, norm_back = jax.vjp(layer_norm, residual, gain_two, shift_two)
        grad_resid_norm, grad_gain_two, grad_shift_two = norm_back(grad_mid)
        acc_gain_two = acc_gain_two + grad_gain_two
        acc_shift_two = acc_shift_two + grad_shift_two
        grad_residual = grad_out + grad_resid_norm
        grad_branch = grad_residual.astype(jnp.bfloat16)
        acc_merge_bias = acc_merge_bias + jnp.sum(grad_branch, axis=0, dtype=jnp.float32)
        acc_merge = acc_merge + jnp.dot(
            mixed_heads.T, grad_branch, preferred_element_type=jnp.float32
        )
        grad_mixed = jnp.dot(grad_branch, merge_full.T, preferred_element_type=jnp.float32)
        grad_mixed = grad_mixed.astype(jnp.bfloat16).reshape(slot, local_heads, HEAD_DIM)
        again_scores = attention_scores(query_low, key_low, slopes, length)
        soft_weights = jnp.exp(again_scores - log_total[..., None])
        grad_probs = jnp.einsum(
            "qhe,khe->hqk", grad_mixed, value_low, preferred_element_type=jnp.float32
        )
        grad_value = jnp.einsum(
            "hqk,qhe->khe",
            soft_weights.astype(jnp.bfloat16),
            grad_mixed,
            preferred_element_type=jnp.float32,
        ).astype(jnp.bfloat16)
        row_terms = jnp.sum(soft_weights * grad_probs, axis=-1, keepdims=True)
        grad_scores = (soft_weights * (grad_probs - row_terms)).astype(jnp.bfloat16)
        grad_query = (
            0.125
            * jnp.einsum("hqk,khe->qhe", grad_scores, key_low, preferred_element_type=jnp.float32)
        ).astype(jnp.bfloat16)
        grad_key = (
            0.125
            * jnp.einsum("hqk,qhe->khe", grad_scores, query_low, preferred_element_type=jnp.float32)
        ).astype(jnp.bfloat16)
        grad_triple = jnp.stack([grad_query, grad_key, grad_value], axis=1).reshape(
            slot, 3, head_cols
        )
        acc_pair_bias = acc_pair_bias + jnp.stack(
            [
                jnp.sum(grad_triple[:, 0], axis=0, dtype=jnp.float32),
                jnp.sum(grad_triple[:, 2], axis=0, dtype=jnp.float32),
            ]
        )
        acc_triple = acc_triple + jnp.einsum(
            "td,tcf->dcf", norm_in, grad_triple, preferred_element_type=jnp.float32
        )
        grad_in_part = jnp.einsum(
            "tcf,dcf->td", grad_triple, triple_full, preferred_element_type=jnp.float32
        )
        grad_in = lax.psum(grad_in_part.astype(jnp.bfloat16), "mp").astype(jnp.float32)
        first_value, first_back = jax.vjp(layer_norm, token_rows, gain_one, shift_one)
        grad_rows_norm, grad_gain_one, grad_shift_one = first_back(grad_in)
        acc_gain_one = acc_gain_one + grad_gain_one
        acc_shift_one = acc_shift_one + grad_shift_one
        input_rows_grad = (grad_residual + grad_rows_norm).astype(jnp.bfloat16)
        grad_parts.append(input_rows_grad)
    owned = (
        lax.psum_scatter(
            acc_triple.astype(jnp.bfloat16), "dp", scatter_dimension=0, tiled=True
        ).astype(jnp.float32),
        lax.psum_scatter(
            acc_merge.astype(jnp.bfloat16), "dp", scatter_dimension=1, tiled=True
        ).astype(jnp.float32),
        lax.psum_scatter(
            acc_expand.astype(jnp.bfloat16), "dp", scatter_dimension=0, tiled=True
        ).astype(jnp.float32),
        lax.psum_scatter(
            acc_reduce.astype(jnp.bfloat16), "dp", scatter_dimension=1, tiled=True
        ).astype(jnp.float32),
        lax.psum_scatter(
            acc_gain_one.astype(jnp.bfloat16), "dp", scatter_dimension=0, tiled=True
        ).astype(jnp.float32),
        lax.psum_scatter(
            acc_shift_one.astype(jnp.bfloat16), "dp", scatter_dimension=0, tiled=True
        ).astype(jnp.float32),
        lax.psum_scatter(
            acc_merge_bias.astype(jnp.bfloat16), "dp", scatter_dimension=0, tiled=True
        ).astype(jnp.float32),
        lax.psum_scatter(
            acc_gain_two.astype(jnp.bfloat16), "dp", scatter_dimension=0, tiled=True
        ).astype(jnp.float32),
        lax.psum_scatter(
            acc_shift_two.astype(jnp.bfloat16), "dp", scatter_dimension=0, tiled=True
        ).astype(jnp.float32),
        lax.psum_scatter(
            acc_reduce_bias.astype(jnp.bfloat16), "dp", scatter_dimension=0, tiled=True
        ).astype(jnp.float32),
    )
    pair_grad, unit_grad, total_sums = lax.psum((acc_pair_bias, acc_unit_bias, square_sums), "dp")
    root_means = jnp.sqrt(total_sums[:3] / (total_sums[3] * width))
    layer_output = jnp.concatenate(output_parts, axis=0)
    hidden_grad = jnp.concatenate(grad_parts, axis=0)
    return (
        layer_output,
        hidden_grad,
        owned[4],
        owned[5],
        owned[0],
        pair_grad,
        owned[1],
        owned[6],
        owned[7],
        owned[8],
        owned[2],
        unit_grad,
        owned[3],
        owned[9],
        root_means,
    )


def solution(mesh):
    return jax.shard_map(
        local,
        mesh=mesh,
        in_specs=(
            P("dp", None),
            P("dp", None),
            P("dp"),
            P("dp"),
            P("dp"),
            P("dp", None, "mp"),
            P(None, "mp"),
            P("mp", "dp"),
            P("dp"),
            P("dp"),
            P("dp"),
            P("dp", "mp"),
            P("mp"),
            P("mp", "dp"),
            P("dp"),
        ),
        out_specs=(
            P("dp", None),
            P("dp", None),
            P("dp"),
            P("dp"),
            P("dp", None, "mp"),
            P(None, "mp"),
            P("mp", "dp"),
            P("dp"),
            P("dp"),
            P("dp"),
            P("dp", "mp"),
            P("mp"),
            P("mp", "dp"),
            P("dp"),
            P(),
        ),
        check_vma=False,
    )
```

profile of v0, /device:TPU:0, one launch (start us, length us, event | category | flops | bytes accessed | tf_op | source)
XLA Modules:
  0.0 1231.0 jit_solution(12049603003931523445)
XLA Ops:
  17.5 10.6 all-gather
  28.1 8.9 all-gather.1
  37.4 22.4 %all-gather.11.cloned.1.call-done = bf16[2048,3,512]{0,2,1:T(8,128)(2,1)} async-done(((bf16[256,3,512]{0,2,1:T(8,128)(2,1)}), bf16[2048,3,512]{0,2,1:T(8,128)(2,1)}) %all-gather.11.cloned.1.call-update) | async-done | bytes 6291472 | tf_op jit(solution)/shard_map/all_gather | solution.py:64
  59.8 6.5 fusion.86
  73.6 16.2 %all-gather.13.cloned.1.call-done = bf16[512,2048]{1,0:T(8,128)(2,1)} async-done(((bf16[512,256]{1,0:T(8,128)(2,1)}), bf16[512,2048]{1,0:T(8,128)(2,1)}) %all-gather.13.cloned.1.call-update) | async-done | bytes 2097168 | tf_op jit(solution)/shard_map/all_gather | solution.py:65
  94.1 9.1 all-gather.2
  104.1 76.3 %all-reduce.15.cloned.1.call-done = bf16[512,2048]{1,0:T(8,128)(2,1)} async-done(((bf16[512,2048]{1,0:T(8,128)(2,1)}), bf16[512,2048]{1,0:T(8,128)(2,1)}) %all-reduce.15.cloned.1.call-update) | async-done | bytes 2097168 | tf_op jit(solution)/shard_map/psum | solution.py:118
  180.3 4.3 fusion.51
  185.3 5.9 fusion.83
  203.0 8.9 all-gather.3
  212.0 9.3 all-gather.4
  221.3 65.8 %all-reduce.17.cloned.1.call-done = bf16[512,2048]{1,0:T(8,128)(2,1)} async-done(((bf16[512,2048]{1,0:T(8,128)(2,1)}), bf16[512,2048]{1,0:T(8,128)(2,1)}) %all-reduce.17.cloned.1.call-update) | async-done | bytes 2097168 | tf_op jit(solution)/shard_map/psum | solution.py:118
  292.9 49.2 %all-gather.15.cloned.1.call-done = bf16[2048,2048]{1,0:T(8,128)(2,1)} async-done(((bf16[256,2048]{1,0:T(8,128)(2,1)}), bf16[2048,2048]{1,0:T(8,128)(2,1)}) %all-gather.15.cloned.1.call-update) | async-done | bytes 8388624 | tf_op jit(solution)/shard_map/all_gather | solution.py:71
  342.2 8.7 fusion.108
  353.0 26.1 %multiply_convert_fusion.3 = (bf16[512,2048]{1,0:T(8,128)(2,1)}, f32[512,2048]{1,0:T(8,128)}, bf16[512,2048]{1,0:T(8,128)(2,1)}, f32[512,2048]{1,0:T(8,128)}, f32[512,2048]{1,0:T(8,128)}) fusion(f32[2048]{0:T(1024)S(1)} %convert_element_type.369, f32[512,2048]{1,0:T(8,128)S(1)} %fusion.108, bf16[2048,2048]{1,0:T(8,128)(2,1)S(1)} %copy-done.105, ...), kind=kOutput, calls=%fused_computation.120 | convolution fusion | flops 4442816512 | bytes 33591296 | tf_op jit(solution)/shard_map/dot_general | solution.py:124
  379.1 20.7 %all-gather.17.cloned.1.call-done = bf16[2048,2048]{1,0:T(8,128)(2,1)} async-done(((bf16[2048,256]{1,0:T(8,128)(2,1)}), bf16[2048,2048]{1,0:T(8,128)(2,1)}) %all-gather.17.cloned.1.call-update) | async-done | bytes 8388624 | tf_op jit(solution)/shard_map/all_gather | solution.py:72
  399.8 12.9 %convert_reduce_fusion.6 = (f32[2048]{0:T(1024)}, bf16[512,2048]{1,0:T(8,128)(2,1)S(1)}) fusion(f32[512,2048]{1,0:T(8,128)} %get-tuple-element.85, bf16[2048,2048]{1,0:T(8,128)(2,1)} %all-gather.17.cloned.1.call-done, pred[512]{0:T(512)(128)(4,1)S(1)} %iota_compare_fusion.1, bf16[1024,2048]{1,0:T(8,128)(2,1)} %param.16, f32[512,2048]{1,0:T(8,128)} %copy-done.120, ...), kind=kOutput, calls=%fused_computation.81 | convolution fusion | flops 4315936768 | bytes 20988416 | tf_op jit(solution)/shard_map/dot_general | solution.py:146
  412.7 9.9 convolution_convert_fusion
  422.6 11.5 convert_reduce_fusion.7
  434.1 10.0 convolution_convert_fusion.1
  444.1 9.8 convolution_convert_fusion.2
  453.9 5.7 convolution_convert_fusion.4
  460.3 8.9 all-gather.5
  469.2 281.5 %all-reduce.21.cloned.1.call-done = (bf16[512,2048]{1,0:T(8,128)(2,1)}, bf16[512,2048]{1,0:T(8,128)(2,1)}, bf16[512,2048]{1,0:T(8,128)(2,1)}, bf16[512,2048]{1,0:T(8,128)(2,1)}) async-done(((bf16[512,2048]{1,0:T(8,128)(2,1)}, bf16[512,2048]{1,0:T(8,128)(2,1)}, bf16[512,2048]{1,0:T(8,128)(2,1)}, bf16[512,2048]{1,0:T(8,128)(2,1)}), (bf16[512,2048]{1,0:T(8,128)(2,1)}, bf16[512,2048]{1,0:T(8,128)(2,1)}, ...) | async-done | bytes 8388624 | tf_op jit(solution)/shard_map/psum | solution.py:127
  750.7 14.7 %select_reduce_fusion.5 = (f32[]{:T(128)}, f32[512]{0:T(512)S(1)}, f32[512]{0:T(512)S(1)}, f32[]{:T(128)}, f32[]{:T(128)}, /*index=5*/f32[]{:T(128)}, f32[]{:T(1...) fusion(bf16[512,2048]{1,0:T(8,128)(2,1)} %get-tuple-element.67,, ...), kind=kLoop, calls=%fused_computation.80 | loop fusion | flops 55567360 | bytes 25224216 | tf_op jit(solution)/shard_map/reduce_sum | solution.py:134
  765.5 6.0 fusion.30
  782.8 4.5 multiply_convert_fusion.1
  796.7 4.3 multiply_reduce_fusion
  807.9 9.5 multiply_convert_fusion
  817.3 5.5 convert_reduce_fusion.12
  832.1 5.7 convert_reduce_fusion.10
  838.8 7.5 bitcast_convert_fusion.1
  846.3 7.4 bitcast_convert_fusion
  854.4 13.8 %fusion.106 = f32[2048,2048]{1,0:T(8,128)} fusion(bf16[512,2048]{1,0:T(8,128)(2,1)} %copy-done.119, f32[2048]{0:T(1024)S(1)} %bitcast.180, f32[2048]{0:T(1024)S(1)} %bitcast.161, f32[512]{0:T(512)S(1)} %copy-done.74, bf16[512,2048]{1,0:T(8,128)(2,1)} %all-reduce.15.cloned.1.call-done, f32[512]{0:T(512)S(1)} %broadcast_multiply_fusion.3, ...), kind=kOutput, calls=%fused_computation.249 | convolution fusion | flops 4304404480 | bytes 23097344 | tf_op jit(solution)/shard_map/dot_general | solution.py:150
  868.2 15.6 %add_convert_fusion.1 = bf16[2048,2048]{1,0:T(8,128)(2,1)} fusion(f32[2048,2048]{1,0:T(8,128)} %fusion.106, bf16[512,2048]{1,0:T(8,128)(2,1)} %copy-done.121, f32[512]{0:T(512)S(1)} %copy-done.72, f32[2048]{0:T(1024)S(1)} %bitcast.181, f32[2048]{0:T(1024)S(1)} %bitcast.162, bf16[512,2048]{1,0:T(8,128)(2,1)} %all-reduce.17.cloned.1.call-done, ...), kind=kOutput, calls=%fused_computation.1 | convolution fusion | flops 4312793088 | bytes 31485952 | tf_op jit(solution)/shard_map/dot_general | solution.py:150
  885.3 10.0 fusion.71
  895.3 11.0 add_convert_fusion
  907.7 8.8 fusion.70
  916.5 8.6 add_convert_fusion.2
  932.2 25.5 %all-reduce.6 = (f32[2,512]{1,0:T(2,128)}, f32[2048]{0:T(1024)}, f32[4]{0:T(128)S(1)}) all-reduce(f32[2,512]{1,0:T(2,128)S(1)} %maximum_add_fusion, f32[2048]{0:T(1024)S(1)} %add.360, f32[4]{0:T(128)S(1)} %maximum_add_fusion.1), channel_id=1, replica_groups=mesh['dp'=8,'mp'=4] {'dp'}, use_global_device_ids=true, to_apply=%region_41.42 | all-reduce | flops 3076 | bytes 24608 | tf_op jit(solution)/shard_map/psum | solution.py:240
  965.4 42.5 %all-reduce.19.cloned.1.call-done = (bf16[512,2048]{1,0:T(8,128)(2,1)}, bf16[512,2048]{1,0:T(8,128)(2,1)}) async-done(((bf16[512,2048]{1,0:T(8,128)(2,1)}, bf16[512,2048]{1,0:T(8,128)(2,1)}), (bf16[512,2048]{1,0:T(8,128)(2,1)}, bf16[512,2048]{1,0:T(8,128)(2,1)})) %all-reduce.19.cloned.1.call-update) | async-done | bytes 4194320 | tf_op jit(solution)/shard_map/psum | solution.py:201
  1008.0 4.7 fusion.25
  1018.0 24.3 %all-reduce.7 = (bf16[2048]{0:T(1024)(128)(2,1)S(1)}, bf16[2048]{0:T(1024)(128)(2,1)S(1)}, bf16[2048]{0:T(1024)(128)(2,1)S(1)}, bf16[2048]{0:T(1024)(128)(2,1)S(...) all-reduce(bf16[2048]{0:T(1024)(128)(2,1)S(1)} %add_convert_fusion., ...), channel_id=2, replica_groups=mesh['dp'=8,'mp'=4] {'dp'}, use_global_device_ids=true, to_apply=%region_32.33.clone | all-reduce | flops 12288 | bytes 49152
  1046.2 8.3 add_convert_fusion.6
  1054.5 5.9 add_convert_fusion.4
  1063.0 18.8 %reduce-scatter.9.cloned.1.call-done = bf16[256,2048]{1,0:T(8,128)(2,1)} async-done(((bf16[2048,2048]{1,0:T(8,128)(2,1)}), bf16[256,2048]{1,0:T(8,128)(2,1)}) %reduce-scatter.9.cloned.1.call-update) | async-done | bytes 1048592 | tf_op jit(solution)/shard_map/reduce_scatter | solution.py:215
  1084.5 72.0 %reduce-scatter.11.cloned.1.call-done = bf16[2048,256]{1,0:T(8,128)(2,1)} async-done(((bf16[2048,2048]{1,0:T(8,128)(2,1)}), bf16[2048,256]{1,0:T(8,128)(2,1)}) %reduce-scatter.11.cloned.1.call-update) | async-done | bytes 1048592 | tf_op jit(solution)/shard_map/reduce_scatter | solution.py:218
  1159.2 62.2 %reduce-scatter.5.cloned.1.call-done = bf16[256,3,512]{2,0,1:T(8,128)(2,1)} async-done(((bf16[2048,3,512]{2,0,1:T(8,128)(2,1)}), bf16[256,3,512]{2,0,1:T(8,128)(2,1)}) %reduce-scatter.5.cloned.1.call-update) | async-done | bytes 786448 | tf_op jit(solution)/shard_map/reduce_scatter | solution.py:209
  (390 shorter events, 116.2 us)
Async XLA Ops:
  7.2 20.8 %copy-start.110 = (bf16[256]{0:T(256)(128)(2,1)S(1)}, bf16[256]{0:T(256)(128)(2,1)}, u32[]{:S(2)}) copy-start(bf16[256]{0:T(256)(128)(2,1)} %param.19) | copy-start | bytes 1540
  7.2 52.6 %all-gather.11.cloned.1.call-start = ((), (), s32[]{:S(2)}) async-start(), calls=%async_computation.4 | async-start | bytes 7077888 | tf_op jit(solution)/shard_map/all_gather | solution.py:64
  9.6 80.3 %all-gather.13.cloned.1.call-start = ((), (), s32[]{:S(2)}) async-start(), calls=%async_computation.5 | async-start | bytes 2359296 | tf_op jit(solution)/shard_map/all_gather | solution.py:65
  10.3 170.0 %all-reduce.15.cloned.1.call-start = ((), (), s32[]{:S(2)}) async-start(), calls=%async_computation.6 | async-start | bytes 4194304 | tf_op jit(solution)/shard_map/psum | solution.py:118
  12.3 54.0 %copy-start.62 = (f32[512]{0:T(512)}, f32[512]{0:T(512)S(1)}, u32[]{:S(2)}) copy-start(f32[512]{0:T(512)S(1)} %broadcast_multiply_fusion.4) | copy-start | bytes 6148
  16.1 50.3 %copy-start.79 = (f32[512]{0:T(512)}, f32[512]{0:T(512)S(1)}, u32[]{:S(2)}) copy-start(f32[512]{0:T(512)S(1)} %fusion.90) | copy-start | bytes 6148
  17.4 754.1 %copy-start.97 = (pred[512]{0:T(512)(128)(4,1)}, pred[512]{0:T(512)(128)(4,1)S(1)}, u32[]{:S(2)}) copy-start(pred[512]{0:T(512)(128)(4,1)S(1)} %iota_compare_fusion.2) | copy-start | bytes 1540
  28.1 156.6 %copy-start.56 = (f32[8,1,256]{2,1,0:T(1,128)}, f32[8,1,256]{2,1,0:T(1,128)S(1)}, u32[]{:S(2)}) copy-start(f32[8,1,256]{2,1,0:T(1,128)S(1)} %convert_element_type.455) | copy-start | bytes 24580
  37.0 147.7 %copy-start.93 = (f32[8,1,256]{2,1,0:T(1,128)}, f32[8,1,256]{2,1,0:T(1,128)S(1)}, u32[]{:S(2)}) copy-start(f32[8,1,256]{2,1,0:T(1,128)S(1)} %convert_element_type.456) | copy-start | bytes 24580
  37.1 154.4 %copy-start.64 = (f32[8,64]{1,0:T(8,128)}, f32[8,64]{1,0:T(8,128)S(1)}, u32[]{:S(2)}) copy-start(f32[8,64]{1,0:T(8,128)S(1)} %add.314) | copy-start | bytes 6148
  37.2 157.8 %copy-start.58 = (f32[8,64]{1,0:T(8,128)}, f32[8,64]{1,0:T(8,128)S(1)}, u32[]{:S(2)}) copy-start(f32[8,64]{1,0:T(8,128)S(1)} %add.311) | copy-start | bytes 6148
  73.6 111.1 %copy-start.39 = (bf16[8,64,512]{2,1,0:T(8,128)(2,1)}, bf16[8,64,512]{2,1,0:T(8,128)(2,1)S(1)}, u32[]{:S(2)}) copy-start(bf16[8,64,512]{2,1,0:T(8,128)(2,1)S(1)} %convolution_convert_fusion.11) | copy-start | bytes 1572868
  73.6 20.5 %copy-start.111 = (bf16[256]{0:T(256)(128)(2,1)S(1)}, bf16[256]{0:T(256)(128)(2,1)}, u32[]{:S(2)}) copy-start(bf16[256]{0:T(256)(128)(2,1)} %param.23) | copy-start | bytes 1540
  94.0 193.1 %all-reduce.17.cloned.1.call-start = ((), (), s32[]{:S(2)}) async-start(), calls=%async_computation.9 | async-start | bytes 4194304 | tf_op jit(solution)/shard_map/psum | solution.py:118
  103.9 646.8 %copy-start.99 = (pred[512]{0:T(512)(128)(4,1)}, pred[512]{0:T(512)(128)(4,1)S(1)}, u32[]{:S(2)}) copy-start(pred[512]{0:T(512)(128)(4,1)S(1)} %iota_compare_fusion.1) | copy-start | bytes 1540
  103.9 87.3 %copy-start.60 = (f32[512]{0:T(512)}, f32[512]{0:T(512)S(1)}, u32[]{:S(2)}) copy-start(f32[512]{0:T(512)S(1)} %broadcast_multiply_fusion.2) | copy-start | bytes 6148
  199.2 12.8 %copy-start.113 = (bf16[256]{0:T(256)(128)(2,1)S(1)}, bf16[256]{0:T(256)(128)(2,1)}, u32[]{:S(2)}) copy-start(bf16[256]{0:T(256)(128)(2,1)} %param.25) | copy-start | bytes 1540
  199.2 22.1 %copy-start.102 = (bf16[2048]{0:T(1024)(128)(2,1)S(1)}, bf16[2048]{0:T(1024)(128)(2,1)}, u32[]{:S(2)}) copy-start(bf16[2048]{0:T(1024)(128)(2,1)} %param.27) | copy-start | bytes 12292
  199.2 88.0 %copy-start.10 = (bf16[512,2048]{1,0:T(8,128)(2,1)S(1)}, bf16[512,2048]{1,0:T(8,128)(2,1)}, u32[]{:S(2)}) copy-start(bf16[512,2048]{1,0:T(8,128)(2,1)} %all-reduce.15.cloned.1.call-done) | copy-start | bytes 6291460
  201.8 140.4 %all-gather.15.cloned.1.call-start = ((), (), s32[]{:S(2)}) async-start(), calls=%async_computation.7 | async-start | bytes 9437184 | tf_op jit(solution)/shard_map/all_gather | solution.py:71
  202.4 197.4 %all-gather.17.cloned.1.call-start = ((), (), s32[]{:S(2)}) async-start(), calls=%async_computation.8 | async-start | bytes 9437184 | tf_op jit(solution)/shard_map/all_gather | solution.py:72
  203.0 547.8 %all-reduce.21.cloned.1.call-start = ((), (), s32[]{:S(2)}) async-start(), calls=%async_computation.15 | async-start | bytes 16777216 | tf_op jit(solution)/shard_map/psum | solution.py:127
  221.3 129.6 %copy-start.95 = (f32[8,1,256]{2,1,0:T(1,128)}, f32[8,1,256]{2,1,0:T(1,128)S(1)}, u32[]{:S(2)}) copy-start(f32[8,1,256]{2,1,0:T(1,128)S(1)} %convert_element_type.459) | copy-start | bytes 24580
  292.9 498.8 %copy-start.71 = (f32[512]{0:T(512)}, f32[512]{0:T(512)S(1)}, u32[]{:S(2)}) copy-start(f32[512]{0:T(512)S(1)} %fusion.93) | copy-start | bytes 6148
  292.9 478.6 %copy-start.73 = (f32[512]{0:T(512)}, f32[512]{0:T(512)S(1)}, u32[]{:S(2)}) copy-start(f32[512]{0:T(512)S(1)} %fusion.91) | copy-start | bytes 6148
  434.1 19.8 %slice-start.4 = ((s8[8388608]{0:T(1024)(128)(4,1)}), s8[4194304]{0:T(1024)(128)(4,1)S(1)}, s32[]{:S(2)}) async-start(s8[8388608]{0:T(1024)(128)(4,1)} %bitcast.182), calls=%async_computation.20 | async-start | bytes 8388608
  459.7 504.0 %reduce-scatter.7.cloned.1.call-start = ((), (), s32[]{:S(2)}) async-start(), calls=%async_computation.11 | async-start | bytes 2359296 | tf_op jit(solution)/shard_map/reduce_scatter | solution.py:212
  750.7 14.7 %copy-start.3 = (bf16[1024,2048]{1,0:T(8,128)(2,1)S(1)}, bf16[1024,2048]{1,0:T(8,128)(2,1)}, u32[]{:S(2)}) copy-start(bf16[1024,2048]{1,0:T(8,128)(2,1)} %param.15) | copy-start | bytes 12582916
  750.7 14.7 %copy-start.13 = (bf16[512,2048]{1,0:T(8,128)(2,1)S(1)}, bf16[512,2048]{1,0:T(8,128)(2,1)}, u32[]{:S(2)}) copy-start(bf16[512,2048]{1,0:T(8,128)(2,1)} %all-reduce.17.cloned.1.call-done) | copy-start | bytes 6291460
  750.7 14.7 %copy-start.19 = (bf16[512,2048]{1,0:T(8,128)(2,1)S(1)}, bf16[512,2048]{1,0:T(8,128)(2,1)}, u32[]{:S(2)}) copy-start(bf16[512,2048]{1,0:T(8,128)(2,1)} %get-tuple-element.69) | copy-start | bytes 6291460
  750.7 14.7 %copy-start.21 = (bf16[512,2048]{1,0:T(8,128)(2,1)S(1)}, bf16[512,2048]{1,0:T(8,128)(2,1)}, u32[]{:S(2)}) copy-start(bf16[512,2048]{1,0:T(8,128)(2,1)} %get-tuple-element.68) | copy-start | bytes 6291460
  771.5 20.2 %copy-start.83 = (f32[512]{0:T(512)}, f32[512]{0:T(512)S(1)}, u32[]{:S(2)}) copy-start(f32[512]{0:T(512)S(1)} %get-tuple-element.111) | copy-start | bytes 6148
  803.7 204.2 %all-reduce.19.cloned.1.call-start = ((), (), s32[]{:S(2)}) async-start(), calls=%async_computation.14 | async-start | bytes 8388608 | tf_op jit(solution)/shard_map/psum | solution.py:201
  823.1 15.7 %copy-start.45 = (bf16[512,1,512]{2,0,1:T(8,128)(2,1)}, bf16[512,1,512]{2,0,1:T(8,128)(2,1)S(1)}, u32[]{:S(2)}) copy-start(bf16[512,1,512]{2,0,1:T(8,128)(2,1)S(1)} %copy.57) | copy-start | bytes 1572868
  832.1 14.2 %copy-start.48 = (bf16[512,1,512]{2,0,1:T(8,128)(2,1)}, bf16[512,1,512]{2,0,1:T(8,128)(2,1)S(1)}, u32[]{:S(2)}) copy-start(bf16[512,1,512]{2,0,1:T(8,128)(2,1)S(1)} %copy.63) | copy-start | bytes 1572868
  853.7 14.4 %copy-start.72 = (f32[512]{0:T(512)S(1)}, f32[512]{0:T(512)}, u32[]{:S(2)}) copy-start(f32[512]{0:T(512)} %copy-done.71) | copy-start | bytes 6148
  853.7 228.0 %reduce-scatter.9.cloned.1.call-start = ((), (), s32[]{:S(2)}) async-start(), calls=%async_computation.12 | async-start | bytes 9437184 | tf_op jit(solution)/shard_map/reduce_scatter | solution.py:215
  854.4 13.8 %copy-start.4 = (bf16[1024,2048]{1,0:T(8,128)(2,1)S(1)}, bf16[1024,2048]{1,0:T(8,128)(2,1)}, u32[]{:S(2)}) copy-start(bf16[1024,2048]{1,0:T(8,128)(2,1)} %param.15) | copy-start | bytes 12582916
  883.7 11.6 copy-start.101
  883.8 272.8 %reduce-scatter.11.cloned.1.call-start = ((), (), s32[]{:S(2)}) async-start(), calls=%async_computation.13 | async-start | bytes 9437184 | tf_op jit(solution)/shard_map/reduce_scatter | solution.py:218
  906.4 315.1 %reduce-scatter.5.cloned.1.call-start = ((), (), s32[]{:S(2)}) async-start(), calls=%async_computation.10 | async-start | bytes 7077888 | tf_op jit(solution)/shard_map/reduce_scatter | solution.py:209
  925.1 34.3 %copy-start.66 = (f32[2048]{0:T(1024)S(1)}, f32[2048]{0:T(1024)}, u32[]{:S(2)}) copy-start(f32[2048]{0:T(1024)} %get-tuple-element.30) | copy-start | bytes 24580
  925.1 34.3 %copy-start.67 = (f32[2048]{0:T(1024)S(1)}, f32[2048]{0:T(1024)}, u32[]{:S(2)}) copy-start(f32[2048]{0:T(1024)} %get-tuple-element.72) | copy-start | bytes 24580
  925.2 34.3 %copy-start.68 = (f32[2048]{0:T(1024)S(1)}, f32[2048]{0:T(1024)}, u32[]{:S(2)}) copy-start(f32[2048]{0:T(1024)} %get-tuple-element.70) | copy-start | bytes 24580
  925.2 34.3 %copy-start.28 = (bf16[512,2048]{1,0:T(8,128)(2,1)S(1)}, bf16[512,2048]{1,0:T(8,128)(2,1)}, u32[]{:S(2)}) copy-start(bf16[512,2048]{1,0:T(8,128)(2,1)} %get-tuple-element.78) | copy-start | bytes 6291460
  1013.9 32.2 %copy-start.11 = (bf16[512,2048]{1,0:T(8,128)(2,1)S(1)}, bf16[512,2048]{1,0:T(8,128)(2,1)}, u32[]{:S(2)}) copy-start(bf16[512,2048]{1,0:T(8,128)(2,1)} %all-reduce.15.cloned.1.call-done) | copy-start | bytes 6291460
  1013.9 32.2 %copy-start.70 = (f32[512]{0:T(512)S(1)}, f32[512]{0:T(512)}, u32[]{:S(2)}) copy-start(f32[512]{0:T(512)} %copy-done.69) | copy-start | bytes 6148
  1013.9 32.2 %copy-start.86 = (f32[512]{0:T(512)S(1)}, f32[512]{0:T(512)}, u32[]{:S(2)}) copy-start(f32[512]{0:T(512)} %copy-done.85) | copy-start | bytes 6148
  (92 other events, 433.9 us)
Sparse Core Ops, SparseCore 0:
  10.5 49.2 all-gather.10
  61.7 28.0 all-gather.12
  94.2 86.1 all-reduce.14
  201.9 85.1 all-reduce.16
  288.9 53.2 all-gather.14
  343.9 55.8 all-gather.16
  459.8 290.8 all-reduce.20
  803.8 40.1 reduce-scatter.6
  853.8 154.0 all-reduce.18
  1011.3 70.4 reduce-scatter.8
  1085.2 71.2 reduce-scatter.10
  1159.8 61.6 reduce-scatter.4
where the time goes:
time: 1240 us; the launch traced here: 1230 us
  waiting for transfers between devices  730 us (59%)
  matrix products  242 us (20%)
  other arithmetic  108 us (9%)
  blocking collectives  105 us (8%)
  local copies, waits for them, and re-layouts  25.9 us (2%)
  between operations  18.7 us (2%)
    psum x1, waiting for transfers between devices, local(): lax.psum(feed_part.astype(jnp.bfloat16), 'mp').astype(jnp.float32)  282 us
    psum x2, waiting for transfers between devices, local(): lax.psum(attention_part.astype(jnp.bfloat16), 'mp').astype(jnp.float32)  142 us
    reduce_scatter x1, waiting for transfers between devices, local(): lax.psum_scatter(acc_reduce.astype(jnp.bfloat16), 'dp', scatter_dimension...  72 us
    reduce_scatter x1, waiting for transfers between devices, local(): lax.psum_scatter(acc_triple.astype(jnp.bfloat16), 'dp', scatter_dimension...  62.2 us
    all_gather x1, waiting for transfers between devices, local(): lax.all_gather(expand_weight, 'dp', axis=0, tiled=True)  49.2 us
    psum x1, waiting for transfers between devices, local(): lax.psum(grad_in_part.astype(jnp.bfloat16), 'mp').astype(jnp.float32)  42.5 us
    dot_general x2, matrix products, local(): jnp.dot(norm_mid, expand_full, preferred_element_type=jnp.float32)  34.9 us
    dot_general x2, matrix products, local(): jnp.dot(norm_mid.T, grad_pre, preferred_element_type=jnp.float32)  29.3 us
  transfers between devices with their start and end apart: 12, of which 11 were waited for; matrix products, arithmetic and copies ran while one was open for 18% of the time, Pallas kernels for 0%

commit v1 on v0

v1 whole, which is shorter than its diff:
```python
import functools

import jax
import jax.numpy as jnp
from jax import lax
from jax.experimental import pallas as pl
from jax.experimental.pallas import tpu as pltpu
from jax.sharding import PartitionSpec as P

HEADS = 32
HEAD_DIM = 64
SLOT = 512
PIECE = 64
TILE = 256
BLOCK = 512
F32 = jnp.float32
BF16 = jnp.bfloat16
MESH = pl.DeviceIdType.MESH
VMEM = pl.BlockSpec(memory_space=pltpu.VMEM)
ANY = pl.BlockSpec(memory_space=pl.ANY)


def dot32(a, b):
    return jnp.dot(a, b, preferred_element_type=F32)


def dot_nt(a, b):
    return lax.dot_general(a, b, (((1,), (1,)), ((), ())), preferred_element_type=F32)


def dot_tn(a, b):
    return lax.dot_general(a, b, (((0,), (0,)), ((), ())), preferred_element_type=F32)


def norm_parts(values):
    center = values - jnp.mean(values, axis=-1, keepdims=True)
    spread = jnp.mean(center * center, axis=-1, keepdims=True)
    rate = lax.rsqrt(spread + 1e-05)
    return center * rate, rate


def norm_back(grad, gain, normed, rate):
    scaled = grad * gain
    first = jnp.mean(scaled, axis=-1, keepdims=True)
    second = jnp.mean(scaled * normed, axis=-1, keepdims=True)
    return rate * (scaled - first - normed * second)


def block(index, size):
    return pl.ds(pl.multiple_of(index * size, size), size)


def greet(count):
    me, group = lax.axis_index("mp"), lax.axis_index("dp")
    barrier = pltpu.get_barrier_semaphore()

    @pl.when(me < count - 1)
    def _():
        pl.semaphore_signal(barrier, inc=1, device_id=(group, me + 1), device_id_type=MESH)

    @pl.when(me > 0)
    def _():
        pl.semaphore_signal(barrier, inc=1, device_id=(group, me - 1), device_id_type=MESH)

    peers = jnp.where(me > 0, 1, 0) + jnp.where(me < count - 1, 1, 0)
    pl.semaphore_wait(barrier, peers)


LAG = 1


class Line:
    def __init__(self, count, part, inbox, extra, sems):
        self.count, self.part, self.inbox, self.extra = count, part, inbox, extra
        self.pieces = part.shape[0] // PIECE
        self.sum_out, self.sum_in, self.extra_in, self.own_out, self.all_out, self.all_in = sems
        self.rows = PIECE // count
        self.me, self.group = lax.axis_index("mp"), lax.axis_index("dp")

    @staticmethod
    def scratch(count, pieces, width):
        rows = PIECE // count
        return [
            pltpu.VMEM((pieces * rows, width), BF16),
            pltpu.SemaphoreType.DMA((pieces, count)),
            pltpu.SemaphoreType.DMA((pieces, count)),
            pltpu.SemaphoreType.DMA((pieces,)),
            pltpu.SemaphoreType.DMA((pieces,)),
            pltpu.SemaphoreType.DMA((pieces, count)),
            pltpu.SemaphoreType.DMA((pieces, count)),
        ]

    def at(self, piece, owner):
        return pl.ds(pl.multiple_of(piece * PIECE + owner * self.rows, self.rows), self.rows)

    def own(self, piece):
        return block(piece, self.rows)

    def copy(self, src, dst, out, into, to):
        return pltpu.make_async_remote_copy(
            src_ref=src,
            dst_ref=dst,
            send_sem=out,
            recv_sem=into,
            device_id=(self.group, to),
            device_id_type=MESH,
        )

    def sum_copy(self, piece, owner, to):
        rows = self.at(piece, owner)
        return self.copy(
            self.part.at[rows],
            self.inbox.at[rows],
            self.sum_out.at[piece, owner],
            self.sum_in.at[piece, owner],
            to,
        )

    def extra_copy(self, piece, owner, to):
        return self.copy(
            self.part.at[self.at(piece, owner)],
            self.extra.at[self.own(piece)],
            self.sum_out.at[piece, owner],
            self.extra_in.at[piece],
            to,
        )

    def all_copy(self, piece, owner, to, own_left=False):
        rows = self.at(piece, owner)
        return self.copy(
            self.inbox.at[rows],
            self.inbox.at[rows],
            self.own_out.at[piece] if own_left else self.all_out.at[piece, owner],
            self.all_in.at[piece, owner],
            to,
        )

    def add(self, piece, owner):
        rows = self.at(piece, owner)
        self.sum_copy(piece, owner, self.me).wait_recv()
        self.part[rows, :] = (
            self.part[rows, :].astype(F32) + self.inbox[rows, :].astype(F32)
        ).astype(BF16)

    def send_right(self, piece):
        me, last = self.me, self.count - 1
        for owner in range(last, 0, -1):

            @pl.when(me < owner)
            def _(owner=owner):
                @pl.when(me > 0)
                def _():
                    self.add(piece, owner)

                self.sum_copy(piece, owner, me + 1).start()

    def send_left(self, piece):
        me, last = self.me, self.count - 1
        for owner in range(last):

            @pl.when(me > owner)
            def _(owner=owner):
                @pl.when(me < last)
                def _():
                    self.add(piece, owner)

                @pl.when(me == owner + 1)
                def _():
                    self.extra_copy(piece, owner, me - 1).start()

                @pl.when(me > owner + 1)
                def _():
                    self.sum_copy(piece, owner, me - 1).start()

    def total(self, piece, acc):
        me, rows = self.me, self.at(piece, self.me)
        acc[...] = self.part[rows, :].astype(F32)

        @pl.when(me > 0)
        def _():
            self.sum_copy(piece, me, me).wait_recv()
            acc[...] = acc[...] + self.inbox[rows, :].astype(F32)

        @pl.when(me < self.count - 1)
        def _():
            self.extra_copy(piece, me, me).wait_recv()
            acc[...] = acc[...] + self.extra[self.own(piece), :].astype(F32)

    def share(self, piece, values):
        me = self.me
        self.inbox[self.at(piece, me), :] = values

        @pl.when(me < self.count - 1)
        def _():
            self.all_copy(piece, me, me + 1).start()

        @pl.when(me > 0)
        def _():
            self.all_copy(piece, me, me - 1, own_left=True).start()

    def forward(self, piece, away):
        me, last = self.me, self.count - 1

        @pl.when(me >= away)
        def _(owner=me - away):
            self.all_copy(piece, owner, me).wait_recv()

            @pl.when(me < last)
            def _():
                self.all_copy(piece, owner, me + 1).start()

        @pl.when(me + away <= last)
        def _(owner=me + away):
            self.all_copy(piece, owner, me).wait_recv()

            @pl.when(me > 0)
            def _():
                self.all_copy(piece, owner, me - 1).start()

    def settle(self, piece):
        me, last = self.me, self.count - 1
        for owner in range(self.count):

            @pl.when(me != owner)
            def _():
                self.sum_copy(piece, owner, me).wait_send()

            @pl.when(jnp.logical_or(jnp.logical_and(me >= owner, me < last), jnp.logical_and(me < owner, me > 0)))
            def _():
                self.all_copy(piece, owner, me).wait_send()

        @pl.when(me > 0)
        def _():
            self.all_copy(piece, me, me, own_left=True).wait_send()


def tick(line, step, finish):
    def when(piece, work, *more):
        @pl.when(jnp.logical_and(piece >= 0, piece < line.pieces))
        def _():
            work(piece, *more)

    last = line.count - 1
    when(step - LAG * line.me, line.send_right)
    when(step - LAG * (last - line.me), line.send_left)
    when(step - LAG * last, finish)
    for away in range(1, line.count):
        when(step - LAG * (last + away), line.forward, away)


def ticks(count, pieces):
    return pieces + 2 * LAG * (count - 1)


def params(index):
    return pltpu.CompilerParams(
        collective_id=index, has_side_effects=True, vmem_limit_bytes=63 << 20
    )


def merge_kernel(count, pieces, mixed, merge, own, valid, vectors, middle, residual, sums, part, acc, *rest):
    line = Line(count, part, middle, rest[0], rest[1:])
    greet(count)
    sums[...] = jnp.zeros_like(sums)

    def finish(piece):
        line.total(piece, acc)
        rows = line.own(piece)
        branch = acc[...] + vectors[2:3, :]
        result = own[rows, :].astype(F32) + branch
        residual[rows, :] = result
        normed, _ = norm_parts(result)
        line.share(piece, (normed * vectors[3:4, :] + vectors[4:5, :]).astype(BF16))
        sums[0:1, :] += jnp.sum(branch * branch * valid[rows, :], axis=0, keepdims=True)

    ratio = TILE // PIECE

    @pl.loop(0, ticks(count, pieces))
    def _(step):
        @pl.when(jnp.logical_and(step < pieces, lax.rem(step, ratio) == 0))
        def _():
            rows = block(step // ratio, TILE)

            @pl.loop(0, part.shape[1] // BLOCK)
            def _(k):
                cols = block(k, BLOCK)
                part[rows, cols] = dot32(mixed[rows, :], merge[:, cols]).astype(BF16)

        tick(line, step, finish)

    @pl.loop(0, pieces)
    def _(piece):
        line.settle(piece)


def merge_call(count, mixed, merge, own, valid, vectors):
    rows, width = mixed.shape[0], merge.shape[1]
    pieces = rows // PIECE
    return pl.pallas_call(
        functools.partial(merge_kernel, count, pieces),
        name="merge_line",
        out_shape=(
            jax.ShapeDtypeStruct((rows, width), BF16),
            jax.ShapeDtypeStruct((rows // count, width), F32),
            jax.ShapeDtypeStruct((8, width), F32),
        ),
        in_specs=[VMEM] * 5,
        out_specs=(VMEM,) * 3,
        scratch_shapes=[
            pltpu.VMEM((rows, width), BF16),
            pltpu.VMEM((PIECE // count, width), F32),
            *Line.scratch(count, pieces, width),
        ],
        compiler_params=params(1),
    )(mixed, merge, own, valid, vectors)


def feed_kernel(
    count, pieces, middle_hbm, expand_hbm, reduce_hbm, grad_hbm, residual, own_grad, unit_shift, vectors,
    branch_grad, residual_grad, sums, unit_grad, feed_hbm, expand_grad, reduce_grad,
    middle, expand, reduce, grad, active, pre_grad, part, acc, stage, load_sem, stage_sem, *rest,
):
    line = Line(count, part, branch_grad, rest[0], rest[1:])
    units = expand.shape[1]
    width = expand.shape[0]
    blocks = units // BLOCK

    def load(k):
        cols = block(k, BLOCK)
        return (
            pltpu.make_async_copy(expand_hbm.at[:, cols], expand.at[:, cols], load_sem.at[0, k]),
            pltpu.make_async_copy(reduce_hbm.at[cols], reduce.at[cols], load_sem.at[1, k]),
        )

    def load_rows(k):
        rows = block(k, TILE)
        return (
            pltpu.make_async_copy(middle_hbm.at[rows], middle.at[rows], load_sem.at[2, k]),
            pltpu.make_async_copy(grad_hbm.at[rows], grad.at[rows], load_sem.at[3, k]),
        )

    tiles = middle.shape[0] // TILE
    for copy in (*load_rows(0), *load(0)):
        copy.start()
    for k in range(1, blocks):
        for copy in load(k):
            copy.start()
    for k in range(1, tiles):
        for copy in load_rows(k):
            copy.start()
    greet(count)
    sums[...] = jnp.zeros_like(sums)
    unit_grad[...] = jnp.zeros_like(unit_grad)

    def finish(piece):
        line.total(piece, acc)
        rows = line.own(piece)
        grad_mid = acc[...]
        normed, rate = norm_parts(residual[rows, :])
        grad_out = own_grad[rows, :].astype(F32)
        result = grad_out + norm_back(grad_mid, vectors[3:4, :], normed, rate)
        residual_grad[rows, :] = result
        low = result.astype(BF16)
        line.share(piece, low)
        for k, values in enumerate((low.astype(F32), grad_mid * normed, grad_mid, grad_out)):
            sums[k : k + 1, :] += jnp.sum(values, axis=0, keepdims=True)

    def load_tile(tile):
        for copy in load_rows(tile):
            copy.wait()

    def forward_tile(tile, k):
        rows, cols = block(tile, TILE), block(k, BLOCK)

        @pl.when(tile == 0)
        def _():
            for copy in load(k):
                copy.wait()

        pre = dot32(middle[rows, :], expand[:, cols]) + unit_shift[:, cols]
        half = 0.5 + 0.5 * lax.erf(pre * 0.7071067811865476)
        slope = half + pre * (0.3989422804014327 * jnp.exp(-0.5 * pre * pre))
        active[rows, cols] = (pre * half).astype(BF16)
        low = (dot_nt(grad[rows, :], reduce[cols, :]) * slope).astype(BF16)
        pre_grad[rows, cols] = low
        unit_grad[:, cols] += jnp.sum(low.astype(F32), axis=0, keepdims=True)

    def back_tile(tile, k):
        rows, cols = block(tile, TILE), block(k, BLOCK)
        part[rows, cols] = dot_nt(pre_grad[rows, :], expand[cols, :]).astype(BF16)

    def put(slot, target):
        return pltpu.make_async_copy(stage.at[slot], target, stage_sem.at[slot])

    rows_all = middle.shape[0] // BLOCK
    per_feed = rows_all * (width // BLOCK)
    per_grad = (units // BLOCK) * (width // BLOCK)
    jobs = per_feed + 2 * per_grad

    def job(index):
        slot = lax.rem(index, 2)
        across = width // BLOCK

        @pl.when(index >= 2)
        def _():
            put(slot, expand_grad.at[pl.ds(0, BLOCK), pl.ds(0, BLOCK)]).wait()

        @pl.when(index < per_grad)
        def _():
            r, c = block(index // across, BLOCK), block(lax.rem(index, across), BLOCK)
            stage[slot] = dot_tn(active[:, r], grad[:, c]).astype(BF16)
            put(slot, reduce_grad.at[r, c]).start()

        @pl.when(jnp.logical_and(index >= per_grad, index < 2 * per_grad))
        def _():
            local = index - per_grad
            r, c = block(local // across, BLOCK), block(lax.rem(local, across), BLOCK)
            stage[slot] = dot_tn(middle[:, r], pre_grad[:, c]).astype(BF16)
            put(slot, expand_grad.at[r, c]).start()

        @pl.when(index >= 2 * per_grad)
        def _():
            local = index - 2 * per_grad
            r, c = block(local // across, BLOCK), block(lax.rem(local, across), BLOCK)
            stage[slot] = dot32(active[r, :], reduce[:, c]).astype(BF16)
            put(slot, feed_hbm.at[r, c]).start()

    ratio = TILE // PIECE
    backs = width // BLOCK
    load_tile(0)
    pl.loop(0, blocks)(functools.partial(forward_tile, 0))
    pl.loop(0, backs)(functools.partial(back_tile, 0))
    steps = ticks(count, pieces)
    late = (tiles - 1) * ratio
    per_step = -(-jobs // (steps - late))

    @pl.loop(0, steps)
    def _(step):
        tick(line, step, finish)
        tile, phase = step // ratio + 1, lax.rem(step, ratio)

        @pl.when(tile < tiles)
        def _():
            @pl.when(phase == 0)
            def _():
                load_tile(tile)

            @pl.loop(phase * (blocks + backs) // ratio, (phase + 1) * (blocks + backs) // ratio)
            def _(k):
                @pl.when(k < blocks)
                def _():
                    forward_tile(tile, k)

                @pl.when(k >= blocks)
                def _():
                    back_tile(tile, k - blocks)

        @pl.when(tile >= tiles)
        def _():
            first = (step - late) * per_step

            @pl.loop(first, jnp.minimum(first + per_step, jobs))
            def _(index):
                job(index)

    for slot in range(2):
        put(slot, expand_grad.at[pl.ds(0, BLOCK), pl.ds(0, BLOCK)]).wait()

    @pl.loop(0, pieces)
    def _(piece):
        line.settle(piece)


def feed_call(count, middle, expand, reduce, grad, residual, own_grad, unit_shift, vectors):
    rows, width = middle.shape
    units = expand.shape[1]
    pieces = rows // PIECE
    most = max(units // BLOCK, rows // TILE)
    return pl.pallas_call(
        functools.partial(feed_kernel, count, pieces),
        name="feed_line",
        out_shape=(
            jax.ShapeDtypeStruct((rows, width), BF16),
            jax.ShapeDtypeStruct((rows // count, width), F32),
            jax.ShapeDtypeStruct((8, width), F32),
            jax.ShapeDtypeStruct((1, units), F32),
            jax.ShapeDtypeStruct((rows, width), BF16),
            jax.ShapeDtypeStruct((width, units), BF16),
            jax.ShapeDtypeStruct((units, width), BF16),
        ),
        in_specs=[ANY] * 4 + [VMEM] * 4,
        out_specs=(VMEM,) * 4 + (ANY,) * 3,
        scratch_shapes=[
            pltpu.VMEM((rows, width), BF16),
            pltpu.VMEM((width, units), BF16),
            pltpu.VMEM((units, width), BF16),
            pltpu.VMEM((rows, width), BF16),
            pltpu.VMEM((rows, units), BF16),
            pltpu.VMEM((rows, units), BF16),
            pltpu.VMEM((rows, width), BF16),
            pltpu.VMEM((PIECE // count, width), F32),
            pltpu.VMEM((2, BLOCK, BLOCK), BF16),
            pltpu.SemaphoreType.DMA((4, most)),
            pltpu.SemaphoreType.DMA((2,)),
            *Line.scratch(count, pieces, width),
        ],
        compiler_params=params(2),
    )(middle, expand, reduce, grad, residual, own_grad, unit_shift, vectors)


def last_kernel(
    count, pieces, triple_grad, triple, feed, own, residual, residual_grad, valid, vectors,
    hidden_grad, output, sums, part, acc, *rest,
):
    half = len(rest) // 2
    line = Line(count, part, hidden_grad, rest[0], rest[1:half])
    feed_line = Line(count, feed, output, rest[half], rest[half + 1 :])
    greet(count)
    sums[...] = jnp.zeros_like(sums)

    def finish(piece):
        line.total(piece, acc)
        rows = line.own(piece)
        grad_in = acc[...]
        normed, rate = norm_parts(own[rows, :].astype(F32))
        result = residual_grad[rows, :] + norm_back(grad_in, vectors[0:1, :], normed, rate)
        line.share(piece, result.astype(BF16))
        sums[0:1, :] += jnp.sum(grad_in * normed, axis=0, keepdims=True)
        sums[1:2, :] += jnp.sum(grad_in, axis=0, keepdims=True)

    def finish_feed(piece):
        feed_line.total(piece, acc)
        rows = feed_line.own(piece)
        branch = acc[...] + vectors[5:6, :]
        keep = valid[rows, :] > 0.5
        result = jnp.where(keep, residual[rows, :] + branch, 0.0)
        feed_line.share(piece, result.astype(BF16))
        branch = jnp.where(keep, branch, 0.0)
        sums[2:3, :] += jnp.sum(result * result, axis=0, keepdims=True)
        sums[3:4, :] += jnp.sum(branch * branch, axis=0, keepdims=True)

    ratio = TILE // PIECE

    @pl.loop(0, ticks(count, pieces))
    def _(step):
        tick(feed_line, step, finish_feed)

        @pl.when(jnp.logical_and(step < pieces, lax.rem(step, ratio) == 0))
        def _():
            rows = block(step // ratio, TILE)

            @pl.loop(0, part.shape[1] // BLOCK)
            def _(k):
                cols = block(k, BLOCK)
                part[rows, cols] = dot_nt(triple_grad[rows, :], triple[cols, :]).astype(BF16)

        tick(line, step, finish)

    @pl.loop(0, pieces)
    def _(piece):
        line.settle(piece)
        feed_line.settle(piece)


def last_call(count, triple_grad, triple, feed, own, residual, residual_grad, valid, vectors):
    rows, width = feed.shape
    pieces = rows // PIECE
    return pl.pallas_call(
        functools.partial(last_kernel, count, pieces),
        name="last_line",
        out_shape=(
            jax.ShapeDtypeStruct((rows, width), BF16),
            jax.ShapeDtypeStruct((rows, width), BF16),
            jax.ShapeDtypeStruct((8, width), F32),
        ),
        in_specs=[VMEM] * 8,
        out_specs=(VMEM,) * 3,
        scratch_shapes=[
            pltpu.VMEM((rows, width), BF16),
            pltpu.VMEM((PIECE // count, width), F32),
            *Line.scratch(count, pieces, width),
            *Line.scratch(count, pieces, width),
        ],
        compiler_params=params(3),
    )(triple_grad, triple, feed, own, residual, residual_grad, valid, vectors)


def small_kernel(groups, count, over_all, over_dp, all_out, dp_out, all_in, dp_in, own_sum, mp_in, sems, mp_sems):
    me, group = lax.axis_index("mp"), lax.axis_index("dp")
    barrier = pltpu.get_barrier_semaphore()

    @pl.loop(1, groups)
    def _(away):
        to = lax.rem(group + away, groups)
        pl.semaphore_signal(barrier, inc=1, device_id=(to, me), device_id_type=MESH)

    @pl.loop(1, count)
    def _(away):
        to = lax.rem(me + away, count)
        pl.semaphore_signal(barrier, inc=1, device_id=(group, to), device_id_type=MESH)

    pl.semaphore_wait(barrier, groups + count - 2)

    def pair(away):
        to = lax.rem(group + away, groups)
        return [
            pltpu.make_async_remote_copy(
                src_ref=src,
                dst_ref=dst,
                send_sem=sems.at[k, away],
                recv_sem=sems.at[k + 2, away],
                device_id=(to, me),
                device_id_type=MESH,
            )
            for k, (src, dst) in enumerate(
                ((over_all.at[to], all_in.at[away]), (over_dp, dp_in.at[away]))
            )
        ]

    def across(away):
        return pltpu.make_async_remote_copy(
            src_ref=own_sum,
            dst_ref=mp_in.at[away],
            send_sem=mp_sems.at[0, away],
            recv_sem=mp_sems.at[1, away],
            device_id=(group, lax.rem(me + away, count)),
            device_id_type=MESH,
        )

    @pl.loop(1, groups)
    def _(away):
        for copy in pair(away):
            copy.start()

    own_sum[...] = over_all[group]
    dp_out[...] = over_dp[...]

    @pl.loop(1, groups)
    def _(away):
        for copy in pair(away):
            copy.wait_recv()
        own_sum[...] = own_sum[...] + all_in[away]
        dp_out[...] = dp_out[...] + dp_in[away]

    @pl.loop(1, count)
    def _(away):
        across(away).start()

    all_out[...] = own_sum[...]

    @pl.loop(1, count)
    def _(away):
        across(away).wait_recv()
        all_out[...] = all_out[...] + mp_in[away]

    @pl.loop(1, groups)
    def _(away):
        for copy in pair(away):
            copy.wait_send()

    @pl.loop(1, count)
    def _(away):
        across(away).wait_send()


def small_call(groups, count, over_all, over_dp):
    return pl.pallas_call(
        functools.partial(small_kernel, groups, count),
        name="small_sums",
        out_shape=(
            jax.ShapeDtypeStruct(over_all.shape[1:], F32),
            jax.ShapeDtypeStruct(over_dp.shape, F32),
        ),
        in_specs=[VMEM] * 2,
        out_specs=(VMEM,) * 2,
        scratch_shapes=[
            pltpu.VMEM(over_all.shape, F32),
            pltpu.VMEM((groups, *over_dp.shape), F32),
            pltpu.VMEM(over_all.shape[1:], F32),
            pltpu.VMEM((count, *over_all.shape[1:]), F32),
            pltpu.SemaphoreType.DMA((4, groups)),
            pltpu.SemaphoreType.DMA((2, count)),
        ],
        compiler_params=params(4),
    )(over_all, over_dp)


def attention_scores(query_low, key_low, slopes, length):
    raw_scores = jnp.einsum("qhe,khe->hqk", query_low, key_low, preferred_element_type=F32)
    places = jnp.arange(query_low.shape[0], dtype=jnp.int32)
    key_place = places.astype(F32)
    scores = (raw_scores + slopes[:, None, None] * key_place[None, None, :]) * 0.125
    allowed = (places[None, :] <= places[:, None]) & (places[None, :] < length)
    return jnp.where(allowed[None], scores, -1000000000.0)


def make_local(groups, count):
    def local(
        hidden,
        cotangent,
        lengths,
        input_gain,
        input_shift,
        triple_weight,
        triple_bias,
        merge_weight,
        merge_bias,
        middle_gain,
        middle_shift,
        expand_weight,
        expand_bias,
        reduce_weight,
        reduce_bias,
    ):
        slot = SLOT
        rows, width = hidden.shape
        head_cols = triple_weight.shape[2]
        units = expand_weight.shape[1]
        local_heads = head_cols // HEAD_DIM
        micro = rows // slot
        me = lax.axis_index("mp")
        slopes = 2.0 ** (
            -8.0
            * (me * local_heads + jnp.arange(local_heads, dtype=jnp.int32) + 1).astype(F32)
            / HEADS
        )
        bias_pair = triple_bias.astype(F32)
        triple_full = lax.all_gather(
            triple_weight.reshape(-1, 3 * head_cols), "dp", axis=0, tiled=True
        )
        merge_full = lax.all_gather(merge_weight, "dp", axis=1, tiled=True)
        expand_full = lax.all_gather(expand_weight, "dp", axis=0, tiled=True)
        reduce_full = lax.all_gather(reduce_weight, "dp", axis=1, tiled=True)
        vectors = jnp.stack(
            [input_gain, input_shift, merge_bias, middle_gain, middle_shift, reduce_bias]
        )
        vectors = lax.all_gather(vectors, "dp", axis=1, tiled=True).astype(F32)
        vectors = jnp.pad(vectors, ((0, 2), (0, 0)))

        def own_rows(array):
            pieces = array.reshape(rows // PIECE, count, PIECE // count, -1)
            mine = lax.dynamic_index_in_dim(pieces, me, axis=1, keepdims=False)
            return mine.reshape(rows // count, -1)

        valid = (jnp.arange(slot, dtype=jnp.int32)[None, :] < lengths[:, None]).reshape(rows, 1)
        own = own_rows(hidden)
        own_valid = own_rows(valid.astype(F32))
        grad_feed = jnp.where(valid, cotangent, jnp.zeros((), BF16))
        own_grad = own_rows(grad_feed)

        normed, _ = norm_parts(hidden.astype(F32))
        norm_in = (normed * vectors[0] + vectors[1]).astype(BF16)
        saved, mixed = [], []
        shape = (slot, local_heads, HEAD_DIM)
        for b in range(micro):
            triple = dot32(norm_in[b * slot : (b + 1) * slot], triple_full)
            query = (triple[:, :head_cols] + bias_pair[0]).astype(BF16).reshape(shape)
            key = triple[:, head_cols : 2 * head_cols].astype(BF16).reshape(shape)
            value = (triple[:, 2 * head_cols :] + bias_pair[1]).astype(BF16).reshape(shape)
            scores = attention_scores(query, key, slopes, lengths[b])
            log_total = jax.nn.logsumexp(scores, axis=-1)
            probs = jnp.exp(scores - log_total[..., None]).astype(BF16)
            heads = jnp.einsum("hqk,khe->qhe", probs, value, preferred_element_type=F32)
            mixed.append(heads.reshape(slot, head_cols).astype(BF16))
            saved.append((query, key, value, log_total))
        mixed = jnp.concatenate(mixed, axis=0)
        norm_mid, residual, sums_one = merge_call(
            count, mixed, merge_full, own, own_valid, vectors
        )
        branch_grad, residual_grad, sums_two, unit_grad, feed_part, expand_grad, reduce_grad = (
            feed_call(
                count,
                norm_mid,
                expand_full,
                reduce_full,
                grad_feed,
                residual,
                own_grad,
                expand_bias.astype(F32)[None],
                vectors,
            )
        )

        def scatter(array, dim):
            return lax.psum_scatter(array, "dp", scatter_dimension=dim, tiled=True).astype(F32)

        reduce_grad = scatter(reduce_grad, 1)
        expand_grad = scatter(expand_grad, 0)
        triples = []
        for b in range(micro):
            query, key, value, log_total = saved[b]
            grad_mixed = dot_nt(branch_grad[b * slot : (b + 1) * slot], merge_full)
            grad_mixed = grad_mixed.astype(BF16).reshape(shape)
            scores = attention_scores(query, key, slopes, lengths[b])
            soft = jnp.exp(scores - log_total[..., None])
            grad_probs = jnp.einsum("qhe,khe->hqk", grad_mixed, value, preferred_element_type=F32)
            grad_value = jnp.einsum(
                "hqk,qhe->khe", soft.astype(BF16), grad_mixed, preferred_element_type=F32
            ).astype(BF16)
            row_terms = jnp.sum(soft * grad_probs, axis=-1, keepdims=True)
            grad_scores = (soft * (grad_probs - row_terms)).astype(BF16)
            grad_query = (
                0.125
                * jnp.einsum("hqk,khe->qhe", grad_scores, key, preferred_element_type=F32)
            ).astype(BF16)
            grad_key = (
                0.125
                * jnp.einsum("hqk,qhe->khe", grad_scores, query, preferred_element_type=F32)
            ).astype(BF16)
            triples.append(
                jnp.concatenate(
                    [
                        grad_query.reshape(slot, head_cols),
                        grad_key.reshape(slot, head_cols),
                        grad_value.reshape(slot, head_cols),
                    ],
                    axis=1,
                )
            )
        grad_triple = jnp.concatenate(triples, axis=0)
        merge_grad = scatter(dot_tn(mixed, branch_grad).astype(BF16), 1)
        triple_grad = scatter(dot_tn(norm_in, grad_triple).astype(BF16), 0)
        column_sums = jnp.sum(grad_triple, axis=0, dtype=F32)

        hidden_grad, output, sums_three = last_call(
            count,
            grad_triple,
            triple_full,
            feed_part,
            own,
            residual,
            residual_grad,
            own_valid,
            vectors,
        )
        squares = jnp.stack(
            [
                jnp.sum(sums_three[2]),
                jnp.sum(sums_one[0]),
                jnp.sum(sums_three[3]),
                jnp.sum(own_valid),
            ]
        )
        over_all = jnp.concatenate([sums_three[0:2], sums_two[0:4]], axis=0)
        over_all = over_all.reshape(6, groups, width // groups).transpose(1, 0, 2)
        over_all = jnp.pad(over_all, ((0, 0), (0, 2), (0, 0)))
        over_all = over_all.at[:, 6, :4].set(squares[None])
        over_dp = jnp.concatenate([column_sums, unit_grad[0]]).reshape(-1, 128)
        tail = (-over_dp.shape[0]) % 8
        over_dp = jnp.pad(over_dp, ((0, tail), (0, 0)))
        return_small, dp_small = small_call(groups, count, over_all, over_dp)
        flat = dp_small.reshape(-1)
        triple_sums = flat[: 3 * head_cols]
        unit_sums = flat[3 * head_cols : 3 * head_cols + units]
        totals = return_small[6, :4]
        root_means = jnp.sqrt(totals[:3] / (totals[3] * width))
        pair_grad = jnp.stack([triple_sums[:head_cols], triple_sums[2 * head_cols :]])
        return (
            output,
            hidden_grad,
            return_small[0],
            return_small[1],
            triple_grad.reshape(-1, 3, head_cols),
            pair_grad,
            merge_grad,
            return_small[2],
            return_small[3],
            return_small[4],
            expand_grad,
            unit_sums,
            reduce_grad,
            return_small[5],
            root_means,
        )

    return local


def solution(mesh):
    return jax.shard_map(
        make_local(mesh.shape["dp"], mesh.shape["mp"]),
        mesh=mesh,
        in_specs=(
            P("dp", None),
            P("dp", None),
            P("dp"),
            P("dp"),
            P("dp"),
            P("dp", None, "mp"),
            P(None, "mp"),
            P("mp", "dp"),
            P("dp"),
            P("dp"),
            P("dp"),
            P("dp", "mp"),
            P("mp"),
            P("mp", "dp"),
            P("dp"),
        ),
        out_specs=(
            P("dp", None),
            P("dp", None),
            P("dp"),
            P("dp"),
            P("dp", None, "mp"),
            P(None, "mp"),
            P("mp", "dp"),
            P("dp"),
            P("dp"),
            P("dp"),
            P("dp", "mp"),
            P("mp"),
            P("mp", "dp"),
            P("dp"),
            P(),
        ),
        check_vma=False,
    )
```

time: 1240 us -> 717 us (0.58)
  waiting for transfers between devices: 730 us -> 21.2 us
  Pallas kernels: 0 us -> 484 us
  matrix products: 242 us -> 63.3 us
  blocking collectives: 105 us -> 10.9 us
  other arithmetic: 108 us -> 60.1 us
  local copies, waits for them, and re-layouts: 25.9 us -> 51.7 us
    pallas_call x0 -> x4, Pallas kernels: none -> 484 us  [the longest x1 220 us: last_call(): pl.pallas_call(functools.partial(last_kernel, count, pieces), name='last_...]
    psum x4 -> x0, waiting for transfers between devices: 466 us -> none  [the longest x1 282 us: local(): lax.psum(feed_part.astype(jnp.bfloat16), 'mp').astype(jnp.float32)]
    dot_general x36 -> x18, matrix products: 242 us -> 63.3 us  [the longest x2 15.4 us: dot_tn(): lax.dot_general(a, b, (((0,), (0,)), ((), ())), preferred_element_type=F32)]
    reduce_scatter x4, waiting for transfers between devices: 153 us -> 0.01 us  [scatter(): lax.psum_scatter(array, 'dp', scatter_dimension=dim, tiled=True).astype(F32)]
    all_gather x4, waiting for transfers between devices: 109 us -> 17.9 us  [the longest x1 17.8 us: local(): lax.all_gather(triple_weight.reshape(-1, 3 * head_cols), 'dp', axis=0, ti...]
    all_gather x6 -> x1, blocking collectives: 55.7 us -> 10.9 us  [local(): vectors = lax.all_gather(vectors, 'dp', axis=1, tiled=True).astype(F32)]
    reduce_sum x11 -> x6, other arithmetic: 51.1 us -> 24.3 us  [the longest x1 16.6 us: local(): column_sums = jnp.sum(grad_triple, axis=0, dtype=F32)]
    psum x1 -> x0, blocking collectives: 25.5 us -> none  [local(): lax.psum((acc_pair_bias, acc_unit_bias, square_sums), 'dp')]
  transfers between devices with their start and end apart: 12 -> 8, of which waited for: 11 -> 1; matrix products, arithmetic and copies ran while one was open for 18% -> 17% of each run, Pallas kernels for 0% -> 49%
where the time goes in v1:
time: 717 us; the launch traced here: 708 us
  Pallas kernels  484 us (68%)
  matrix products  63.3 us (9%)
  other arithmetic  60.1 us (8%)
  local copies, waits for them, and re-layouts  51.7 us (7%)
  waiting for transfers between devices  21.2 us (3%)
  between operations  16.1 us (2%)
  blocking collectives  10.9 us (2%)
    pallas_call x1, Pallas kernels, last_call(): pl.pallas_call(functools.partial(last_kernel, count, pieces), name='last_...  220 us
    pallas_call x1, Pallas kernels, feed_call(): pl.pallas_call(functools.partial(feed_kernel, count, pieces), name='feed_...  136 us
    pallas_call x1, Pallas kernels, merge_call(): pl.pallas_call(functools.partial(merge_kernel, count, pieces), name='merg...  117 us
    unnamed x84, local copies, waits for them, and re-layouts  21.3 us
    all_gather x1, waiting for transfers between devices, local(): lax.all_gather(triple_weight.reshape(-1, 3 * head_cols), 'dp', axis=0, ti...  17.8 us
    reduce_sum x1, other arithmetic, local(): column_sums = jnp.sum(grad_triple, axis=0, dtype=F32)  16.6 us
    dot_general x2, matrix products, dot_tn(): lax.dot_general(a, b, (((0,), (0,)), ((), ())), preferred_element_type=F32)  15.4 us
  transfers between devices with their start and end apart: 8, of which 1 were waited for; matrix products, arithmetic and copies ran while one was open for 17% of the time, Pallas kernels for 49%

profile of v1, /device:TPU:0, one launch (start us, length us, event | category | flops | bytes accessed | tf_op | source)
XLA Modules:
  0.0 707.6 jit_solution(15813602348125494411)
XLA Ops:
  7.3 1.4 copy.62
  14.5 10.9 %all_gather.15 = bf16[6,2048]{1,0:T(8,128)(2,1)S(1)} all-gather(bf16[6,256]{1,0:T(8,128)(2,1)S(1)} %stack.51), channel_id=1, replica_groups=mesh['dp'=8,'mp'=4] {'dp'}, dimensions={1}, use_global_device_ids=true | all-gather | bytes 27648 | tf_op jit(solution)/shard_map/all_gather | solution.py:737
  28.0 2.8 convert_reduce_fusion
  34.6 2.0 copy-done.4
  37.7 3.2 fusion.5
  40.9 17.8 %all-gather.5.cloned.1.call-done.triple = bf16[2048,1536]{1,0:T(8,128)(2,1)} async-done(((bf16[256,1536]{1,0:T(8,128)(2,1)}), bf16[2048,1536]{1,0:T(8,128)(2,1)}) %all-gather.5.cloned.1.call-update) | async-done | bytes 6291472 | tf_op jit(solution)/shard_map/all_gather | solution.py:728
  58.7 6.2 fusion.8
  65.7 2.1 copy.70
  67.8 6.2 fusion.10
  74.1 1.6 copy-done.11
  76.5 2.0 copy.64
  78.6 3.3 fusion.30
  83.2 1.4 copy.68
  85.9 1.4 copy.65
  87.4 3.6 fusion.45
  92.3 1.4 convolution_convert_fusion.5
  95.3 2.1 fusion.44
  98.7 1.4 convolution_convert_fusion.4
  102.4 117.0 %merge_line.1 = (bf16[1024,2048]{1,0:T(8,128)(2,1)}, f32[256,2048]{1,0:T(8,128)}, f32[8,2048]{1,0:T(8,128)}) custom-call(bf16[1024,512]{1,0:T(8,128)(2,1)} %pad_maximum_fusion.mixed, bf16[512,2048]{1,0:T(8,128)(2,1)} %all-gather.7.cloned.1.call-done.merge, bf16[256,2048]{1,0:T(8,128)(2,1)} %bitcast.111, f32[256,1]{1,0:T(8,128)} %reshape.379.valid, ...), custom_call_target="tpu_custom_call" | custom-call | tf_op jit(solution)/shard_map/merge_line/pallas_call | solution.py:299
  219.5 136.0 %feed_line.1 = (bf16[1024,2048]{1,0:T(8,128)(2,1)}, f32[256,2048]{1,0:T(8,128)}, f32[8,2048]{1,0:T(8,128)}, f32[1,2048]{1,0:T(1,128)}, bf16[1024,2048]{1,0:T(8,1...) custom-call(bf16[1024,2048]{1,0:T(8,128)(2,1)} %get-tuple-element.42.middle_hbm, ...), custom_call_target="tpu_custom_call" | custom-call | tf_op jit(solution)/shard_map/feed_line/pallas_call | solution.py:479
  355.5 6.3 convolution_convert_fusion.1
  361.9 3.0 fusion.16
  364.9 5.0 convolution_convert_fusion.3
  369.9 2.2 multiply_reduce_fusion.1
  372.1 2.8 multiply_convert_fusion.1
  374.9 1.4 fusion.23
  380.4 2.2 convolution_convert_fusion.2
  382.6 5.1 multiply_reduce_fusion
  389.7 7.6 %multiply_convert_fusion = bf16[8,512,512]{1,2,0:T(8,128)(2,1)S(1)} fusion(f32[8,512,512]{1,2,0:T(8,128)} %get-tuple-element.118, f32[8,512,512]{1,2,0:T(8,128)} %copy-done, f32[8,512]{1,0:T(8,128)S(1)} %get-tuple-element.117, f32[8,512]{1,0:T(8,128)S(1)} %log_add_fusion), kind=kLoop, calls=%fused_computation.8 | loop fusion | flops 8388608 | bytes 21004288 | tf_op jit(solution)/shard_map/convert_element_type | solution.py:801
  397.4 2.0 copy-done.3
  399.4 1.6 fusion.24
  402.2 4.4 fusion.25
  407.9 16.6 %convert_reduce_fusion.1 = (f32[1536]{0:T(1024)S(1)}, bf16[1024,1536]{1,0:T(8,128)(2,1)S(1)}) fusion(bf16[512,512]{1,0:T(8,128)(2,1)S(1)} %copy.88, bf16[512,512]{1,0:T(8,128)(2,1)S(1)} %copy.87, bf16[512,512]{1,0:T(8,128)(2,1)S(1)} %copy.86, bf16[512,512]{1,0:T(8,128)(2,1)S(1)} %copy.82, bf16[512,512]{1,0:T(8,128)(2,1)S(1)} %copy.81, ...), kind=kLoop, calls=%fused_computation.21 | loop fusion | flops 22018560 | bytes 6297600 | tf_op jit(solution)/shard_map/reduce_sum | solution.py:823
  424.6 1.7 copy-done.5
  426.2 9.1 %convolution_convert_fusion = bf16[2048,1536]{1,0:T(8,128)(2,1)} fusion(bf16[1024,2048]{1,0:T(8,128)(2,1)S(1)} %copy-done.8, bf16[1024,1536]{1,0:T(8,128)(2,1)S(1)} %get-tuple-element.90.triple_grad), kind=kOutput, calls=%fused_computation.18 | convolution fusion | flops 6445596672 | bytes 13631488 | tf_op jit(solution)/shard_map/dot_general | solution.py:32
  436.8 1.5 slice_reduce_fusion.1
  438.9 219.7 %last_line.1 = (bf16[1024,2048]{1,0:T(8,128)(2,1)}, bf16[1024,2048]{1,0:T(8,128)(2,1)}, f32[8,2048]{1,0:T(8,128)}) custom-call(bf16[1024,1536]{1,0:T(8,128)(2,1)} %copy-done.5, bf16[2048,1536]{1,0:T(8,128)(2,1)} %all-gather.5.cloned.1.call-done.triple, bf16[1024,2048]{1,0:T(8,128)(2,1)} %get-tuple-element.45.feed, bf16[256,2048]{1,0:T(8,128)(2,1)} %bitcast.112, ...), custom_call_target="tpu_custom_call" | custom-call | tf_op jit(solution)/shard_map/last_line/pallas_call | solution.py:568
  659.6 1.5 slice_reduce_fusion.2
  661.1 2.7 pad_maximum_fusion.3
  664.7 11.1 %small_sums.1 = (f32[8,256]{1,0:T(8,128)}, f32[32,128]{1,0:T(8,128)}) custom-call(f32[8,8,256]{2,1,0:T(8,128)} %copy-done.23, f32[32,128]{1,0:T(8,128)} %pad.18.over_dp), custom_call_target="tpu_custom_call" | custom-call | tf_op jit(solution)/shard_map/small_sums/pallas_call | solution.py:667
  680.2 1.5 fusion.41
  683.0 1.8 convert_element_type.193
  684.8 1.4 copy.90
  686.2 1.6 copy.91
  687.8 2.7 convert_element_type.195
  690.5 2.9 convert_element_type.194
  693.5 4.8 copy.105
  698.3 2.0 copy.106
  (169 shorter events, 41.1 us)
Async XLA Ops:
  7.2 4.8 copy-start.30
  7.2 4.9 copy-start.31
  7.2 4.9 copy-start.32
  7.2 4.9 copy-start.33
  7.2 4.9 copy-start.34
  7.2 4.9 copy-start.35
  7.2 4.9 copy-start.27
  7.3 5.2 copy-start.28
  7.3 20.7 %copy-start.25 = (bf16[2,512]{1,0:T(2,128)(2,1)S(1)}, bf16[2,512]{1,0:T(2,128)(2,1)}, u32[]{:S(2)}) copy-start(bf16[2,512]{1,0:T(2,128)(2,1)} %param.23) | copy-start | bytes 6148
  7.3 51.4 %all-gather.5.cloned.1.call-start = ((), (), s32[]{:S(2)}) async-start(), calls=%async_computation.4 | async-start | bytes 7077888 | tf_op jit(solution)/shard_map/all_gather | solution.py:728
  9.9 92.5 %all-gather.7.cloned.1.call-start = ((), (), s32[]{:S(2)}) async-start(), calls=%async_computation.5 | async-start | bytes 2359296 | tf_op jit(solution)/shard_map/all_gather | solution.py:731
  10.7 208.8 %all-gather.9.cloned.1.call-start = ((), (), s32[]{:S(2)}) async-start(), calls=%async_computation.6 | async-start | bytes 9437184 | tf_op jit(solution)/shard_map/all_gather | solution.py:732
  11.4 208.1 %all-gather.11.cloned.1.call-start = ((), (), s32[]{:S(2)}) async-start(), calls=%async_computation.7 | async-start | bytes 9437184 | tf_op jit(solution)/shard_map/all_gather | solution.py:733
  12.0 671.0 %reduce-scatter.7.cloned.1.call-start = ((), (), s32[]{:S(2)}) async-start(), calls=%async_computation.9 | async-start | bytes 2359296 | tf_op jit(solution)/shard_map/reduce_scatter | solution.py:785
  14.5 16.3 %copy-start.2 = (bf16[1024,2048]{1,0:T(8,128)(2,1)S(1)}, bf16[1024,2048]{1,0:T(8,128)(2,1)}, u32[]{:S(2)}) copy-start(bf16[1024,2048]{1,0:T(8,128)(2,1)} %param.17) | copy-start | bytes 12582916
  14.5 19.7 %copy-start.9 = (bf16[1024,2048]{1,0:T(8,128)(2,1)S(1)}, bf16[1024,2048]{1,0:T(8,128)(2,1)}, u32[]{:S(2)}) copy-start(bf16[1024,2048]{1,0:T(8,128)(2,1)} %param.18) | copy-start | bytes 12582916
  34.6 2.0 copy-start.4
  74.1 1.6 copy-start.11
  83.2 12.2 %copy-start.14 = (bf16[512,512]{0,1:T(8,128)(2,1)}, bf16[512,512]{0,1:T(8,128)(2,1)S(1)}, u32[]{:S(2)}) copy-start(bf16[512,512]{0,1:T(8,128)(2,1)S(1)} %copy.69) | copy-start | bytes 1572868
  85.9 6.4 copy-start.6
  87.4 3.7 copy-start.17
  91.0 3.3 copy-start.1
  92.3 3.1 copy-start.12
  97.4 3.6 copy-start
  98.7 2.6 copy-start.21
  101.3 1.1 copy-start.22
  355.5 6.4 copy-start.19
  361.9 8.0 %slice-start.2 = ((s8[8388608]{0:T(1024)(128)(4,1)}), s8[4194304]{0:T(1024)(128)(4,1)S(1)}, s32[]{:S(2)}) async-start(s8[8388608]{0:T(1024)(128)(4,1)} %bitcast.107), calls=%async_computation.14 | async-start | bytes 8388608
  364.9 5.0 copy-start.7
  364.9 5.0 slice-start.3
  372.1 2.8 copy-start.18
  372.1 4.2 copy-start.16
  374.9 2.2 copy-start.20
  374.9 2.8 copy-start.29
  374.9 4.1 slice-start
  376.3 4.0 slice-start.1
  387.7 297.1 %reduce-scatter.5.cloned.1.call-start = ((), (), s32[]{:S(2)}) async-start(), calls=%async_computation.8 | async-start | bytes 7077888 | tf_op jit(solution)/shard_map/reduce_scatter | solution.py:785
  389.7 9.7 %copy-start.13 = (bf16[512,512]{0,1:T(8,128)(2,1)S(1)}, bf16[512,512]{0,1:T(8,128)(2,1)}, u32[]{:S(2)}) copy-start(bf16[512,512]{0,1:T(8,128)(2,1)} %copy.70) | copy-start | bytes 1572868
  397.4 2.0 copy-start.3
  399.4 2.9 copy-start.15
  407.9 18.3 %copy-start.8 = (bf16[1024,2048]{1,0:T(8,128)(2,1)S(1)}, bf16[1024,2048]{1,0:T(8,128)(2,1)}, u32[]{:S(2)}) copy-start(bf16[1024,2048]{1,0:T(8,128)(2,1)} %fusion.5) | copy-start | bytes 12582916
  424.6 1.7 copy-start.5
  435.3 252.5 %reduce-scatter.11.cloned.1.call-start = ((), (), s32[]{:S(2)}) async-start(), calls=%async_computation.11 | async-start | bytes 9437184 | tf_op jit(solution)/shard_map/reduce_scatter | solution.py:785
  436.1 2.2 copy-start.24
  436.1 2.2 copy-start.26
  436.1 254.4 %reduce-scatter.9.cloned.1.call-start = ((), (), s32[]{:S(2)}) async-start(), calls=%async_computation.10 | async-start | bytes 9437184 | tf_op jit(solution)/shard_map/reduce_scatter | solution.py:785
  664.1 0.6 copy-start.23
  690.5 7.7 %copy-start.10 = (bf16[1024,2048]{1,0:T(8,128)(2,1)S(1)}, bf16[1024,2048]{1,0:T(8,128)(2,1)}, u32[]{:S(2)}) copy-start(bf16[1024,2048]{1,0:T(8,128)(2,1)} %get-tuple-element.137) | copy-start | bytes 12582916
Sparse Core Ops, SparseCore 0:
  10.5 48.1 all-gather.4
  60.6 28.0 all-gather.6
  90.6 54.3 all-gather.8
  146.7 55.9 all-gather.10
  387.9 39.1 reduce-scatter.6
  435.4 59.3 reduce-scatter.4
  498.3 71.2 reduce-scatter.10
  573.1 71.5 reduce-scatter.8

commit v2 on v1

--- a/solution.py
+++ b/solution.py
@@ -252,14 +252,60 @@
     return pieces + 2 * LAG * (count - 1)
 
 
+def cost(micros):
+    return pl.CostEstimate(flops=int(micros * 1e9), bytes_accessed=1 << 20, transcendentals=0)
+
+
 def params(index):
     return pltpu.CompilerParams(
         collective_id=index, has_side_effects=True, vmem_limit_bytes=63 << 20
     )
 
 
-def merge_kernel(count, pieces, mixed, merge, own, valid, vectors, middle, residual, sums, part, acc, *rest):
+def tiles_of(rows):
+    return [(start, min(TILE, rows - start)) for start in range(0, rows, TILE)]
+
+
+def spread(work, parts):
+    return [work[len(work) * k // parts : len(work) * (k + 1) // parts] for k in range(parts)]
+
+
+def paced(line_tick, tiles, steps, later, drain):
+    step = 0
+    plans = [spread(work, size // PIECE) for (_, size), work in zip(tiles, later)]
+    assert len(later) == len(tiles) and len(drain) == steps - sum(map(len, plans))
+    for shares in (*plans, drain):
+        span = len(shares)
+
+        @pl.loop(0, span)
+        def _(k, step=step, shares=shares):
+            line_tick(step + k)
+            for phase, share in enumerate(shares):
+                if share:
+
+                    @pl.when(k == phase)
+                    def _(share=share):
+                        for closure in share:
+                            closure()
+
+        step += span
+
+
+def halves(values):
+    low = lax.broadcasted_iota(jnp.int32, values.shape, 1) < HEAD_DIM
+    zero = jnp.zeros((), values.dtype)
+    return jnp.where(low, values, zero), jnp.where(low, zero, values)
+
+
+PAIR = 2 * HEAD_DIM
+
+
+def front_kernel(
+    count, head_cols, slopes, norm_in, weights, shift, own, valid, segment_col, segment_row, place_row, vectors,
+    middle, residual, sums, qkv, mixed, totals, part, acc, mask, *rest,
+):
     line = Line(count, part, middle, rest[0], rest[1:])
+    rows_all, width = middle.shape
     greet(count)
     sums[...] = jnp.zeros_like(sums)
 
@@ -273,46 +319,97 @@
         line.share(piece, (normed * vectors[3:4, :] + vectors[4:5, :]).astype(BF16))
         sums[0:1, :] += jnp.sum(branch * branch * valid[rows, :], axis=0, keepdims=True)
 
-    ratio = TILE // PIECE
-
-    @pl.loop(0, ticks(count, pieces))
-    def _(step):
-        @pl.when(jnp.logical_and(step < pieces, lax.rem(step, ratio) == 0))
-        def _():
-            rows = block(step // ratio, TILE)
-
-            @pl.loop(0, part.shape[1] // BLOCK)
-            def _(k):
-                cols = block(k, BLOCK)
-                part[rows, cols] = dot32(mixed[rows, :], merge[:, cols]).astype(BF16)
-
-        tick(line, step, finish)
-
-    @pl.loop(0, pieces)
+    def project(start, size):
+        rows = pl.ds(start, size)
+
+        @pl.loop(0, 3 * head_cols // BLOCK)
+        def _(k):
+            cols = block(k, BLOCK)
+            qkv[rows, cols] = (dot32(norm_in[rows, :], weights[:, cols]) + shift[:, cols]).astype(BF16)
+
+    def masks(start, size):
+        keys = start + size
+        row = lax.broadcasted_iota(jnp.int32, (size, keys), 0) + start
+        col = lax.broadcasted_iota(jnp.int32, (size, keys), 1)
+        same = segment_col[start : start + size, :] == segment_row[:, :keys]
+        mask[:size, :keys] = jnp.where(jnp.logical_and(same, col <= row), 1.0, 0.0)
+
+    def attend(start, size, pair):
+        keys = start + size
+        query = halves(qkv[pl.ds(start, size), block(pair, PAIR)])
+        key = qkv[:keys, pl.ds(pl.multiple_of(head_cols + pair * PAIR, PAIR), PAIR)]
+        value = halves(qkv[:keys, pl.ds(pl.multiple_of(2 * head_cols + pair * PAIR, PAIR), PAIR)])
+        out = jnp.zeros((size, PAIR), F32)
+        for k in range(2):
+            scores = dot_nt(query[k], key) + slopes[2 * pair + k] * place_row[:, :keys]
+            scores = jnp.where(mask[:size, :keys] > 0.5, scores * 0.125, -1000000000.0)
+            most = jnp.max(scores, axis=1, keepdims=True)
+            raised = jnp.exp(scores - most)
+            total = jnp.sum(raised, axis=1, keepdims=True)
+            out = out + dot32((raised * (1.0 / total)).astype(BF16), value[k])
+            totals[pair, pl.ds(start, size), k : k + 1] = most + jnp.log(total)
+        mixed[pl.ds(start, size), block(pair, PAIR)] = out.astype(BF16)
+
+    def project_back(start, size):
+        rows = pl.ds(start, size)
+
+        @pl.loop(0, width // BLOCK)
+        def _(k):
+            cols = block(k, BLOCK)
+            part[rows, cols] = dot_nt(mixed[rows, :], weights[cols, 3 * head_cols :]).astype(BF16)
+
+    pairs = head_cols // PAIR
+
+    def work(start, size):
+        return [
+            functools.partial(project, start, size),
+            functools.partial(masks, start, size),
+            *[functools.partial(attend, start, size, pair) for pair in range(pairs)],
+            functools.partial(project_back, start, size),
+        ]
+
+    tiles = tiles_of(rows_all)
+    for closure in work(*tiles[0]):
+        closure()
+    later = [work(*tile) for tile in tiles[1:]] + [[]]
+    steps = ticks(count, line.pieces)
+    drain = [[]] * (steps - line.pieces)
+    paced(lambda step: tick(line, step, finish), tiles, steps, later, drain)
+
+    @pl.loop(0, line.pieces)
     def _(piece):
         line.settle(piece)
 
 
-def merge_call(count, mixed, merge, own, valid, vectors):
-    rows, width = mixed.shape[0], merge.shape[1]
+SMEM = pl.BlockSpec(memory_space=pltpu.SMEM)
+
+
+def front_call(count, slopes, norm_in, weights, shift, own, valid, segments, vectors):
+    rows, width = norm_in.shape
+    head_cols = weights.shape[1] // 4
     pieces = rows // PIECE
     return pl.pallas_call(
-        functools.partial(merge_kernel, count, pieces),
-        name="merge_line",
+        functools.partial(front_kernel, count, head_cols),
+        name="front_line",
         out_shape=(
             jax.ShapeDtypeStruct((rows, width), BF16),
             jax.ShapeDtypeStruct((rows // count, width), F32),
             jax.ShapeDtypeStruct((8, width), F32),
+            jax.ShapeDtypeStruct((rows, 3 * head_cols), BF16),
+            jax.ShapeDtypeStruct((rows, head_cols), BF16),
+            jax.ShapeDtypeStruct((head_cols // PAIR, rows, 128), F32),
         ),
-        in_specs=[VMEM] * 5,
-        out_specs=(VMEM,) * 3,
+        in_specs=[SMEM] + [VMEM] * 9,
+        out_specs=(VMEM,) * 6,
         scratch_shapes=[
             pltpu.VMEM((rows, width), BF16),
             pltpu.VMEM((PIECE // count, width), F32),
+            pltpu.VMEM((TILE, rows), F32),
             *Line.scratch(count, pieces, width),
         ],
         compiler_params=params(1),
-    )(mixed, merge, own, valid, vectors)
+        cost_estimate=cost(120),
+    )(slopes, norm_in, weights, shift, own, valid, *segments[:3], vectors)
 
 
 def feed_kernel(
@@ -505,18 +602,237 @@
             *Line.scratch(count, pieces, width),
         ],
         compiler_params=params(2),
+        cost_estimate=cost(130),
     )(middle, expand, reduce, grad, residual, own_grad, unit_shift, vectors)
 
 
-def last_kernel(
-    count, pieces, triple_grad, triple, feed, own, residual, residual_grad, valid, vectors,
-    hidden_grad, output, sums, part, acc, *rest,
+def back_kernel(
+    count, head_cols, slopes, branch_grad, merge, qkv, mixed, norm_in, totals, segment_col, segment_row, place_col,
+    feed, residual, valid, vectors,
+    triple_grad, column_sums, output, sums, weight_out,
+    mixed_grad, key_grad, value_grad, acc, mask, stage, stage_sem, *rest,
 ):
-    half = len(rest) // 2
-    line = Line(count, part, hidden_grad, rest[0], rest[1:half])
-    feed_line = Line(count, feed, output, rest[half], rest[half + 1 :])
+    line = Line(count, feed, output, rest[0], rest[1:])
+    rows_all, width = output.shape
     greet(count)
     sums[...] = jnp.zeros_like(sums)
+    column_sums[...] = jnp.zeros_like(column_sums)
+
+    def finish(piece):
+        line.total(piece, acc)
+        rows = line.own(piece)
+        branch = acc[...] + vectors[5:6, :]
+        keep = valid[rows, :] > 0.5
+        result = jnp.where(keep, residual[rows, :] + branch, 0.0)
+        line.share(piece, result.astype(BF16))
+        branch = jnp.where(keep, branch, 0.0)
+        sums[0:1, :] += jnp.sum(result * result, axis=0, keepdims=True)
+        sums[1:2, :] += jnp.sum(branch * branch, axis=0, keepdims=True)
+
+    def open_tile(start, size):
+        rows = pl.ds(start, size)
+        mixed_grad[rows, :] = dot32(branch_grad[rows, :], merge[...]).astype(BF16)
+        keys = start + size
+        row = lax.broadcasted_iota(jnp.int32, (keys, size), 1) + start
+        col = lax.broadcasted_iota(jnp.int32, (keys, size), 0)
+        same = segment_row[:keys, :] == segment_col[:, start : start + size]
+        mask[:keys, :size] = jnp.where(jnp.logical_and(same, col <= row), 1.0, 0.0)
+
+    def back(start, size, first, pair):
+        keys = start + size
+        rows, cols = pl.ds(start, size), block(pair, PAIR)
+        query = halves(qkv[rows, cols])
+        key = qkv[:keys, pl.ds(pl.multiple_of(head_cols + pair * PAIR, PAIR), PAIR)]
+        value = qkv[:keys, pl.ds(pl.multiple_of(2 * head_cols + pair * PAIR, PAIR), PAIR)]
+        grad = halves(mixed_grad[rows, cols])
+        keys_apart = halves(key)
+        query_grad = jnp.zeros((size, PAIR), F32)
+        key_sum = jnp.zeros((keys, PAIR), F32)
+        value_sum = jnp.zeros((keys, PAIR), F32)
+        for k in range(2):
+            scores = dot_nt(key, query[k]) + slopes[2 * pair + k] * place_col[:keys, :]
+            scores = jnp.where(mask[:keys, :size] > 0.5, scores * 0.125, -1000000000.0)
+            soft = jnp.exp(scores - totals[2 * pair + k : 2 * pair + k + 1, rows])
+            grad_probs = dot_nt(value, grad[k])
+            row_terms = jnp.sum(soft * grad_probs, axis=0, keepdims=True)
+            grad_scores = (soft * (grad_probs - row_terms)).astype(BF16)
+            value_sum = value_sum + dot32(soft.astype(BF16), grad[k])
+            key_sum = key_sum + dot32(grad_scores, query[k])
+            query_grad = query_grad + dot_tn(grad_scores, keys_apart[k])
+        triple_grad[rows, cols] = (0.125 * query_grad).astype(BF16)
+        if first:
+            key_grad[:keys, cols] = key_sum
+            value_grad[:keys, cols] = value_sum
+        else:
+            key_grad[:keys, cols] += key_sum
+            value_grad[:keys, cols] += value_sum
+
+    def close_tile(start, size):
+        rows = pl.ds(start, size)
+        triple_grad[rows, head_cols : 2 * head_cols] = (0.125 * key_grad[rows, :]).astype(BF16)
+        triple_grad[rows, 2 * head_cols :] = value_grad[rows, :].astype(BF16)
+        column_sums[...] += jnp.sum(triple_grad[rows, :].astype(F32), axis=0, keepdims=True)
+
+    def put(slot, target):
+        return pltpu.make_async_copy(stage.at[slot], target, stage_sem.at[slot])
+
+    def job(index, left, right, r, c, shift):
+        slot = index % 2
+        r, c, to = pl.ds(r, BLOCK), pl.ds(c, BLOCK), pl.ds(c + shift, BLOCK)
+        if index >= 2:
+            put(slot, weight_out.at[r, to]).wait()
+        stage[slot] = dot_tn(left[:, r], right[:, c]).astype(BF16)
+        put(slot, weight_out.at[r, to]).start()
+
+    pairs = head_cols // PAIR
+
+    def work(start, size, first):
+        return [
+            functools.partial(open_tile, start, size),
+            *[functools.partial(back, start, size, first, pair) for pair in range(pairs)],
+            functools.partial(close_tile, start, size),
+        ]
+
+    tiles = tiles_of(rows_all)
+    products = [
+        (branch_grad, mixed, r, c, 3 * head_cols)
+        for r in range(0, width, BLOCK)
+        for c in range(0, head_cols, BLOCK)
+    ] + [
+        (norm_in, triple_grad, r, c, 0)
+        for r in range(0, width, BLOCK)
+        for c in range(0, 3 * head_cols, BLOCK)
+    ]
+    jobs = [functools.partial(job, k, *product) for k, product in enumerate(products)]
+    later = [work(*tile, k == 0) for k, tile in enumerate(reversed(tiles))]
+    steps = ticks(count, line.pieces)
+    drain = spread(jobs, steps - line.pieces)
+    paced(lambda step: tick(line, step, finish), tiles, steps, later, drain)
+    for slot in range(2):
+        put(slot, weight_out.at[pl.ds(0, BLOCK), pl.ds(0, BLOCK)]).wait()
+
+    @pl.loop(0, line.pieces)
+    def _(piece):
+        line.settle(piece)
+
+
+def back_call(count, slopes, branch_grad, weights, qkv, mixed, norm_in, totals, segments, feed, residual, valid, vectors):
+    rows, width = branch_grad.shape
+    head_cols = weights.shape[1] // 4
+    merge_spec = pl.BlockSpec((width, head_cols), lambda i: (0, 3), memory_space=pltpu.VMEM)
+    pieces = rows // PIECE
+    return pl.pallas_call(
+        functools.partial(back_kernel, count, head_cols),
+        name="back_line",
+        out_shape=(
+            jax.ShapeDtypeStruct((rows, 3 * head_cols), BF16),
+            jax.ShapeDtypeStruct((1, 3 * head_cols), F32),
+            jax.ShapeDtypeStruct((rows, width), BF16),
+            jax.ShapeDtypeStruct((8, width), F32),
+            jax.ShapeDtypeStruct((width, 4 * head_cols), BF16),
+        ),
+        grid=(1,),
+        in_specs=[SMEM, VMEM, merge_spec] + [VMEM] * 11,
+        out_specs=(VMEM,) * 4 + (ANY,),
+        scratch_shapes=[
+            pltpu.VMEM((rows, head_cols), BF16),
+            pltpu.VMEM((rows, head_cols), F32),
+            pltpu.VMEM((rows, head_cols), F32),
+            pltpu.VMEM((PIECE // count, width), F32),
+            pltpu.VMEM((rows, TILE), F32),
+            pltpu.VMEM((2, BLOCK, BLOCK), BF16),
+            pltpu.SemaphoreType.DMA((2,)),
+            *Line.scratch(count, pieces, width),
+        ],
+        compiler_params=params(3),
+        cost_estimate=cost(120),
+    )(slopes, branch_grad, weights, qkv, mixed, norm_in, totals, *segments[3:], feed, residual, valid, vectors)
+
+
+def greet_all(groups, count):
+    me, group = lax.axis_index("mp"), lax.axis_index("dp")
+    barrier = pltpu.get_barrier_semaphore()
+
+    @pl.loop(1, groups)
+    def _(away):
+        to = lax.rem(group + away, groups)
+        pl.semaphore_signal(barrier, inc=1, device_id=(to, me), device_id_type=MESH)
+
+    @pl.loop(1, count)
+    def _(away):
+        to = lax.rem(me + away, count)
+        pl.semaphore_signal(barrier, inc=1, device_id=(group, to), device_id_type=MESH)
+
+    pl.semaphore_wait(barrier, groups + count - 2)
+
+
+def last_kernel(
+    groups, count, triple_grad, triple, own, residual_grad, known, over_dp, vectors,
+    hidden_grad, all_out, dp_out, sums, cut, all_in, dp_in, own_sum, mp_in, sems, mp_sems, part, acc, *rest,
+):
+    line = Line(count, part, hidden_grad, rest[0], rest[1:])
+    me, group = line.me, line.group
+    span = own_sum.shape[0]
+    blocks = cut.shape[0]
+    greet_all(groups, count)
+    sums[...] = known[...]
+
+    def copy_to(src, dst, out, into, to):
+        return pltpu.make_async_remote_copy(
+            src_ref=src, dst_ref=dst, send_sem=out, recv_sem=into, device_id=to, device_id_type=MESH
+        )
+
+    def dp_copy(away):
+        to = lax.rem(group + away, groups)
+        return copy_to(over_dp, dp_in.at[away], sems.at[0, away], sems.at[1, away], (to, me))
+
+    def block_copy(away):
+        to = lax.rem(group + away, groups)
+        src = cut.at[pl.ds(to * blocks // groups, span)]
+        return copy_to(src, all_in.at[away], sems.at[2, away], sems.at[3, away], (to, me))
+
+    def mp_copy(away):
+        to = lax.rem(me + away, count)
+        return copy_to(own_sum, mp_in.at[away], mp_sems.at[0, away], mp_sems.at[1, away], (group, to))
+
+    @pl.loop(1, groups)
+    def _(away):
+        dp_copy(away).start()
+
+    def send_blocks():
+        for k in range(blocks):
+            cut[k] = sums[:, 128 * k : 128 * (k + 1)]
+
+        @pl.loop(1, groups)
+        def _(away):
+            block_copy(away).start()
+
+    def add_blocks():
+        own_sum[...] = cut[pl.ds(group * blocks // groups, span)]
+
+        @pl.loop(1, groups)
+        def _(away):
+            block_copy(away).wait_recv()
+            own_sum[...] = own_sum[...] + all_in[away]
+
+        @pl.loop(1, count)
+        def _(away):
+            mp_copy(away).start()
+
+    def add_rest():
+        dp_out[...] = over_dp[...]
+
+        @pl.loop(1, groups)
+        def _(away):
+            dp_copy(away).wait_recv()
+            dp_out[...] = dp_out[...] + dp_in[away]
+
+        all_out[...] = own_sum[...]
+
+        @pl.loop(1, count)
+        def _(away):
+            mp_copy(away).wait_recv()
+            all_out[...] = all_out[...] + mp_in[away]
 
     def finish(piece):
         line.total(piece, acc)
@@ -528,170 +844,75 @@
         sums[0:1, :] += jnp.sum(grad_in * normed, axis=0, keepdims=True)
         sums[1:2, :] += jnp.sum(grad_in, axis=0, keepdims=True)
 
-    def finish_feed(piece):
-        feed_line.total(piece, acc)
-        rows = feed_line.own(piece)
-        branch = acc[...] + vectors[5:6, :]
-        keep = valid[rows, :] > 0.5
-        result = jnp.where(keep, residual[rows, :] + branch, 0.0)
-        feed_line.share(piece, result.astype(BF16))
-        branch = jnp.where(keep, branch, 0.0)
-        sums[2:3, :] += jnp.sum(result * result, axis=0, keepdims=True)
-        sums[3:4, :] += jnp.sum(branch * branch, axis=0, keepdims=True)
-
-    ratio = TILE // PIECE
-
-    @pl.loop(0, ticks(count, pieces))
-    def _(step):
-        tick(feed_line, step, finish_feed)
-
-        @pl.when(jnp.logical_and(step < pieces, lax.rem(step, ratio) == 0))
-        def _():
-            rows = block(step // ratio, TILE)
-
-            @pl.loop(0, part.shape[1] // BLOCK)
-            def _(k):
-                cols = block(k, BLOCK)
-                part[rows, cols] = dot_nt(triple_grad[rows, :], triple[cols, :]).astype(BF16)
-
-        tick(line, step, finish)
-
-    @pl.loop(0, pieces)
+    tiles = tiles_of(part.shape[0])
+
+    def product(start, size, c):
+        part[pl.ds(start, size), c : c + BLOCK] = dot_nt(
+            triple_grad[pl.ds(start, size), :], triple[c : c + BLOCK, :]
+        ).astype(BF16)
+
+    def work(start, size):
+        return [functools.partial(product, start, size, c) for c in range(0, part.shape[1], BLOCK)]
+
+    for closure in work(*tiles[0]):
+        closure()
+    later = [work(*tile) for tile in tiles[1:]] + [[]]
+    steps = ticks(count, line.pieces)
+    done = LAG * (count - 1) - 1
+    drain = [[] for _ in range(steps - line.pieces)]
+    drain[done].append(send_blocks)
+    drain[done + 2 * LAG].append(add_blocks)
+    paced(lambda step: tick(line, step, finish), tiles, steps, later, drain)
+    add_rest()
+
+    @pl.loop(0, line.pieces)
     def _(piece):
         line.settle(piece)
-        feed_line.settle(piece)
-
-
-def last_call(count, triple_grad, triple, feed, own, residual, residual_grad, valid, vectors):
-    rows, width = feed.shape
+
+    @pl.loop(1, groups)
+    def _(away):
+        dp_copy(away).wait_send()
+        block_copy(away).wait_send()
+
+    @pl.loop(1, count)
+    def _(away):
+        mp_copy(away).wait_send()
+
+
+def last_call(groups, count, triple_grad, weights, own, residual_grad, known, over_dp, vectors):
+    rows, columns = triple_grad.shape
+    width = weights.shape[0]
+    triple_spec = pl.BlockSpec((width, columns), lambda i: (0, 0), memory_space=pltpu.VMEM)
     pieces = rows // PIECE
+    blocks = width // 128
+    span = max(1, blocks // groups)
     return pl.pallas_call(
-        functools.partial(last_kernel, count, pieces),
+        functools.partial(last_kernel, groups, count),
         name="last_line",
         out_shape=(
             jax.ShapeDtypeStruct((rows, width), BF16),
-            jax.ShapeDtypeStruct((rows, width), BF16),
-            jax.ShapeDtypeStruct((8, width), F32),
+            jax.ShapeDtypeStruct((span, 8, 128), F32),
+            jax.ShapeDtypeStruct(over_dp.shape, F32),
         ),
-        in_specs=[VMEM] * 8,
+        grid=(1,),
+        in_specs=[VMEM, triple_spec] + [VMEM] * 5,
         out_specs=(VMEM,) * 3,
         scratch_shapes=[
+            pltpu.VMEM((8, width), F32),
+            pltpu.VMEM((blocks, 8, 128), F32),
+            pltpu.VMEM((groups, span, 8, 128), F32),
+            pltpu.VMEM((groups, *over_dp.shape), F32),
+            pltpu.VMEM((span, 8, 128), F32),
+            pltpu.VMEM((count, span, 8, 128), F32),
+            pltpu.SemaphoreType.DMA((4, groups)),
+            pltpu.SemaphoreType.DMA((2, count)),
             pltpu.VMEM((rows, width), BF16),
             pltpu.VMEM((PIECE // count, width), F32),
             *Line.scratch(count, pieces, width),
-            *Line.scratch(count, pieces, width),
         ],
-        compiler_params=params(3),
-    )(triple_grad, triple, feed, own, residual, residual_grad, valid, vectors)
-
-
-def small_kernel(groups, count, over_all, over_dp, all_out, dp_out, all_in, dp_in, own_sum, mp_in, sems, mp_sems):
-    me, group = lax.axis_index("mp"), lax.axis_index("dp")
-    barrier = pltpu.get_barrier_semaphore()
-
-    @pl.loop(1, groups)
-    def _(away):
-        to = lax.rem(group + away, groups)
-        pl.semaphore_signal(barrier, inc=1, device_id=(to, me), device_id_type=MESH)
-
-    @pl.loop(1, count)
-    def _(away):
-        to = lax.rem(me + away, count)
-        pl.semaphore_signal(barrier, inc=1, device_id=(group, to), device_id_type=MESH)
-
-    pl.semaphore_wait(barrier, groups + count - 2)
-
-    def pair(away):
-        to = lax.rem(group + away, groups)
-        return [
-            pltpu.make_async_remote_copy(
-                src_ref=src,
-                dst_ref=dst,
-                send_sem=sems.at[k, away],
-                recv_sem=sems.at[k + 2, away],
-                device_id=(to, me),
-                device_id_type=MESH,
-            )
-            for k, (src, dst) in enumerate(
-                ((over_all.at[to], all_in.at[away]), (over_dp, dp_in.at[away]))
-            )
-        ]
-
-    def across(away):
-        return pltpu.make_async_remote_copy(
-            src_ref=own_sum,
-            dst_ref=mp_in.at[away],
-            send_sem=mp_sems.at[0, away],
-            recv_sem=mp_sems.at[1, away],
-            device_id=(group, lax.rem(me + away, count)),
-            device_id_type=MESH,
-        )
-
-    @pl.loop(1, groups)
-    def _(away):
-        for copy in pair(away):
-            copy.start()
-
-    own_sum[...] = over_all[group]
-    dp_out[...] = over_dp[...]
-
-    @pl.loop(1, groups)
-    def _(away):
-        for copy in pair(away):
-            copy.wait_recv()
-        own_sum[...] = own_sum[...] + all_in[away]
-        dp_out[...] = dp_out[...] + dp_in[away]
-
-    @pl.loop(1, count)
-    def _(away):
-        across(away).start()
-
-    all_out[...] = own_sum[...]
-
-    @pl.loop(1, count)
-    def _(away):
-        across(away).wait_recv()
-        all_out[...] = all_out[...] + mp_in[away]
-
-    @pl.loop(1, groups)
-    def _(away):
-        for copy in pair(away):
-            copy.wait_send()
-
-    @pl.loop(1, count)
-    def _(away):
-        across(away).wait_send()
-
-
-def small_call(groups, count, over_all, over_dp):
-    return pl.pallas_call(
-        functools.partial(small_kernel, groups, count),
-        name="small_sums",
-        out_shape=(
-            jax.ShapeDtypeStruct(over_all.shape[1:], F32),
-            jax.ShapeDtypeStruct(over_dp.shape, F32),
-        ),
-        in_specs=[VMEM] * 2,
-        out_specs=(VMEM,) * 2,
-        scratch_shapes=[
-            pltpu.VMEM(over_all.shape, F32),
-            pltpu.VMEM((groups, *over_dp.shape), F32),
-            pltpu.VMEM(over_all.shape[1:], F32),
-            pltpu.VMEM((count, *over_all.shape[1:]), F32),
-            pltpu.SemaphoreType.DMA((4, groups)),
-            pltpu.SemaphoreType.DMA((2, count)),
-        ],
-        compiler_params=params(4),
-    )(over_all, over_dp)
-
-
-def attention_scores(query_low, key_low, slopes, length):
-    raw_scores = jnp.einsum("qhe,khe->hqk", query_low, key_low, preferred_element_type=F32)
-    places = jnp.arange(query_low.shape[0], dtype=jnp.int32)
-    key_place = places.astype(F32)
-    scores = (raw_scores + slopes[:, None, None] * key_place[None, None, :]) * 0.125
-    allowed = (places[None, :] <= places[:, None]) & (places[None, :] < length)
-    return jnp.where(allowed[None], scores, -1000000000.0)
+        compiler_params=params(5),
+        cost_estimate=cost(115),
+    )(triple_grad, weights, own, residual_grad, known, over_dp, vectors)
 
 
 def make_local(groups, count):
@@ -717,7 +938,6 @@
         head_cols = triple_weight.shape[2]
         units = expand_weight.shape[1]
         local_heads = head_cols // HEAD_DIM
-        micro = rows // slot
         me = lax.axis_index("mp")
         slopes = 2.0 ** (
             -8.0
@@ -725,10 +945,8 @@
             / HEADS
         )
         bias_pair = triple_bias.astype(F32)
-        triple_full = lax.all_gather(
-            triple_weight.reshape(-1, 3 * head_cols), "dp", axis=0, tiled=True
-        )
-        merge_full = lax.all_gather(merge_weight, "dp", axis=1, tiled=True)
+        first = jnp.concatenate([triple_weight.reshape(-1, 3 * head_cols), merge_weight.T], axis=1)
+        first_full = lax.all_gather(first, "dp", axis=0, tiled=True)
         expand_full = lax.all_gather(expand_weight, "dp", axis=0, tiled=True)
         reduce_full = lax.all_gather(reduce_weight, "dp", axis=1, tiled=True)
         vectors = jnp.stack(
@@ -750,23 +968,24 @@
 
         normed, _ = norm_parts(hidden.astype(F32))
         norm_in = (normed * vectors[0] + vectors[1]).astype(BF16)
-        saved, mixed = [], []
-        shape = (slot, local_heads, HEAD_DIM)
-        for b in range(micro):
-            triple = dot32(norm_in[b * slot : (b + 1) * slot], triple_full)
-            query = (triple[:, :head_cols] + bias_pair[0]).astype(BF16).reshape(shape)
-            key = triple[:, head_cols : 2 * head_cols].astype(BF16).reshape(shape)
-            value = (triple[:, 2 * head_cols :] + bias_pair[1]).astype(BF16).reshape(shape)
-            scores = attention_scores(query, key, slopes, lengths[b])
-            log_total = jax.nn.logsumexp(scores, axis=-1)
-            probs = jnp.exp(scores - log_total[..., None]).astype(BF16)
-            heads = jnp.einsum("hqk,khe->qhe", probs, value, preferred_element_type=F32)
-            mixed.append(heads.reshape(slot, head_cols).astype(BF16))
-            saved.append((query, key, value, log_total))
-        mixed = jnp.concatenate(mixed, axis=0)
-        norm_mid, residual, sums_one = merge_call(
-            count, mixed, merge_full, own, own_valid, vectors
-        )
+        seats = jnp.arange(rows, dtype=jnp.int32)
+        segment = seats // slot
+        places = lax.rem(seats, slot).astype(F32)
+        as_key = jnp.where(valid[:, 0], segment, -1)
+        as_query = jnp.where(valid[:, 0], segment, -2)
+        segments = (
+            as_query[:, None],
+            as_key[None, :],
+            places[None, :],
+            as_query[None, :],
+            as_key[:, None],
+            places[:, None],
+        )
+        shift = jnp.concatenate([bias_pair[0], jnp.zeros_like(bias_pair[0]), bias_pair[1]])[None]
+        norm_mid, residual, sums_one, qkv, mixed, totals = front_call(
+            count, slopes, norm_in, first_full, shift, own, own_valid, segments, vectors
+        )
+        totals = totals[:, :, :2].transpose(0, 2, 1).reshape(local_heads, rows)
         branch_grad, residual_grad, sums_two, unit_grad, feed_part, expand_grad, reduce_grad = (
             feed_call(
                 count,
@@ -782,94 +1001,73 @@
         )
 
         def scatter(array, dim):
-            return lax.psum_scatter(array, "dp", scatter_dimension=dim, tiled=True).astype(F32)
+            own_block = lax.psum_scatter(array, "dp", scatter_dimension=dim, tiled=True)
+            return own_block.astype(F32)
 
         reduce_grad = scatter(reduce_grad, 1)
         expand_grad = scatter(expand_grad, 0)
-        triples = []
-        for b in range(micro):
-            query, key, value, log_total = saved[b]
-            grad_mixed = dot_nt(branch_grad[b * slot : (b + 1) * slot], merge_full)
-            grad_mixed = grad_mixed.astype(BF16).reshape(shape)
-            scores = attention_scores(query, key, slopes, lengths[b])
-            soft = jnp.exp(scores - log_total[..., None])
-            grad_probs = jnp.einsum("qhe,khe->hqk", grad_mixed, value, preferred_element_type=F32)
-            grad_value = jnp.einsum(
-                "hqk,qhe->khe", soft.astype(BF16), grad_mixed, preferred_element_type=F32
-            ).astype(BF16)
-            row_terms = jnp.sum(soft * grad_probs, axis=-1, keepdims=True)
-            grad_scores = (soft * (grad_probs - row_terms)).astype(BF16)
-            grad_query = (
-                0.125
-                * jnp.einsum("hqk,khe->qhe", grad_scores, key, preferred_element_type=F32)
-            ).astype(BF16)
-            grad_key = (
-                0.125
-                * jnp.einsum("hqk,qhe->khe", grad_scores, query, preferred_element_type=F32)
-            ).astype(BF16)
-            triples.append(
-                jnp.concatenate(
-                    [
-                        grad_query.reshape(slot, head_cols),
-                        grad_key.reshape(slot, head_cols),
-                        grad_value.reshape(slot, head_cols),
-                    ],
-                    axis=1,
-                )
-            )
-        grad_triple = jnp.concatenate(triples, axis=0)
-        merge_grad = scatter(dot_tn(mixed, branch_grad).astype(BF16), 1)
-        triple_grad = scatter(dot_tn(norm_in, grad_triple).astype(BF16), 0)
-        column_sums = jnp.sum(grad_triple, axis=0, dtype=F32)
-
-        hidden_grad, output, sums_three = last_call(
+        grad_triple, column_sums, output, sums_three, first_grad = back_call(
             count,
-            grad_triple,
-            triple_full,
+            slopes,
+            branch_grad,
+            first_full,
+            qkv,
+            mixed,
+            norm_in,
+            totals,
+            segments,
             feed_part,
-            own,
             residual,
-            residual_grad,
             own_valid,
             vectors,
         )
+        first_grad = scatter(first_grad, 0)
+        triple_grad = first_grad[:, : 3 * head_cols]
+        merge_grad = first_grad[:, 3 * head_cols :].T
         squares = jnp.stack(
             [
-                jnp.sum(sums_three[2]),
+                jnp.sum(sums_three[0]),
                 jnp.sum(sums_one[0]),
-                jnp.sum(sums_three[3]),
+                jnp.sum(sums_three[1]),
                 jnp.sum(own_valid),
             ]
         )
-        over_all = jnp.concatenate([sums_three[0:2], sums_two[0:4]], axis=0)
-        over_all = over_all.reshape(6, groups, width // groups).transpose(1, 0, 2)
-        over_all = jnp.pad(over_all, ((0, 0), (0, 2), (0, 0)))
-        over_all = over_all.at[:, 6, :4].set(squares[None])
-        over_dp = jnp.concatenate([column_sums, unit_grad[0]]).reshape(-1, 128)
+        lanes = jnp.tile(jnp.pad(squares, (0, 124)), width // 128)
+        known = jnp.concatenate(
+            [jnp.zeros((2, width), F32), sums_two[:4], lanes[None], jnp.zeros((1, width), F32)]
+        )
+        over_dp = jnp.concatenate([column_sums[0], unit_grad[0]]).reshape(-1, 128)
         tail = (-over_dp.shape[0]) % 8
         over_dp = jnp.pad(over_dp, ((0, tail), (0, 0)))
-        return_small, dp_small = small_call(groups, count, over_all, over_dp)
+        hidden_grad, small, dp_small = last_call(
+            groups, count, grad_triple, first_full, own, residual_grad, known, over_dp, vectors
+        )
+        share = width // groups
+        small = small.transpose(1, 0, 2).reshape(8, -1)
+        totals = small[6, :4]
+        if share < 128:
+            place = lax.rem(lax.axis_index("dp") * share, 128)
+            small = lax.dynamic_slice_in_dim(small, place, share, axis=1)
         flat = dp_small.reshape(-1)
         triple_sums = flat[: 3 * head_cols]
         unit_sums = flat[3 * head_cols : 3 * head_cols + units]
-        totals = return_small[6, :4]
         root_means = jnp.sqrt(totals[:3] / (totals[3] * width))
         pair_grad = jnp.stack([triple_sums[:head_cols], triple_sums[2 * head_cols :]])
         return (
             output,
             hidden_grad,
-            return_small[0],
-            return_small[1],
+            small[0],
+            small[1],
             triple_grad.reshape(-1, 3, head_cols),
             pair_grad,
             merge_grad,
-            return_small[2],
-            return_small[3],
-            return_small[4],
+            small[2],
+            small[3],
+            small[4],
             expand_grad,
             unit_sums,
             reduce_grad,
-            return_small[5],
+            small[5],
             root_means,
         )
 
@@ -877,8 +1075,10 @@
 
 
 def solution(mesh):
+    local = make_local(mesh.shape["dp"], mesh.shape["mp"])
+
     return jax.shard_map(
-        make_local(mesh.shape["dp"], mesh.shape["mp"]),
+        local,
         mesh=mesh,
         in_specs=(
             P("dp", None),

time: 717 us -> 698 us (0.974)
  waiting for transfers between devices: 21.2 us -> 95.4 us
  matrix products: 63.3 us -> 0 us
  other arithmetic: 60.1 us -> 29.3 us
  Pallas kernels: 484 us -> 509 us
  local copies, waits for them, and re-layouts: 51.7 us -> 33 us
    reduce_scatter x4 -> x3, waiting for transfers between devices: 0.01 us -> 70.5 us  [scatter(): own_block = lax.psum_scatter(array, 'dp', scatter_dimension=dim, tiled=True)]
    dot_general x18 -> x0, matrix products: 63.3 us -> none  [the longest x2 15.4 us: dot_tn(): lax.dot_general(a, b, (((0,), (0,)), ((), ())), preferred_element_type=F32)]
    pallas_call x3, Pallas kernels: 348 us -> 373 us  [the longest x1 126 us: front_call(): pl.pallas_call(functools.partial(front_kernel, count, head_cols), name='f...]
    reduce_sum x4 -> x1, other arithmetic: 20.6 us -> 1.54 us  [local(): jnp.sum(sums_three[0])]
    convert_element_type x7 -> x4, other arithmetic: 21.2 us -> 6.32 us  [the longest x3 5.73 us: scatter(): return own_block.astype(F32)]
    unnamed x84 -> x42, local copies, waits for them, and re-layouts: 21.3 us -> 16 us
    all_gather x2 -> x1, waiting for transfers between devices: 17.8 us -> 22.9 us  [local(): first_full = lax.all_gather(first, 'dp', axis=0, tiled=True)]
  transfers between devices with their start and end apart: 8 -> 6, of which waited for: 1 -> 2; matrix products, arithmetic and copies ran while one was open for 17% -> 7% of each run, Pallas kernels for 49% -> 36%
where the time goes in v2:
time: 698 us; the launch traced here: 693 us
  Pallas kernels  509 us (73%)
  waiting for transfers between devices  95.4 us (14%)
  local copies, waits for them, and re-layouts  33 us (5%)
  other arithmetic  29.3 us (4%)
  between operations  15.4 us (2%)
  blocking collectives  10.8 us (2%)
    pallas_call x1, Pallas kernels, feed_call(): pl.pallas_call(functools.partial(feed_kernel, count, pieces), name='feed_...  136 us
    pallas_call x1, Pallas kernels, front_call(): pl.pallas_call(functools.partial(front_kernel, count, head_cols), name='f...  126 us
    pallas_call x1, Pallas kernels, last_call(): pl.pallas_call(functools.partial(last_kernel, groups, count), name='last_...  125 us
    pallas_call x1, Pallas kernels, back_call(): pl.pallas_call(functools.partial(back_kernel, count, head_cols), name='ba...  123 us
    reduce_scatter x3, waiting for transfers between devices, scatter(): own_block = lax.psum_scatter(array, 'dp', scatter_dimension=dim, tiled=True)  70.5 us
    all_gather x1, waiting for transfers between devices, local(): first_full = lax.all_gather(first, 'dp', axis=0, tiled=True)  22.9 us
    unnamed x42, local copies, waits for them, and re-layouts  16 us
  transfers between devices with their start and end apart: 6, of which 2 were waited for; matrix products, arithmetic and copies ran while one was open for 7% of the time, Pallas kernels for 36%

profile of v2, /device:TPU:0, one launch (start us, length us, event | category | flops | bytes accessed | tf_op | source)
XLA Modules:
  0.0 693.0 jit_solution(3127238910880325921)
XLA Ops:
  7.2 1.1 copy.38
  8.4 1.4 copy.37
  10.1 1.1 pad_maximum_fusion
  11.3 0.7 all-gather.6.cloned.1.call-update
  12.1 0.7 all-gather.8.cloned.1.call-update
  12.8 0.6 fusion.13.place_row
  14.3 2.8 convert_reduce_fusion
  17.1 0.6 broadcast_in_dim.47.shift
  17.8 0.6 broadcast_in_dim.56
  18.4 10.8 %all_gather.12 = bf16[6,2048]{1,0:T(8,128)(2,1)S(1)} all-gather(bf16[6,256]{1,0:T(8,128)(2,1)S(1)} %stack.51), channel_id=1, replica_groups=mesh['dp'=8,'mp'=4] {'dp'}, dimensions={1}, use_global_device_ids=true | all-gather | bytes 27648 | tf_op jit(solution)/shard_map/all_gather | solution.py:955
  29.2 0.6 pad.12.vectors
  29.8 0.7 fusion.17
  30.5 0.8 reshape.309.valid
  31.6 3.6 fusion.2
  35.1 0.6 broadcast_select_fusion.1
  35.7 1.3 fusion.9
  37.4 2.1 copy-done.2
  39.5 1.2 copy-done
  40.7 1.6 constant_dynamic-slice_fusion
  42.3 3.2 fusion.5.norm_in
  45.5 22.9 %all-gather.4.cloned.1.call-done.weights.merge.triple = bf16[2048,2048]{1,0:T(8,128)(2,1)} async-done(((bf16[256,2048]{1,0:T(8,128)(2,1)}), bf16[2048,2048]{1,0:T(8,128)(2,1)}) %all-gather.4.cloned.1.call-update) | async-done | bytes 8388624 | tf_op jit(solution)/shard_map/all_gather | solution.py:949
  68.4 125.5 %front_line.1 = (bf16[1024,2048]{1,0:T(8,128)(2,1)}, f32[256,2048]{1,0:T(8,128)}, f32[8,2048]{1,0:T(8,128)}, bf16[1024,1536]{1,0:T(8,128)(2,1)}, bf16[1024,512]{1,0:T(8,128)(2,1)}, /*index=5*/f32[4,1024,128]{2,1,0:T(8,128)}) custom-call(f32[8]{0:T(128)} %multiply_power_fusion.slopes, bf16[1024,2048]{1,0:T(8,128)(2,1)} %fusion.5.norm_in, ...), custom_call_target="tpu_custom_call" | custom-call | flops 120000004096 | bytes 1048576 | tf_op jit(solution)/shard_map/front_line/pallas_call | solution.py:391
  194.0 1.7 slice_bitcast_fusion
  195.7 0.6 copy.44
  196.3 0.7 reshape.304.totals
  197.0 135.9 %feed_line.1 = (bf16[1024,2048]{1,0:T(8,128)(2,1)}, f32[256,2048]{1,0:T(8,128)}, f32[8,2048]{1,0:T(8,128)}, f32[1,2048]{1,0:T(1,128)}, bf16[1024,2048]{1,0:T(8,1...) custom-call(bf16[1024,2048]{1,0:T(8,128)(2,1)} %get-tuple-element.36.middle_hbm, ...), custom_call_target="tpu_custom_call" | custom-call | flops 130000003072 | bytes 1048576 | tf_op jit(solution)/shard_map/feed_line/pallas_call | solution.py:576
  332.9 122.6 %back_line.1 = (bf16[1024,1536]{1,0:T(8,128)(2,1)}, f32[1,1536]{1,0:T(1,128)}, bf16[1024,2048]{1,0:T(8,128)(2,1)}, f32[8,2048]{1,0:T(8,128)}, bf16[2048,2048]{1,0:T(8,128)(2,1)}) custom-call(f32[8]{0:T(128)} %multiply_power_fusion.slopes, bf16[1024,2048]{1,0:T(8,128)(2,1)} %get-tuple-element.38.branch_grad, ...), custom_call_target="tpu_custom_call" | custom-call | flops 120000004096 | bytes 1048576 | tf_op jit(solution)/shard_map/back_line/pallas_call | solution.py:724
  456.6 0.6 pad.14.over_dp
  457.2 1.5 slice_reduce_fusion.1
  458.6 1.5 slice_reduce_fusion.2
  460.2 2.7 select_maximum_fusion
  462.9 0.7 maximum_maximum_fusion.known
  463.6 124.6 %last_line.1 = (bf16[1024,2048]{1,0:T(8,128)(2,1)}, f32[2,8,128]{2,1,0:T(8,128)}, f32[32,128]{1,0:T(8,128)}) custom-call(bf16[1024,1536]{1,0:T(8,128)(2,1)} %get-tuple-element.44.triple_grad, bf16[2048,2048]{1,0:T(8,128)(2,1)} %all-gather.4.cloned.1.call-done.weights.merge.triple, bf16[256,2048]{1,0:T(8,128)(2,1)} %bitcast.66, ...), custom_call_target="tpu_custom_call" | custom-call | flops 115000000512 | bytes 1048576 | tf_op jit(solution)/shard_map/last_line/pallas_call | solution.py:889
  588.2 1.3 slice.124
  590.2 0.7 fusion.20
  590.8 0.6 pad_maximum_fusion.2
  591.4 1.2 fusion.15
  592.6 1.5 fusion.21
  594.2 1.3 slice_bitcast_fusion.2
  595.5 2.6 slice.117
  598.0 1.9 copy.47
  600.0 1.6 copy.48
  601.9 1.0 copy.49
  602.9 2.7 convert_element_type.72
  605.6 70.5 %reduce-scatter.6.cloned.1.call-done = bf16[256,2048]{1,0:T(8,128)(2,1)} async-done(((bf16[2048,2048]{1,0:T(8,128)(2,1)}), bf16[256,2048]{1,0:T(8,128)(2,1)}) %reduce-scatter.6.cloned.1.call-update) | async-done | bytes 1048592 | tf_op jit(solution)/shard_map/reduce_scatter | solution.py:1004
  676.1 2.8 convert_element_type.71
  678.9 4.9 copy.57
  683.9 2.0 copy.58
  (79 shorter events, 3.2 us)
Async XLA Ops:
  7.2 61.3 %all-gather.4.cloned.1.call-start = ((), (), s32[]{:S(2)}) async-start(), calls=%async_computation.3 | async-start | bytes 9437184 | tf_op jit(solution)/shard_map/all_gather | solution.py:949
  8.3 5.6 copy-start.11
  8.3 5.6 copy-start.12
  8.3 5.6 copy-start.13
  8.4 5.6 copy-start.14
  8.4 5.6 copy-start.15
  8.4 5.6 copy-start.16
  8.4 5.6 copy-start.10
  11.2 5.9 copy-start.6
  11.2 6.5 copy-start.9
  11.3 185.7 %all-gather.6.cloned.1.call-start = ((), (), s32[]{:S(2)}) async-start(), calls=%async_computation.4 | async-start | bytes 9437184 | tf_op jit(solution)/shard_map/all_gather | solution.py:950
  12.0 185.0 %all-gather.8.cloned.1.call-start = ((), (), s32[]{:S(2)}) async-start(), calls=%async_computation.5 | async-start | bytes 9437184 | tf_op jit(solution)/shard_map/all_gather | solution.py:951
  12.7 582.7 %reduce-scatter.4.cloned.1.call-start = ((), (), s32[]{:S(2)}) async-start(), calls=%async_computation.6 | async-start | bytes 9437184 | tf_op jit(solution)/shard_map/reduce_scatter | solution.py:1004
  31.5 5.5 copy-start.3
  37.0 3.7 copy-start
  37.4 2.1 copy-start.2
  455.6 147.3 %reduce-scatter.8.cloned.1.call-start = ((), (), s32[]{:S(2)}) async-start(), calls=%async_computation.8 | async-start | bytes 9437184 | tf_op jit(solution)/shard_map/reduce_scatter | solution.py:1004
  455.6 0.8 copy-start.5
  455.7 0.8 copy-start.8
  455.7 0.9 copy-start.7
  456.2 219.9 %reduce-scatter.6.cloned.1.call-start = ((), (), s32[]{:S(2)}) async-start(), calls=%async_computation.7 | async-start | bytes 9437184 | tf_op jit(solution)/shard_map/reduce_scatter | solution.py:1004
  595.5 6.1 copy-start.1
  678.9 4.9 copy-start.4
Sparse Core Ops, SparseCore 0:
  11.4 57.0 all-gather.3
  70.3 54.2 all-gather.5
  126.5 55.9 all-gather.7
  455.7 70.1 reduce-scatter.3
  529.3 71.9 reduce-scatter.7
  604.6 71.5 reduce-scatter.5

commit v3 on v2

--- a/solution.py
+++ b/solution.py
@@ -70,10 +70,10 @@
 
 
 class Line:
-    def __init__(self, count, part, inbox, extra, sems):
-        self.count, self.part, self.inbox, self.extra = count, part, inbox, extra
+    def __init__(self, count, part, result, inbox, extra, *sems):
+        self.count, self.part, self.inbox, self.extra, self.result = count, part, inbox, extra, result
         self.pieces = part.shape[0] // PIECE
-        self.sum_out, self.sum_in, self.extra_in, self.own_out, self.all_out, self.all_in = sems
+        self.sum_out, self.sum_in, self.extra_in, self.own_out, self.all_out, self.all_in, self.flushed = sems
         self.rows = PIECE // count
         self.me, self.group = lax.axis_index("mp"), lax.axis_index("dp")
 
@@ -81,6 +81,7 @@
     def scratch(count, pieces, width):
         rows = PIECE // count
         return [
+            pltpu.VMEM((pieces * PIECE, width), BF16),
             pltpu.VMEM((pieces * rows, width), BF16),
             pltpu.SemaphoreType.DMA((pieces, count)),
             pltpu.SemaphoreType.DMA((pieces, count)),
@@ -88,6 +89,7 @@
             pltpu.SemaphoreType.DMA((pieces,)),
             pltpu.SemaphoreType.DMA((pieces, count)),
             pltpu.SemaphoreType.DMA((pieces, count)),
+            pltpu.SemaphoreType.DMA((pieces,)),
         ]
 
     def at(self, piece, owner):
@@ -217,8 +219,16 @@
             def _():
                 self.all_copy(piece, owner, me - 1).start()
 
+    def flush_copy(self, piece):
+        rows = block(piece, PIECE)
+        return pltpu.make_async_copy(self.inbox.at[rows], self.result.at[rows], self.flushed.at[piece])
+
+    def flush(self, piece):
+        self.flush_copy(piece).start()
+
     def settle(self, piece):
         me, last = self.me, self.count - 1
+        self.flush_copy(piece).wait()
         for owner in range(self.count):
 
             @pl.when(me != owner)
@@ -246,6 +256,7 @@
     when(step - LAG * last, finish)
     for away in range(1, line.count):
         when(step - LAG * (last + away), line.forward, away)
+    when(step - LAG * 2 * last, line.flush)
 
 
 def ticks(count, pieces):
@@ -301,11 +312,28 @@
 
 
 def front_kernel(
-    count, head_cols, slopes, norm_in, weights, shift, own, valid, segment_col, segment_row, place_row, vectors,
-    middle, residual, sums, qkv, mixed, totals, part, acc, mask, *rest,
+    count, head_cols, slopes, norm_hbm, weights_hbm, shift, own, valid, segment_col, segment_row, place_row, vectors,
+    middle, residual, sums, qkv_hbm, mixed_hbm, totals,
+    norm_in, weights, qkv, mixed, load_sem, save_sem, part, acc, mask, *rest,
 ):
-    line = Line(count, part, middle, rest[0], rest[1:])
+    line = Line(count, part, middle, *rest)
     rows_all, width = middle.shape
+    tiles = tiles_of(rows_all)
+    blocks = weights.shape[1] // BLOCK
+
+    def load_rows(k):
+        rows = pl.ds(tiles[k][0], tiles[k][1])
+        return pltpu.make_async_copy(norm_hbm.at[rows], norm_in.at[rows], load_sem.at[0, k])
+
+    def load_columns(k):
+        cols = block(k, BLOCK)
+        return pltpu.make_async_copy(weights_hbm.at[:, cols], weights.at[:, cols], load_sem.at[1, k])
+
+    load_rows(0).start()
+    for k in range(blocks):
+        load_columns(k).start()
+    for k in range(1, len(tiles)):
+        load_rows(k).start()
     greet(count)
     sums[...] = jnp.zeros_like(sums)
 
@@ -321,10 +349,13 @@
 
     def project(start, size):
         rows = pl.ds(start, size)
+        load_rows(start // TILE).wait()
 
         @pl.loop(0, 3 * head_cols // BLOCK)
         def _(k):
             cols = block(k, BLOCK)
+            if start == 0:
+                load_columns(k).wait()
             qkv[rows, cols] = (dot32(norm_in[rows, :], weights[:, cols]) + shift[:, cols]).astype(BF16)
 
     def masks(start, size):
@@ -340,6 +371,8 @@
         key = qkv[:keys, pl.ds(pl.multiple_of(head_cols + pair * PAIR, PAIR), PAIR)]
         value = halves(qkv[:keys, pl.ds(pl.multiple_of(2 * head_cols + pair * PAIR, PAIR), PAIR)])
         out = jnp.zeros((size, PAIR), F32)
+        sums_log = jnp.zeros((size, 128), F32)
+        lane = lax.broadcasted_iota(jnp.int32, (size, 128), 1)
         for k in range(2):
             scores = dot_nt(query[k], key) + slopes[2 * pair + k] * place_row[:, :keys]
             scores = jnp.where(mask[:size, :keys] > 0.5, scores * 0.125, -1000000000.0)
@@ -347,11 +380,15 @@
             raised = jnp.exp(scores - most)
             total = jnp.sum(raised, axis=1, keepdims=True)
             out = out + dot32((raised * (1.0 / total)).astype(BF16), value[k])
-            totals[pair, pl.ds(start, size), k : k + 1] = most + jnp.log(total)
+            sums_log = jnp.where(lane == k, most + jnp.log(total), sums_log)
+        totals[2 * pair : 2 * pair + 2, start : start + size] = sums_log.T[:2, :]
         mixed[pl.ds(start, size), block(pair, PAIR)] = out.astype(BF16)
 
     def project_back(start, size):
         rows = pl.ds(start, size)
+        if start == 0:
+            for k in range(3 * head_cols // BLOCK, blocks):
+                load_columns(k).wait()
 
         @pl.loop(0, width // BLOCK)
         def _(k):
@@ -368,13 +405,23 @@
             functools.partial(project_back, start, size),
         ]
 
-    tiles = tiles_of(rows_all)
+    saves = (
+        pltpu.make_async_copy(qkv, qkv_hbm, save_sem.at[0]),
+        pltpu.make_async_copy(mixed, mixed_hbm, save_sem.at[1]),
+    )
+
+    def save():
+        for copy in saves:
+            copy.start()
+
     for closure in work(*tiles[0]):
         closure()
-    later = [work(*tile) for tile in tiles[1:]] + [[]]
+    later = [work(*tile) for tile in tiles[1:]] + [[save]]
     steps = ticks(count, line.pieces)
     drain = [[]] * (steps - line.pieces)
     paced(lambda step: tick(line, step, finish), tiles, steps, later, drain)
+    for copy in saves:
+        copy.wait()
 
     @pl.loop(0, line.pieces)
     def _(piece):
@@ -397,11 +444,17 @@
             jax.ShapeDtypeStruct((8, width), F32),
             jax.ShapeDtypeStruct((rows, 3 * head_cols), BF16),
             jax.ShapeDtypeStruct((rows, head_cols), BF16),
-            jax.ShapeDtypeStruct((head_cols // PAIR, rows, 128), F32),
+            jax.ShapeDtypeStruct((head_cols // HEAD_DIM, rows), F32),
         ),
-        in_specs=[SMEM] + [VMEM] * 9,
-        out_specs=(VMEM,) * 6,
+        in_specs=[SMEM] + [ANY] * 2 + [VMEM] * 7,
+        out_specs=(ANY, VMEM, VMEM, ANY, ANY, VMEM),
         scratch_shapes=[
+            pltpu.VMEM((rows, width), BF16),
+            pltpu.VMEM(weights.shape, BF16),
+            pltpu.VMEM((rows, 3 * head_cols), BF16),
+            pltpu.VMEM((rows, head_cols), BF16),
+            pltpu.SemaphoreType.DMA((2, max(len(tiles_of(rows)), weights.shape[1] // BLOCK))),
+            pltpu.SemaphoreType.DMA((2,)),
             pltpu.VMEM((rows, width), BF16),
             pltpu.VMEM((PIECE // count, width), F32),
             pltpu.VMEM((TILE, rows), F32),
@@ -417,7 +470,7 @@
     branch_grad, residual_grad, sums, unit_grad, feed_hbm, expand_grad, reduce_grad,
     middle, expand, reduce, grad, active, pre_grad, part, acc, stage, load_sem, stage_sem, *rest,
 ):
-    line = Line(count, part, branch_grad, rest[0], rest[1:])
+    line = Line(count, part, branch_grad, *rest)
     units = expand.shape[1]
     width = expand.shape[0]
     blocks = units // BLOCK
@@ -586,7 +639,7 @@
             jax.ShapeDtypeStruct((units, width), BF16),
         ),
         in_specs=[ANY] * 4 + [VMEM] * 4,
-        out_specs=(VMEM,) * 4 + (ANY,) * 3,
+        out_specs=(ANY,) + (VMEM,) * 3 + (ANY,) * 3,
         scratch_shapes=[
             pltpu.VMEM((rows, width), BF16),
             pltpu.VMEM((width, units), BF16),
@@ -607,14 +660,36 @@
 
 
 def back_kernel(
-    count, head_cols, slopes, branch_grad, merge, qkv, mixed, norm_in, totals, segment_col, segment_row, place_col,
-    feed, residual, valid, vectors,
+    count, head_cols, slopes, branch_hbm, merge, qkv, mixed, norm_hbm, totals, segment_col, segment_row, place_col,
+    feed_hbm, residual_hbm, valid, vectors,
     triple_grad, column_sums, output, sums, weight_out,
+    branch_grad, norm_in, feed, residual, load_sem, save_sem,
     mixed_grad, key_grad, value_grad, acc, mask, stage, stage_sem, *rest,
 ):
-    line = Line(count, feed, output, rest[0], rest[1:])
+    line = Line(count, feed, output, *rest)
     rows_all, width = output.shape
+    tiles = tiles_of(rows_all)
+
+    def load_feed(k):
+        rows = pl.ds(tiles[k][0], tiles[k][1])
+        return pltpu.make_async_copy(feed_hbm.at[rows], feed.at[rows], load_sem.at[0, k])
+
+    def load_grad(k):
+        rows = pl.ds(tiles[k][0], tiles[k][1])
+        return pltpu.make_async_copy(branch_hbm.at[rows], branch_grad.at[rows], load_sem.at[1, k])
+
+    load_residual = pltpu.make_async_copy(residual_hbm, residual, load_sem.at[2, 0])
+    load_norm = pltpu.make_async_copy(norm_hbm, norm_in, load_sem.at[2, 1])
+    load_feed(0).start()
+    load_grad(len(tiles) - 1).start()
+    load_residual.start()
+    for k in range(1, len(tiles)):
+        load_feed(k).start()
+        load_grad(len(tiles) - 1 - k).start()
+    load_norm.start()
     greet(count)
+    load_feed(0).wait()
+    load_residual.wait()
     sums[...] = jnp.zeros_like(sums)
     column_sums[...] = jnp.zeros_like(column_sums)
 
@@ -631,6 +706,7 @@
 
     def open_tile(start, size):
         rows = pl.ds(start, size)
+        load_grad(start // TILE).wait()
         mixed_grad[rows, :] = dot32(branch_grad[rows, :], merge[...]).astype(BF16)
         keys = start + size
         row = lax.broadcasted_iota(jnp.int32, (keys, size), 1) + start
@@ -693,7 +769,6 @@
             functools.partial(close_tile, start, size),
         ]
 
-    tiles = tiles_of(rows_all)
     products = [
         (branch_grad, mixed, r, c, 3 * head_cols)
         for r in range(0, width, BLOCK)
@@ -705,6 +780,9 @@
     ]
     jobs = [functools.partial(job, k, *product) for k, product in enumerate(products)]
     later = [work(*tile, k == 0) for k, tile in enumerate(reversed(tiles))]
+    for k in range(1, len(tiles)):
+        later[k - 1].append(lambda k=k: load_feed(k).wait())
+    later[-1].append(load_norm.wait)
     steps = ticks(count, line.pieces)
     drain = spread(jobs, steps - line.pieces)
     paced(lambda step: tick(line, step, finish), tiles, steps, later, drain)
@@ -732,9 +810,15 @@
             jax.ShapeDtypeStruct((width, 4 * head_cols), BF16),
         ),
         grid=(1,),
-        in_specs=[SMEM, VMEM, merge_spec] + [VMEM] * 11,
-        out_specs=(VMEM,) * 4 + (ANY,),
+        in_specs=[SMEM, ANY, merge_spec, VMEM, VMEM, ANY] + [VMEM] * 4 + [ANY] * 2 + [VMEM] * 2,
+        out_specs=(VMEM, VMEM, ANY, VMEM, ANY),
         scratch_shapes=[
+            pltpu.VMEM((rows, width), BF16),
+            pltpu.VMEM((rows, width), BF16),
+            pltpu.VMEM((rows, width), BF16),
+            pltpu.VMEM((rows // count, width), F32),
+            pltpu.SemaphoreType.DMA((3, max(2, len(tiles_of(rows))))),
+            pltpu.SemaphoreType.DMA((2,)),
             pltpu.VMEM((rows, head_cols), BF16),
             pltpu.VMEM((rows, head_cols), F32),
             pltpu.VMEM((rows, head_cols), F32),
@@ -767,15 +851,41 @@
 
 
 def last_kernel(
-    groups, count, triple_grad, triple, own, residual_grad, known, over_dp, vectors,
-    hidden_grad, all_out, dp_out, sums, cut, all_in, dp_in, own_sum, mp_in, sems, mp_sems, part, acc, *rest,
+    groups, count, triple_grad, triple_hbm, own, residual_grad, front_sums, feed_sums, back_sums, valid,
+    column_sums, unit_grad, vectors,
+    hidden_grad, all_out, dp_out,
+    triple, load_sem, sums, over_dp, cut, all_in, dp_in, own_sum, mp_in, sems, mp_sems, part, acc, *rest,
 ):
-    line = Line(count, part, hidden_grad, rest[0], rest[1:])
+    line = Line(count, part, hidden_grad, *rest)
     me, group = line.me, line.group
     span = own_sum.shape[0]
     blocks = cut.shape[0]
+    columns = triple.shape[1]
+
+    def load(k):
+        rows = block(k, BLOCK)
+        return pltpu.make_async_copy(
+            triple_hbm.at[rows, pl.ds(0, columns)], triple.at[rows], load_sem.at[k]
+        )
+
+    for k in range(triple.shape[0] // BLOCK):
+        load(k).start()
     greet_all(groups, count)
-    sums[...] = known[...]
+    sums[0:2, :] = jnp.zeros_like(sums[0:2, :])
+    sums[2:6, :] = feed_sums[0:4, :]
+    sums[6:8, :] = jnp.zeros_like(sums[6:8, :])
+    lane = lax.broadcasted_iota(jnp.int32, (1, 128), 1)
+    squares = jnp.zeros((1, 128), F32)
+    for k, row in enumerate((back_sums[0:1, :], front_sums[0:1, :], back_sums[1:2, :])):
+        squares = jnp.where(lane == k, jnp.sum(row, axis=1, keepdims=True), squares)
+    tokens = jnp.sum(valid[...], axis=0, keepdims=True)
+    squares = jnp.where(lane == 3, tokens, squares)
+    over_dp[...] = jnp.zeros_like(over_dp)
+    wide = column_sums.shape[1] // 128
+    for k in range(wide):
+        over_dp[k : k + 1, :] = column_sums[:, 128 * k : 128 * (k + 1)]
+    for k in range(unit_grad.shape[1] // 128):
+        over_dp[wide + k : wide + k + 1, :] = unit_grad[:, 128 * k : 128 * (k + 1)]
 
     def copy_to(src, dst, out, into, to):
         return pltpu.make_async_remote_copy(
@@ -802,6 +912,7 @@
     def send_blocks():
         for k in range(blocks):
             cut[k] = sums[:, 128 * k : 128 * (k + 1)]
+            cut[k, 6:7, :] = squares
 
         @pl.loop(1, groups)
         def _(away):
@@ -847,6 +958,8 @@
     tiles = tiles_of(part.shape[0])
 
     def product(start, size, c):
+        if start == 0:
+            load(c // BLOCK).wait()
         part[pl.ds(start, size), c : c + BLOCK] = dot_nt(
             triple_grad[pl.ds(start, size), :], triple[c : c + BLOCK, :]
         ).astype(BF16)
@@ -879,10 +992,10 @@
         mp_copy(away).wait_send()
 
 
-def last_call(groups, count, triple_grad, weights, own, residual_grad, known, over_dp, vectors):
+def last_call(groups, count, triple_grad, weights, own, residual_grad, sums, valid, column_sums, unit_grad, vectors):
     rows, columns = triple_grad.shape
     width = weights.shape[0]
-    triple_spec = pl.BlockSpec((width, columns), lambda i: (0, 0), memory_space=pltpu.VMEM)
+    apart = (-(-(columns + unit_grad.shape[1]) // 1024) * 8, 128)
     pieces = rows // PIECE
     blocks = width // 128
     span = max(1, blocks // groups)
@@ -892,16 +1005,18 @@
         out_shape=(
             jax.ShapeDtypeStruct((rows, width), BF16),
             jax.ShapeDtypeStruct((span, 8, 128), F32),
-            jax.ShapeDtypeStruct(over_dp.shape, F32),
+            jax.ShapeDtypeStruct(apart, F32),
         ),
-        grid=(1,),
-        in_specs=[VMEM, triple_spec] + [VMEM] * 5,
-        out_specs=(VMEM,) * 3,
+        in_specs=[VMEM, ANY] + [VMEM] * 9,
+        out_specs=(ANY, VMEM, VMEM),
         scratch_shapes=[
+            pltpu.VMEM((width, columns), BF16),
+            pltpu.SemaphoreType.DMA((width // BLOCK,)),
             pltpu.VMEM((8, width), F32),
+            pltpu.VMEM(apart, F32),
             pltpu.VMEM((blocks, 8, 128), F32),
             pltpu.VMEM((groups, span, 8, 128), F32),
-            pltpu.VMEM((groups, *over_dp.shape), F32),
+            pltpu.VMEM((groups, *apart), F32),
             pltpu.VMEM((span, 8, 128), F32),
             pltpu.VMEM((count, span, 8, 128), F32),
             pltpu.SemaphoreType.DMA((4, groups)),
@@ -912,7 +1027,99 @@
         ],
         compiler_params=params(5),
         cost_estimate=cost(115),
-    )(triple_grad, weights, own, residual_grad, known, over_dp, vectors)
+    )(triple_grad, weights, own, residual_grad, *sums, valid, column_sums, unit_grad, vectors)
+
+
+def close_kernel(reduce_hbm, expand_hbm, first_hbm, output_hbm, hidden_hbm, *rest):
+    reduce_out, expand_out, triple_out, merge_out, output_out, hidden_out = rest[:6]
+    reduce, expand, first, output, hidden, reduce_wide, expand_wide, triple, merge, into, out = rest[6:]
+    chunk = 256
+    rows = output.shape[0]
+
+    def copy(src, dst, sem):
+        return pltpu.make_async_copy(src, dst, sem)
+
+    ins = [
+        copy(reduce_hbm, reduce, into.at[0]),
+        copy(expand_hbm, expand, into.at[1]),
+        copy(first_hbm, first, into.at[2]),
+    ]
+    outs = [
+        copy(reduce_wide, reduce_out, out.at[0]),
+        copy(expand_wide, expand_out, out.at[1]),
+        copy(triple, triple_out, out.at[2]),
+        copy(merge, merge_out, out.at[3]),
+    ]
+    large = []
+    for k, (src, held, dst) in enumerate(((output_hbm, output, output_out), (hidden_hbm, hidden, hidden_out))):
+        for start in range(0, rows, chunk):
+            part = pl.ds(start, chunk)
+            sem = 4 + k * (rows // chunk) + start // chunk
+            large.append(
+                (copy(src.at[part], held.at[part], into.at[sem]), copy(held.at[part], dst.at[part], out.at[sem]))
+            )
+    for one in ins:
+        one.start()
+    for one, _ in large:
+        one.start()
+
+    def widen(src, dst):
+        step = 64
+
+        @pl.loop(0, src.shape[0] // step)
+        def _(k):
+            part = block(k, step)
+            dst[part, :] = src[part, :].astype(F32)
+
+    ins[0].wait()
+    widen(reduce, reduce_wide)
+    outs[0].start()
+    ins[1].wait()
+    widen(expand, expand_wide)
+    outs[1].start()
+    ins[2].wait()
+    wide = triple.shape[2]
+    for k in range(3):
+        triple[k] = first[:, k * wide : (k + 1) * wide].astype(F32)
+    outs[2].start()
+    merge[...] = first[:, 3 * wide :].astype(F32).T
+    outs[3].start()
+    for one, two in large:
+        one.wait()
+        two.start()
+    for one in outs:
+        one.wait()
+    for _, two in large:
+        two.wait()
+
+
+def close_call(reduce_grad, expand_grad, first_grad, output, hidden_grad):
+    block_rows, columns = first_grad.shape
+    wide = columns // 4
+    shapes = [
+        (reduce_grad.shape, F32),
+        (expand_grad.shape, F32),
+        ((3, block_rows, wide), F32),
+        ((wide, block_rows), F32),
+        (output.shape, BF16),
+        (hidden_grad.shape, BF16),
+    ]
+    ins = (reduce_grad, expand_grad, first_grad, output, hidden_grad)
+    sems = 4 + 2 * (output.shape[0] // 256)
+    return pl.pallas_call(
+        close_kernel,
+        name="close",
+        out_shape=tuple(jax.ShapeDtypeStruct(*shape) for shape in shapes),
+        in_specs=[ANY] * 5,
+        out_specs=(ANY,) * 6,
+        scratch_shapes=[
+            *[pltpu.VMEM(array.shape, BF16) for array in ins],
+            *[pltpu.VMEM(shape, F32) for shape, _ in shapes[:4]],
+            pltpu.SemaphoreType.DMA((sems,)),
+            pltpu.SemaphoreType.DMA((sems,)),
+        ],
+        compiler_params=pltpu.CompilerParams(vmem_limit_bytes=63 << 20),
+    )(*ins)
 
 
 def make_local(groups, count):
@@ -985,7 +1192,6 @@
         norm_mid, residual, sums_one, qkv, mixed, totals = front_call(
             count, slopes, norm_in, first_full, shift, own, own_valid, segments, vectors
         )
-        totals = totals[:, :, :2].transpose(0, 2, 1).reshape(local_heads, rows)
         branch_grad, residual_grad, sums_two, unit_grad, feed_part, expand_grad, reduce_grad = (
             feed_call(
                 count,
@@ -1001,8 +1207,7 @@
         )
 
         def scatter(array, dim):
-            own_block = lax.psum_scatter(array, "dp", scatter_dimension=dim, tiled=True)
-            return own_block.astype(F32)
+            return lax.psum_scatter(array, "dp", scatter_dimension=dim, tiled=True)
 
         reduce_grad = scatter(reduce_grad, 1)
         expand_grad = scatter(expand_grad, 0)
@@ -1022,25 +1227,21 @@
             vectors,
         )
         first_grad = scatter(first_grad, 0)
-        triple_grad = first_grad[:, : 3 * head_cols]
-        merge_grad = first_grad[:, 3 * head_cols :].T
-        squares = jnp.stack(
-            [
-                jnp.sum(sums_three[0]),
-                jnp.sum(sums_one[0]),
-                jnp.sum(sums_three[1]),
-                jnp.sum(own_valid),
-            ]
-        )
-        lanes = jnp.tile(jnp.pad(squares, (0, 124)), width // 128)
-        known = jnp.concatenate(
-            [jnp.zeros((2, width), F32), sums_two[:4], lanes[None], jnp.zeros((1, width), F32)]
-        )
-        over_dp = jnp.concatenate([column_sums[0], unit_grad[0]]).reshape(-1, 128)
-        tail = (-over_dp.shape[0]) % 8
-        over_dp = jnp.pad(over_dp, ((0, tail), (0, 0)))
         hidden_grad, small, dp_small = last_call(
-            groups, count, grad_triple, first_full, own, residual_grad, known, over_dp, vectors
+            groups,
+            count,
+            grad_triple,
+            first_full,
+            own,
+            residual_grad,
+            (sums_one, sums_two, sums_three),
+            own_valid,
+            column_sums,
+            unit_grad,
+            vectors,
+        )
+        reduce_grad, expand_grad, triple_grad, merge_grad, output, hidden_grad = close_call(
+            reduce_grad, expand_grad, first_grad, output, hidden_grad
         )
         share = width // groups
         small = small.transpose(1, 0, 2).reshape(8, -1)
@@ -1058,7 +1259,7 @@
             hidden_grad,
             small[0],
             small[1],
-            triple_grad.reshape(-1, 3, head_cols),
+            triple_grad.transpose(1, 0, 2),
             pair_grad,
             merge_grad,
             small[2],

time: 698 us -> 594 us (0.85)
  waiting for transfers between devices: 95.4 us -> 25.5 us
  local copies, waits for them, and re-layouts: 33 us -> 15 us
  other arithmetic: 29.3 us -> 16.6 us
    reduce_scatter x3, waiting for transfers between devices: 70.5 us -> 0.01 us  [scatter(): return lax.psum_scatter(array, 'dp', scatter_dimension=dim, tiled=True)]
    pallas_call x0 -> x1, Pallas kernels: none -> 9.78 us  [close_call(): pl.pallas_call(close_kernel, name='close', out_shape=tuple((jax.ShapeDtyp...]
    unnamed x42 -> x28, local copies, waits for them, and re-layouts: 16 us -> 6.18 us
  transfers between devices with their start and end apart: 6 -> 6, of which waited for: 2 -> 1; matrix products, arithmetic and copies ran while one was open for 7% -> 4% of each run, Pallas kernels for 36% -> 61%
where the time goes in v3:
time: 594 us; the launch traced here: 589 us
  Pallas kernels  506 us (85%)
  waiting for transfers between devices  25.5 us (4%)
  other arithmetic  16.6 us (3%)
  between operations  15.3 us (3%)
  local copies, waits for them, and re-layouts  15 us (3%)
  blocking collectives  10.8 us (2%)
    pallas_call x1, Pallas kernels, feed_call(): pl.pallas_call(functools.partial(feed_kernel, count, pieces), name='feed_...  135 us
    pallas_call x1, Pallas kernels, front_call(): pl.pallas_call(functools.partial(front_kernel, count, head_cols), name='f...  121 us
    pallas_call x1, Pallas kernels, last_call(): pl.pallas_call(functools.partial(last_kernel, groups, count), name='last_...  120 us
    pallas_call x1, Pallas kernels, back_call(): pl.pallas_call(functools.partial(back_kernel, count, head_cols), name='ba...  120 us
    all_gather x1, waiting for transfers between devices, local(): first_full = lax.all_gather(first, 'dp', axis=0, tiled=True)  23.5 us
  transfers between devices with their start and end apart: 6, of which 1 were waited for; matrix products, arithmetic and copies ran while one was open for 4% of the time, Pallas kernels for 61%

profile of v3, /device:TPU:0, one launch (start us, length us, event | category | flops | bytes accessed | tf_op | source)
XLA Modules:
  0.0 589.1 jit_solution(16048873546263337974)
XLA Ops:
  7.2 0.0 all-gather.4.cloned.1.call-start
  7.2 1.1 copy.35
  8.3 1.4 copy.34
  9.7 0.3 copy.36
  10.0 1.1 pad_maximum_fusion
  11.2 0.0 all-gather.6.cloned.1.call-start
  11.3 0.7 all-gather.6.cloned.1.call-update
  12.0 0.0 all-gather.8.cloned.1.call-start
  12.0 0.7 all-gather.8.cloned.1.call-update
  12.7 0.0 reduce-scatter.4.cloned.1.call-start
  12.8 0.6 fusion.13.place_row
  13.4 0.1 iota_compare_fusion
  13.4 0.1 lt.97
  13.5 0.1 lt.98
  13.6 2.8 convert_reduce_fusion
  16.5 0.1 fusion.12
  16.5 0.5 multiply_power_fusion.slopes
  17.2 0.6 broadcast_in_dim.41.shift
  17.8 0.6 broadcast_in_dim.48
  18.4 10.8 %all_gather.12 = bf16[6,2048]{1,0:T(8,128)(2,1)S(1)} all-gather(bf16[6,256]{1,0:T(8,128)(2,1)S(1)} %stack.36), channel_id=1, replica_groups=mesh['dp'=8,'mp'=4] {'dp'}, dimensions={1}, use_global_device_ids=true | all-gather | bytes 27648 | tf_op jit(solution)/shard_map/all_gather | solution.py:1162
  29.2 0.6 pad.4.vectors
  29.9 0.8 reshape.296.valid
  30.6 0.3 copy.47
  31.0 3.6 fusion.2
  34.5 0.6 broadcast_select_fusion.1
  35.1 1.3 fusion.9
  36.5 0.4 broadcast_select_fusion.grad_hbm
  36.8 2.1 copy-done.1
  39.0 1.2 copy-done
  40.2 1.6 constant_dynamic-slice_fusion
  41.7 3.2 fusion.5.norm_hbm
  44.9 23.5 %all-gather.4.cloned.1.call-done.weights_hbm.merge.triple_hbm = bf16[2048,2048]{1,0:T(8,128)(2,1)} async-done(((bf16[256,2048]{1,0:T(8,128)(2,1)}), bf16[2048,2048]{1,0:T(8,128)(2,1)}) %all-gather.4.cloned.1.call-update) | async-done | bytes 8388624 | tf_op jit(solution)/shard_map/all_gather | solution.py:1156
  68.4 120.5 %front_line.1 = (bf16[1024,2048]{1,0:T(8,128)(2,1)}, f32[256,2048]{1,0:T(8,128)}, f32[8,2048]{1,0:T(8,128)}, bf16[1024,1536]{1,0:T(8,128)(2,1)}, bf16[1024,512]{1,0:T(8,128)(2,1)}, /*index=5*/f32[8,1024]{1,0:T(8,128)}) custom-call(f32[8]{0:T(128)} %multiply_power_fusion.slopes, bf16[1024,2048]{1,0:T(8,128)(2,1)} %fusion.5.norm_hbm, ...), custom_call_target="tpu_custom_call" | custom-call | flops 120000004096 | bytes 1048576 | tf_op jit(solution)/shard_map/front_line/pallas_call | solution.py:438
  189.0 0.0 all-gather.6.cloned.1.call-done.expand_hbm
  189.0 0.0 all-gather.8.cloned.1.call-done.reduce_hbm
  189.0 135.5 %feed_line.1 = (bf16[1024,2048]{1,0:T(8,128)(2,1)}, f32[256,2048]{1,0:T(8,128)}, f32[8,2048]{1,0:T(8,128)}, f32[1,2048]{1,0:T(1,128)}, bf16[1024,2048]{1,0:T(8,1...) custom-call(bf16[1024,2048]{1,0:T(8,128)(2,1)} %get-tuple-element.42.middle_hbm, ...), custom_call_target="tpu_custom_call" | custom-call | flops 130000003072 | bytes 1048576 | tf_op jit(solution)/shard_map/feed_line/pallas_call | solution.py:629
  324.5 0.0 reduce-scatter.6.cloned.1.call-start
  324.6 0.5 reduce-scatter.6.cloned.1.call-update
  325.1 0.0 reduce-scatter.8.cloned.1.call-start
  325.2 119.6 %back_line.1 = (bf16[1024,1536]{1,0:T(8,128)(2,1)}, f32[1,1536]{1,0:T(1,128)}, bf16[1024,2048]{1,0:T(8,128)(2,1)}, f32[8,2048]{1,0:T(8,128)}, bf16[2048,2048]{1,0:T(8,128)(2,1)}) custom-call(f32[8]{0:T(128)} %multiply_power_fusion.slopes, bf16[1024,2048]{1,0:T(8,128)(2,1)} %get-tuple-element.46.branch_hbm, ...), custom_call_target="tpu_custom_call" | custom-call | flops 120000004096 | bytes 1048576 | tf_op jit(solution)/shard_map/back_line/pallas_call | solution.py:802
  444.8 120.2 %last_line.1 = (bf16[1024,2048]{1,0:T(8,128)(2,1)}, f32[2,8,128]{2,1,0:T(8,128)}, f32[32,128]{1,0:T(8,128)}) custom-call(bf16[1024,1536]{1,0:T(8,128)(2,1)} %get-tuple-element.53.triple_grad, bf16[2048,2048]{1,0:T(8,128)(2,1)} %all-gather.4.cloned.1.call-done.weights_hbm.merge.triple_hbm, bf16[256,2048]{1,0:T(8,128)(2,1)} %bitcast.52, ...), custom_call_target="tpu_custom_call" | custom-call | flops 115000000512 | bytes 1048576 | tf_op jit(solution)/shard_map/last_line/pallas_call | solution.py:1002
  565.0 1.3 slice.94
  566.9 0.7 fusion.18
  567.6 0.6 pad_maximum_fusion.2
  568.2 1.2 fusion.15
  569.4 1.5 fusion.19
  570.9 1.3 slice_bitcast_fusion
  572.2 9.8 %close.1 = (f32[2048,256]{1,0:T(8,128)}, f32[256,2048]{1,0:T(8,128)}, f32[3,256,512]{2,1,0:T(8,128)}, f32[512,256]{1,0:T(8,128)}, bf16[1024,2048]{1,0:T(8,128)(2,1)}, /*index=5*/bf16[1024,2048]{1,0:T(8,128)(2,1)}) custom-call(bf16[2048,256]{1,0:T(8,128)(2,1)} %reduce-scatter.4.cloned.1.call-done.reduce_hbm, ...), custom_call_target="tpu_custom_call" | custom-call | tf_op jit(solution)/shard_map/close/pallas_call | solution.py:1109
  (45 shorter events, 0.2 us)
Async XLA Ops:
  7.2 61.2 %all-gather.4.cloned.1.call-start = ((), (), s32[]{:S(2)}) async-start(), calls=%async_computation.3 | async-start | bytes 9437184 | tf_op jit(solution)/shard_map/all_gather | solution.py:1156
  8.3 5.0 copy-start.5
  11.1 5.3 copy-start.3
  11.1 5.9 %copy-start.6 = (bf16[256]{0:T(256)(128)(2,1)S(1)}, bf16[256]{0:T(256)(128)(2,1)}, u32[]{:S(2)}) copy-start(bf16[256]{0:T(256)(128)(2,1)} %param.18) | copy-start | bytes 1540
  11.1 5.9 %copy-start.7 = (bf16[256]{0:T(256)(128)(2,1)S(1)}, bf16[256]{0:T(256)(128)(2,1)}, u32[]{:S(2)}) copy-start(bf16[256]{0:T(256)(128)(2,1)} %param.19) | copy-start | bytes 1540
  11.1 5.9 %copy-start.8 = (bf16[256]{0:T(256)(128)(2,1)S(1)}, bf16[256]{0:T(256)(128)(2,1)}, u32[]{:S(2)}) copy-start(bf16[256]{0:T(256)(128)(2,1)} %param.23) | copy-start | bytes 1540
  11.1 6.0 %copy-start.9 = (bf16[256]{0:T(256)(128)(2,1)S(1)}, bf16[256]{0:T(256)(128)(2,1)}, u32[]{:S(2)}) copy-start(bf16[256]{0:T(256)(128)(2,1)} %param.24) | copy-start | bytes 1540
  11.2 6.0 %copy-start.10 = (bf16[256]{0:T(256)(128)(2,1)S(1)}, bf16[256]{0:T(256)(128)(2,1)}, u32[]{:S(2)}) copy-start(bf16[256]{0:T(256)(128)(2,1)} %param.25) | copy-start | bytes 1540
  11.2 6.0 %copy-start.11 = (bf16[256]{0:T(256)(128)(2,1)S(1)}, bf16[256]{0:T(256)(128)(2,1)}, u32[]{:S(2)}) copy-start(bf16[256]{0:T(256)(128)(2,1)} %param.29) | copy-start | bytes 1540
  11.2 6.6 %copy-start.4 = (bf16[2048]{0:T(1024)(128)(2,1)S(1)}, bf16[2048]{0:T(1024)(128)(2,1)}, u32[]{:S(2)}) copy-start(bf16[2048]{0:T(1024)(128)(2,1)} %param.27) | copy-start | bytes 12292
  11.2 177.8 %all-gather.6.cloned.1.call-start = ((), (), s32[]{:S(2)}) async-start(), calls=%async_computation.4 | async-start | bytes 9437184 | tf_op jit(solution)/shard_map/all_gather | solution.py:1157
  12.0 177.0 %all-gather.8.cloned.1.call-start = ((), (), s32[]{:S(2)}) async-start(), calls=%async_computation.5 | async-start | bytes 9437184 | tf_op jit(solution)/shard_map/all_gather | solution.py:1158
  12.7 559.5 %reduce-scatter.4.cloned.1.call-start = ((), (), s32[]{:S(2)}) async-start(), calls=%async_computation.6 | async-start | bytes 9437184 | tf_op jit(solution)/shard_map/reduce_scatter | solution.py:1210
  30.9 5.5 copy-start.2
  36.5 3.7 copy-start
  36.8 2.1 copy-start.1
  324.5 247.7 %reduce-scatter.6.cloned.1.call-start = ((), (), s32[]{:S(2)}) async-start(), calls=%async_computation.7 | async-start | bytes 9437184 | tf_op jit(solution)/shard_map/reduce_scatter | solution.py:1210
  325.1 247.1 %reduce-scatter.8.cloned.1.call-start = ((), (), s32[]{:S(2)}) async-start(), calls=%async_computation.8 | async-start | bytes 9437184 | tf_op jit(solution)/shard_map/reduce_scatter | solution.py:1210
Sparse Core Ops, SparseCore 0:
  11.3 57.0 all-gather.3
  70.3 54.2 all-gather.5
  126.5 55.8 all-gather.7
  324.7 69.9 reduce-scatter.3
  398.0 71.4 reduce-scatter.5
  472.8 71.5 reduce-scatter.7

commit v4 on v3

--- a/solution.py
+++ b/solution.py
@@ -4,6 +4,7 @@
 import jax.numpy as jnp
 from jax import lax
 from jax.experimental import pallas as pl
+from jax.experimental.layout import Layout, with_layout_constraint
 from jax.experimental.pallas import tpu as pltpu
 from jax.sharding import PartitionSpec as P
 
@@ -267,9 +268,9 @@
     return pl.CostEstimate(flops=int(micros * 1e9), bytes_accessed=1 << 20, transcendentals=0)
 
 
-def params(index):
+def params(index, variant):
     return pltpu.CompilerParams(
-        collective_id=index, has_side_effects=True, vmem_limit_bytes=63 << 20
+        collective_id=8 * variant + index, has_side_effects=True, vmem_limit_bytes=63 << 20
     )
 
 
@@ -317,7 +318,7 @@
     norm_in, weights, qkv, mixed, load_sem, save_sem, part, acc, mask, *rest,
 ):
     line = Line(count, part, middle, *rest)
-    rows_all, width = middle.shape
+    rows_all, width = norm_in.shape
     tiles = tiles_of(rows_all)
     blocks = weights.shape[1] // BLOCK
 
@@ -431,8 +432,8 @@
 SMEM = pl.BlockSpec(memory_space=pltpu.SMEM)
 
 
-def front_call(count, slopes, norm_in, weights, shift, own, valid, segments, vectors):
-    rows, width = norm_in.shape
+def front_call(count, rows, variant, slopes, norm_in, weights, shift, own, valid, segments, vectors):
+    width = norm_in.shape[1]
     head_cols = weights.shape[1] // 4
     pieces = rows // PIECE
     return pl.pallas_call(
@@ -460,7 +461,7 @@
             pltpu.VMEM((TILE, rows), F32),
             *Line.scratch(count, pieces, width),
         ],
-        compiler_params=params(1),
+        compiler_params=params(1, variant),
         cost_estimate=cost(120),
     )(slopes, norm_in, weights, shift, own, valid, *segments[:3], vectors)
 
@@ -482,20 +483,21 @@
             pltpu.make_async_copy(reduce_hbm.at[cols], reduce.at[cols], load_sem.at[1, k]),
         )
 
+    tiles = tiles_of(middle.shape[0])
+
     def load_rows(k):
-        rows = block(k, TILE)
+        rows = pl.ds(tiles[k][0], tiles[k][1])
         return (
             pltpu.make_async_copy(middle_hbm.at[rows], middle.at[rows], load_sem.at[2, k]),
             pltpu.make_async_copy(grad_hbm.at[rows], grad.at[rows], load_sem.at[3, k]),
         )
 
-    tiles = middle.shape[0] // TILE
     for copy in (*load_rows(0), *load(0)):
         copy.start()
     for k in range(1, blocks):
         for copy in load(k):
             copy.start()
-    for k in range(1, tiles):
+    for k in range(1, len(tiles)):
         for copy in load_rows(k):
             copy.start()
     greet(count)
@@ -515,117 +517,105 @@
         for k, values in enumerate((low.astype(F32), grad_mid * normed, grad_mid, grad_out)):
             sums[k : k + 1, :] += jnp.sum(values, axis=0, keepdims=True)
 
-    def load_tile(tile):
-        for copy in load_rows(tile):
-            copy.wait()
-
-    def forward_tile(tile, k):
-        rows, cols = block(tile, TILE), block(k, BLOCK)
-
-        @pl.when(tile == 0)
-        def _():
-            for copy in load(k):
+    def forward(start, size, low_k, high_k):
+        rows = pl.ds(start, size)
+        if low_k == 0:
+            for copy in load_rows(start // TILE):
                 copy.wait()
 
-        pre = dot32(middle[rows, :], expand[:, cols]) + unit_shift[:, cols]
-        half = 0.5 + 0.5 * lax.erf(pre * 0.7071067811865476)
-        slope = half + pre * (0.3989422804014327 * jnp.exp(-0.5 * pre * pre))
-        active[rows, cols] = (pre * half).astype(BF16)
-        low = (dot_nt(grad[rows, :], reduce[cols, :]) * slope).astype(BF16)
-        pre_grad[rows, cols] = low
-        unit_grad[:, cols] += jnp.sum(low.astype(F32), axis=0, keepdims=True)
-
-    def back_tile(tile, k):
-        rows, cols = block(tile, TILE), block(k, BLOCK)
-        part[rows, cols] = dot_nt(pre_grad[rows, :], expand[cols, :]).astype(BF16)
-
-    def put(slot, target):
-        return pltpu.make_async_copy(stage.at[slot], target, stage_sem.at[slot])
-
-    rows_all = middle.shape[0] // BLOCK
-    per_feed = rows_all * (width // BLOCK)
-    per_grad = (units // BLOCK) * (width // BLOCK)
-    jobs = per_feed + 2 * per_grad
-
-    def job(index):
-        slot = lax.rem(index, 2)
-        across = width // BLOCK
-
-        @pl.when(index >= 2)
-        def _():
-            put(slot, expand_grad.at[pl.ds(0, BLOCK), pl.ds(0, BLOCK)]).wait()
-
-        @pl.when(index < per_grad)
-        def _():
-            r, c = block(index // across, BLOCK), block(lax.rem(index, across), BLOCK)
-            stage[slot] = dot_tn(active[:, r], grad[:, c]).astype(BF16)
-            put(slot, reduce_grad.at[r, c]).start()
-
-        @pl.when(jnp.logical_and(index >= per_grad, index < 2 * per_grad))
-        def _():
-            local = index - per_grad
-            r, c = block(local // across, BLOCK), block(lax.rem(local, across), BLOCK)
-            stage[slot] = dot_tn(middle[:, r], pre_grad[:, c]).astype(BF16)
-            put(slot, expand_grad.at[r, c]).start()
-
-        @pl.when(index >= 2 * per_grad)
-        def _():
-            local = index - 2 * per_grad
-            r, c = block(local // across, BLOCK), block(lax.rem(local, across), BLOCK)
-            stage[slot] = dot32(active[r, :], reduce[:, c]).astype(BF16)
-            put(slot, feed_hbm.at[r, c]).start()
-
-    ratio = TILE // PIECE
+        @pl.loop(low_k, high_k)
+        def _(k):
+            cols = block(k, BLOCK)
+            if start == 0:
+                for copy in load(k):
+                    copy.wait()
+            pre = dot32(middle[rows, :], expand[:, cols]) + unit_shift[:, cols]
+            half = 0.5 + 0.5 * lax.erf(pre * 0.7071067811865476)
+            slope = half + pre * (0.3989422804014327 * jnp.exp(-0.5 * pre * pre))
+            active[rows, cols] = (pre * half).astype(BF16)
+            low = (dot_nt(grad[rows, :], reduce[cols, :]) * slope).astype(BF16)
+            pre_grad[rows, cols] = low
+            unit_grad[:, cols] += jnp.sum(low.astype(F32), axis=0, keepdims=True)
+
+    def backward(start, size, low_k, high_k):
+        rows = pl.ds(start, size)
+
+        @pl.loop(low_k, high_k)
+        def _(k):
+            cols = block(k, BLOCK)
+            part[rows, cols] = dot_nt(pre_grad[rows, :], expand[cols, :]).astype(BF16)
+
+    staged = {"rows": 0}
+
+    def settle_slot(slot):
+        rows = pl.ds(0, staged["rows"])
+        pltpu.make_async_copy(
+            stage.at[slot, rows], feed_hbm.at[rows, pl.ds(0, BLOCK)], stage_sem.at[slot]
+        ).wait()
+
+    def emit(target, start, size, product):
+        before = staged["rows"]
+
+        @pl.loop(0, target.shape[1] // BLOCK)
+        def _(k):
+            slot = lax.rem(k, 4)
+            if before:
+                settle_slot(slot)
+            stage[slot, :size, :] = product(block(k, BLOCK)).astype(BF16)
+            pltpu.make_async_copy(
+                stage.at[slot, pl.ds(0, size)],
+                target.at[pl.ds(start, size), block(k, BLOCK)],
+                stage_sem.at[slot],
+            ).start()
+
+        staged["rows"] = size
+
+    def feed_product(start, size):
+        emit(feed_hbm, start, size, lambda cols: dot32(active[pl.ds(start, size), :], reduce[:, cols]))
+
+    def reduce_product(start):
+        emit(reduce_grad, start, BLOCK, lambda cols: dot_tn(active[:, pl.ds(start, BLOCK)], grad[:, cols]))
+
+    def expand_product(start):
+        emit(expand_grad, start, BLOCK, lambda cols: dot_tn(middle[:, pl.ds(start, BLOCK)], pre_grad[:, cols]))
+
     backs = width // BLOCK
-    load_tile(0)
-    pl.loop(0, blocks)(functools.partial(forward_tile, 0))
-    pl.loop(0, backs)(functools.partial(back_tile, 0))
+    assert backs == 4 and blocks == 4
+
+    def work(start, size):
+        return [
+            functools.partial(forward, start, size, 0, blocks // 2),
+            functools.partial(forward, start, size, blocks // 2, blocks),
+            functools.partial(backward, start, size, 0, backs // 2),
+            functools.partial(backward, start, size, backs // 2, backs),
+        ]
+
+    for closure in work(*tiles[0]):
+        closure()
+    later = [
+        [*work(*after), functools.partial(feed_product, *tile)] for tile, after in zip(tiles, tiles[1:])
+    ]
+    products = [functools.partial(reduce_product, r) for r in range(0, units, BLOCK)]
+    products += [functools.partial(expand_product, r) for r in range(0, width, BLOCK)]
     steps = ticks(count, pieces)
-    late = (tiles - 1) * ratio
-    per_step = -(-jobs // (steps - late))
-
-    @pl.loop(0, steps)
-    def _(step):
-        tick(line, step, finish)
-        tile, phase = step // ratio + 1, lax.rem(step, ratio)
-
-        @pl.when(tile < tiles)
-        def _():
-            @pl.when(phase == 0)
-            def _():
-                load_tile(tile)
-
-            @pl.loop(phase * (blocks + backs) // ratio, (phase + 1) * (blocks + backs) // ratio)
-            def _(k):
-                @pl.when(k < blocks)
-                def _():
-                    forward_tile(tile, k)
-
-                @pl.when(k >= blocks)
-                def _():
-                    back_tile(tile, k - blocks)
-
-        @pl.when(tile >= tiles)
-        def _():
-            first = (step - late) * per_step
-
-            @pl.loop(first, jnp.minimum(first + per_step, jobs))
-            def _(index):
-                job(index)
-
-    for slot in range(2):
-        put(slot, expand_grad.at[pl.ds(0, BLOCK), pl.ds(0, BLOCK)]).wait()
+    beside = tiles[-1][1] // PIECE
+    taken = len(products) * beside // (steps - pieces + beside)
+    later.append([functools.partial(feed_product, *tiles[-1]), *products[:taken]])
+    drain = spread(products[taken:], steps - pieces)
+    paced(lambda step: tick(line, step, finish), tiles, steps, later, drain)
+    for slot in range(4):
+        settle_slot(slot)
 
     @pl.loop(0, pieces)
     def _(piece):
         line.settle(piece)
 
 
-def feed_call(count, middle, expand, reduce, grad, residual, own_grad, unit_shift, vectors):
+def feed_call(count, variant, middle, expand, reduce, grad, residual, own_grad, unit_shift, vectors):
     rows, width = middle.shape
     units = expand.shape[1]
     pieces = rows // PIECE
-    most = max(units // BLOCK, rows // TILE)
+    most = max(units // BLOCK, len(tiles_of(rows)))
     return pl.pallas_call(
         functools.partial(feed_kernel, count, pieces),
         name="feed_line",
@@ -649,12 +639,12 @@
             pltpu.VMEM((rows, units), BF16),
             pltpu.VMEM((rows, width), BF16),
             pltpu.VMEM((PIECE // count, width), F32),
-            pltpu.VMEM((2, BLOCK, BLOCK), BF16),
+            pltpu.VMEM((4, BLOCK, BLOCK), BF16),
             pltpu.SemaphoreType.DMA((4, most)),
-            pltpu.SemaphoreType.DMA((2,)),
+            pltpu.SemaphoreType.DMA((4,)),
             *Line.scratch(count, pieces, width),
         ],
-        compiler_params=params(2),
+        compiler_params=params(2, variant),
         cost_estimate=cost(130),
     )(middle, expand, reduce, grad, residual, own_grad, unit_shift, vectors)
 
@@ -667,7 +657,7 @@
     mixed_grad, key_grad, value_grad, acc, mask, stage, stage_sem, *rest,
 ):
     line = Line(count, feed, output, *rest)
-    rows_all, width = output.shape
+    rows_all, width = branch_grad.shape
     tiles = tiles_of(rows_all)
 
     def load_feed(k):
@@ -679,7 +669,7 @@
         return pltpu.make_async_copy(branch_hbm.at[rows], branch_grad.at[rows], load_sem.at[1, k])
 
     load_residual = pltpu.make_async_copy(residual_hbm, residual, load_sem.at[2, 0])
-    load_norm = pltpu.make_async_copy(norm_hbm, norm_in, load_sem.at[2, 1])
+    load_norm = pltpu.make_async_copy(norm_hbm.at[pl.ds(0, rows_all)], norm_in, load_sem.at[2, 1])
     load_feed(0).start()
     load_grad(len(tiles) - 1).start()
     load_residual.start()
@@ -794,7 +784,7 @@
         line.settle(piece)
 
 
-def back_call(count, slopes, branch_grad, weights, qkv, mixed, norm_in, totals, segments, feed, residual, valid, vectors):
+def back_call(count, whole, variant, slopes, branch_grad, weights, qkv, mixed, norm_in, totals, segments, feed, residual, valid, vectors):
     rows, width = branch_grad.shape
     head_cols = weights.shape[1] // 4
     merge_spec = pl.BlockSpec((width, head_cols), lambda i: (0, 3), memory_space=pltpu.VMEM)
@@ -805,7 +795,7 @@
         out_shape=(
             jax.ShapeDtypeStruct((rows, 3 * head_cols), BF16),
             jax.ShapeDtypeStruct((1, 3 * head_cols), F32),
-            jax.ShapeDtypeStruct((rows, width), BF16),
+            jax.ShapeDtypeStruct((whole, width), BF16),
             jax.ShapeDtypeStruct((8, width), F32),
             jax.ShapeDtypeStruct((width, 4 * head_cols), BF16),
         ),
@@ -828,7 +818,7 @@
             pltpu.SemaphoreType.DMA((2,)),
             *Line.scratch(count, pieces, width),
         ],
-        compiler_params=params(3),
+        compiler_params=params(3, variant),
         cost_estimate=cost(120),
     )(slopes, branch_grad, weights, qkv, mixed, norm_in, totals, *segments[3:], feed, residual, valid, vectors)
 
@@ -852,8 +842,9 @@
 
 def last_kernel(
     groups, count, triple_grad, triple_hbm, own, residual_grad, front_sums, feed_sums, back_sums, valid,
-    column_sums, unit_grad, vectors,
-    hidden_grad, all_out, dp_out,
+    column_sums, unit_grad, vectors, first_hbm,
+    hidden_grad, all_out, dp_out, first_out,
+    mine, theirs, others, pair_sems, chip_sems,
     triple, load_sem, sums, over_dp, cut, all_in, dp_in, own_sum, mp_in, sems, mp_sems, part, acc, *rest,
 ):
     line = Line(count, part, hidden_grad, *rest)
@@ -862,6 +853,11 @@
     blocks = cut.shape[0]
     columns = triple.shape[1]
 
+    def copy_to(src, dst, out, into, to):
+        return pltpu.make_async_remote_copy(
+            src_ref=src, dst_ref=dst, send_sem=out, recv_sem=into, device_id=to, device_id_type=MESH
+        )
+
     def load(k):
         rows = block(k, BLOCK)
         return pltpu.make_async_copy(
@@ -870,7 +866,64 @@
 
     for k in range(triple.shape[0] // BLOCK):
         load(k).start()
+
+    chips, depth = mine.shape[0], mine.shape[1]
+    parity, chip = lax.rem(group, 2), group // 2
+    partner = group + 1 - 2 * parity
+
+    def rows_of(owner):
+        return pl.ds(pl.multiple_of(owner * depth, depth), depth)
+
+    def mine_copy(q):
+        return pltpu.make_async_copy(first_hbm.at[rows_of(2 * q + parity)], mine.at[q], pair_sems.at[0, q])
+
+    def half_copy(q):
+        src = first_hbm.at[rows_of(2 * q + 1 - parity)]
+        return copy_to(src, theirs.at[q], pair_sems.at[1, q], pair_sems.at[2, q], (partner, me))
+
+    def chip_copy(away):
+        to = lax.rem(chip + away, chips)
+        return copy_to(
+            mine.at[to], others.at[away], chip_sems.at[0, away], chip_sems.at[1, away], (2 * to + parity, me)
+        )
+
+    def add_half(away):
+        q = lax.rem(chip + away, chips)
+        mine_copy(q).wait()
+        half_copy(q).wait_recv()
+
+        @pl.loop(0, depth // 64)
+        def _(k):
+            rows = block(k, 64)
+            mine[q, rows, :] = (mine[q, rows, :].astype(F32) + theirs[q, rows, :].astype(F32)).astype(BF16)
+
+    def send_chip(away):
+        add_half(away)
+        chip_copy(away).start()
+
+    def add_chips():
+        add_half(0)
+
+        @pl.loop(1, chips)
+        def _(away):
+            chip_copy(away).wait_recv()
+
+        @pl.loop(0, depth // 64)
+        def _(k):
+            rows = block(k, 64)
+            first_out[rows, :] = mine[chip, rows, :].astype(F32)
+
+            @pl.loop(1, chips)
+            def _(away):
+                first_out[rows, :] += others[away, rows, :].astype(F32)
+
     greet_all(groups, count)
+
+    @pl.loop(0, chips)
+    def _(q):
+        mine_copy(q).start()
+        half_copy(q).start()
+
     sums[0:2, :] = jnp.zeros_like(sums[0:2, :])
     sums[2:6, :] = feed_sums[0:4, :]
     sums[6:8, :] = jnp.zeros_like(sums[6:8, :])
@@ -887,11 +940,6 @@
     for k in range(unit_grad.shape[1] // 128):
         over_dp[wide + k : wide + k + 1, :] = unit_grad[:, 128 * k : 128 * (k + 1)]
 
-    def copy_to(src, dst, out, into, to):
-        return pltpu.make_async_remote_copy(
-            src_ref=src, dst_ref=dst, send_sem=out, recv_sem=into, device_id=to, device_id_type=MESH
-        )
-
     def dp_copy(away):
         to = lax.rem(group + away, groups)
         return copy_to(over_dp, dp_in.at[away], sems.at[0, away], sems.at[1, away], (to, me))
@@ -970,6 +1018,17 @@
     for closure in work(*tiles[0]):
         closure()
     later = [work(*tile) for tile in tiles[1:]] + [[]]
+    sends = [[] for _ in tiles]
+    if chips <= 8:
+        for away in range(1, chips):
+            sends[0].append(functools.partial(send_chip, away))
+    else:
+
+        def send_chips():
+            pl.loop(1, chips)(send_chip)
+
+        sends[0].append(send_chips)
+    later = [one + two for one, two in zip(later, sends)]
     steps = ticks(count, line.pieces)
     done = LAG * (count - 1) - 1
     drain = [[] for _ in range(steps - line.pieces)]
@@ -977,10 +1036,19 @@
     drain[done + 2 * LAG].append(add_blocks)
     paced(lambda step: tick(line, step, finish), tiles, steps, later, drain)
     add_rest()
+    add_chips()
 
     @pl.loop(0, line.pieces)
     def _(piece):
         line.settle(piece)
+
+    @pl.loop(0, chips)
+    def _(q):
+        half_copy(q).wait_send()
+
+    @pl.loop(1, chips)
+    def _(away):
+        chip_copy(away).wait_send()
 
     @pl.loop(1, groups)
     def _(away):
@@ -992,24 +1060,29 @@
         mp_copy(away).wait_send()
 
 
-def last_call(groups, count, triple_grad, weights, own, residual_grad, sums, valid, column_sums, unit_grad, vectors):
+def last_call(groups, count, whole, variant, triple_grad, weights, own, residual_grad, sums, valid, column_sums, unit_grad, vectors, first_grad):
     rows, columns = triple_grad.shape
     width = weights.shape[0]
     apart = (-(-(columns + unit_grad.shape[1]) // 1024) * 8, 128)
     pieces = rows // PIECE
     blocks = width // 128
     span = max(1, blocks // groups)
+    chips, depth = groups // 2, width // groups
     return pl.pallas_call(
         functools.partial(last_kernel, groups, count),
         name="last_line",
         out_shape=(
-            jax.ShapeDtypeStruct((rows, width), BF16),
+            jax.ShapeDtypeStruct((whole, width), BF16),
             jax.ShapeDtypeStruct((span, 8, 128), F32),
             jax.ShapeDtypeStruct(apart, F32),
+            jax.ShapeDtypeStruct((depth, first_grad.shape[1]), F32),
         ),
-        in_specs=[VMEM, ANY] + [VMEM] * 9,
-        out_specs=(ANY, VMEM, VMEM),
+        in_specs=[VMEM, ANY] + [VMEM] * 9 + [ANY],
+        out_specs=(ANY, VMEM, VMEM, VMEM),
         scratch_shapes=[
+            *[pltpu.VMEM((chips, depth, first_grad.shape[1]), BF16)] * 3,
+            pltpu.SemaphoreType.DMA((3, chips)),
+            pltpu.SemaphoreType.DMA((2, chips)),
             pltpu.VMEM((width, columns), BF16),
             pltpu.SemaphoreType.DMA((width // BLOCK,)),
             pltpu.VMEM((8, width), F32),
@@ -1025,16 +1098,14 @@
             pltpu.VMEM((PIECE // count, width), F32),
             *Line.scratch(count, pieces, width),
         ],
-        compiler_params=params(5),
+        compiler_params=params(5, variant),
         cost_estimate=cost(115),
-    )(triple_grad, weights, own, residual_grad, *sums, valid, column_sums, unit_grad, vectors)
-
-
-def close_kernel(reduce_hbm, expand_hbm, first_hbm, output_hbm, hidden_hbm, *rest):
-    reduce_out, expand_out, triple_out, merge_out, output_out, hidden_out = rest[:6]
-    reduce, expand, first, output, hidden, reduce_wide, expand_wide, triple, merge, into, out = rest[6:]
-    chunk = 256
-    rows = output.shape[0]
+    )(triple_grad, weights, own, residual_grad, *sums, valid, column_sums, unit_grad, vectors, first_grad)
+
+
+def close_kernel(reduce_hbm, expand_hbm, first_hbm, *rest):
+    reduce_out, expand_out, triple_out, merge_out = rest[:4]
+    reduce, expand, first, reduce_wide, expand_wide, triple, merge, into, out = rest[4:]
 
     def copy(src, dst, sem):
         return pltpu.make_async_copy(src, dst, sem)
@@ -1050,17 +1121,7 @@
         copy(triple, triple_out, out.at[2]),
         copy(merge, merge_out, out.at[3]),
     ]
-    large = []
-    for k, (src, held, dst) in enumerate(((output_hbm, output, output_out), (hidden_hbm, hidden, hidden_out))):
-        for start in range(0, rows, chunk):
-            part = pl.ds(start, chunk)
-            sem = 4 + k * (rows // chunk) + start // chunk
-            large.append(
-                (copy(src.at[part], held.at[part], into.at[sem]), copy(held.at[part], dst.at[part], out.at[sem]))
-            )
     for one in ins:
-        one.start()
-    for one, _ in large:
         one.start()
 
     def widen(src, dst):
@@ -1080,46 +1141,99 @@
     ins[2].wait()
     wide = triple.shape[2]
     for k in range(3):
-        triple[k] = first[:, k * wide : (k + 1) * wide].astype(F32)
+        triple[k] = first[:, k * wide : (k + 1) * wide]
     outs[2].start()
-    merge[...] = first[:, 3 * wide :].astype(F32).T
+    merge[...] = first[:, 3 * wide :].T
     outs[3].start()
-    for one, two in large:
-        one.wait()
-        two.start()
     for one in outs:
         one.wait()
-    for _, two in large:
-        two.wait()
-
-
-def close_call(reduce_grad, expand_grad, first_grad, output, hidden_grad):
+
+
+def close_call(reduce_grad, expand_grad, first_grad):
     block_rows, columns = first_grad.shape
     wide = columns // 4
-    shapes = [
-        (reduce_grad.shape, F32),
-        (expand_grad.shape, F32),
-        ((3, block_rows, wide), F32),
-        ((wide, block_rows), F32),
-        (output.shape, BF16),
-        (hidden_grad.shape, BF16),
-    ]
-    ins = (reduce_grad, expand_grad, first_grad, output, hidden_grad)
-    sems = 4 + 2 * (output.shape[0] // 256)
+    shapes = [reduce_grad.shape, expand_grad.shape, (3, block_rows, wide), (wide, block_rows)]
+    ins = (reduce_grad, expand_grad, first_grad)
     return pl.pallas_call(
         close_kernel,
         name="close",
-        out_shape=tuple(jax.ShapeDtypeStruct(*shape) for shape in shapes),
-        in_specs=[ANY] * 5,
-        out_specs=(ANY,) * 6,
+        out_shape=tuple(jax.ShapeDtypeStruct(shape, F32) for shape in shapes),
+        in_specs=[ANY] * 3,
+        out_specs=(ANY,) * 4,
         scratch_shapes=[
-            *[pltpu.VMEM(array.shape, BF16) for array in ins],
-            *[pltpu.VMEM(shape, F32) for shape, _ in shapes[:4]],
-            pltpu.SemaphoreType.DMA((sems,)),
-            pltpu.SemaphoreType.DMA((sems,)),
+            *[pltpu.VMEM(array.shape, array.dtype) for array in ins],
+            *[pltpu.VMEM(shape, F32) for shape in shapes],
+            pltpu.SemaphoreType.DMA((3,)),
+            pltpu.SemaphoreType.DMA((4,)),
         ],
         compiler_params=pltpu.CompilerParams(vmem_limit_bytes=63 << 20),
+        cost_estimate=cost(6),
     )(*ins)
+
+
+def unpack_kernel(facts, *rest):
+    sources, (held, into, out) = rest[:6], rest[6:]
+    packed, swapped, results = sources[0:2], sources[2:4], sources[4:6]
+    slots = results[0].shape[0] // SLOT
+
+    def fetch_own(array, slot):
+        source = packed[array].at[pl.ds(pl.multiple_of(facts[slot], 16), SLOT)]
+        return pltpu.make_async_copy(source, held.at[array, pl.ds(slot * SLOT, SLOT)], into.at[array, slot])
+
+    def fetch_other(array, slot):
+        target = held.at[array, pl.ds(slot * SLOT, SLOT)]
+        return pltpu.make_async_copy(swapped[array], target, into.at[array, slot])
+
+    def store(array, slot):
+        rows = pl.ds(slot * SLOT, SLOT)
+        return pltpu.make_async_copy(held.at[array, rows], results[array].at[rows], out.at[array, slot])
+
+    every = [(array, slot) for array in range(2) for slot in range(slots)]
+    for array, slot in every:
+        @pl.when(facts[slots + slot] == 0)
+        def _(array=array, slot=slot):
+            fetch_own(array, slot).start()
+
+        @pl.when(facts[slots + slot] != 0)
+        def _(array=array, slot=slot):
+            fetch_other(array, slot).start()
+
+    for array, slot in every:
+        fetch_other(array, slot).wait()
+        length = facts[2 * slots + slot]
+
+        @pl.loop(0, SLOT // 64)
+        def _(k):
+            rows = pl.ds(pl.multiple_of(slot * SLOT + k * 64, 64), 64)
+            place = lax.broadcasted_iota(jnp.int32, (64, held.shape[2]), 0) + k * 64
+            values = held[array, rows, :].astype(F32)
+            held[array, rows, :] = jnp.where(place < length, values, 0.0).astype(BF16)
+
+        store(array, slot).start()
+    for array, slot in every:
+        store(array, slot).wait()
+
+
+def unpack_call(facts, packed, swapped):
+    rows, width = packed[0].shape
+    slots = rows // SLOT
+    return pl.pallas_call(
+        unpack_kernel,
+        name="unpack",
+        out_shape=(jax.ShapeDtypeStruct((rows, width), BF16),) * 2,
+        in_specs=[SMEM] + [ANY] * 4,
+        out_specs=(ANY,) * 2,
+        scratch_shapes=[
+            pltpu.VMEM((2, rows, width), BF16),
+            pltpu.SemaphoreType.DMA((2, slots)),
+            pltpu.SemaphoreType.DMA((2, slots)),
+        ],
+        compiler_params=pltpu.CompilerParams(vmem_limit_bytes=63 << 20),
+        cost_estimate=cost(6),
+    )(facts, *packed, *swapped)
+
+
+SIZES = (768, 832, 896, 960)
 
 
 def make_local(groups, count):
@@ -1140,12 +1254,13 @@
         reduce_weight,
         reduce_bias,
     ):
-        slot = SLOT
         rows, width = hidden.shape
+        slots = rows // SLOT
         head_cols = triple_weight.shape[2]
         units = expand_weight.shape[1]
         local_heads = head_cols // HEAD_DIM
-        me = lax.axis_index("mp")
+        me, group = lax.axis_index("mp"), lax.axis_index("dp")
+        share = width // groups
         slopes = 2.0 ** (
             -8.0
             * (me * local_heads + jnp.arange(local_heads, dtype=jnp.int32) + 1).astype(F32)
@@ -1153,101 +1268,188 @@
         )
         bias_pair = triple_bias.astype(F32)
         first = jnp.concatenate([triple_weight.reshape(-1, 3 * head_cols), merge_weight.T], axis=1)
-        first_full = lax.all_gather(first, "dp", axis=0, tiled=True)
-        expand_full = lax.all_gather(expand_weight, "dp", axis=0, tiled=True)
-        reduce_full = lax.all_gather(reduce_weight, "dp", axis=1, tiled=True)
+        by_rows = Layout(major_to_minor=(0, 1))
+        first = with_layout_constraint(first, by_rows)
+        first_full = with_layout_constraint(lax.all_gather(first, "dp", axis=0, tiled=True), by_rows)
+        parts = jnp.stack([lengths // 16, lax.rem(lengths, 16)]).reshape(-1)
+        parts = jnp.pad(parts, (0, share - 2 * slots)).astype(BF16)
         vectors = jnp.stack(
-            [input_gain, input_shift, merge_bias, middle_gain, middle_shift, reduce_bias]
+            [input_gain, input_shift, merge_bias, middle_gain, middle_shift, reduce_bias, parts]
         )
         vectors = lax.all_gather(vectors, "dp", axis=1, tiled=True).astype(F32)
-        vectors = jnp.pad(vectors, ((0, 2), (0, 0)))
+        table = vectors[6].reshape(groups, share)[:, : 2 * slots].astype(jnp.int32)
+        table = 16 * table[:, :slots] + table[:, slots:]
+        vectors = jnp.pad(vectors, ((0, 1), (0, 0)))
+
+        whole = -(-table // 16) * 16
+        if slots == 2 and groups % 2 == 0:
+            left, right = whole[0::2], whole[1::2]
+            sums = jnp.stack(
+                [
+                    jnp.maximum(left[:, 0] + left[:, 1], right[:, 0] + right[:, 1]),
+                    jnp.maximum(left[:, 0] + right[:, 0], left[:, 1] + right[:, 1]),
+                    jnp.maximum(left[:, 0] + right[:, 1], left[:, 1] + right[:, 0]),
+                ]
+            )
+            needed = jnp.max(jnp.min(sums, axis=0))
+            choice = jnp.argmin(sums[:, group // 2]).astype(jnp.int32)
+            odd = lax.rem(group, 2)
+            given = jnp.where((odd == 1) & (choice == 1), 0, 1)
+            taken = jnp.where((odd == 0) & (choice == 1), 0, 1)
+            swaps = choice > 0
+            partners = [(k, k + 1 - 2 * (k % 2)) for k in range(groups)]
+
+            def trade(array):
+                return lax.ppermute(array, "dp", partners)
+
+            other_length = table[group + 1 - 2 * odd, taken]
+            changed = [swaps & (given == k) for k in range(slots)]
+            now = [jnp.where(changed[k], other_length, lengths[k]) for k in range(slots)]
+
+            def enter(array):
+                mine = lax.dynamic_slice_in_dim(array, given * SLOT, SLOT, axis=0)
+                came = trade(mine)
+                return [
+                    jnp.where(changed[k], came, array[k * SLOT : (k + 1) * SLOT]) for k in range(slots)
+                ]
+
+        else:
+            needed = jnp.max(jnp.sum(whole, axis=1))
+            changed = [jnp.zeros((), bool)] * slots
+            given = jnp.zeros((), jnp.int32)
+            now = [lengths[k] for k in range(slots)]
+
+            def trade(array):
+                return array
+
+            def enter(array):
+                return [array[k * SLOT : (k + 1) * SLOT] for k in range(slots)]
+
+        starts = [jnp.zeros((), jnp.int32)]
+        for k in range(slots - 1):
+            starts.append(starts[-1] + -(-now[k] // 16) * 16)
+        seats = jnp.arange(rows, dtype=jnp.int32)
+        segment = sum((seats >= starts[k]).astype(jnp.int32) for k in range(1, slots))
+        first_seat = sum(jnp.where(segment == k, starts[k], 0) for k in range(slots))
+        length_at = sum(jnp.where(segment == k, now[k], 0) for k in range(slots))
+        places = seats - first_seat
+        valid = places < length_at
+
+        def pack(pieces):
+            packed = jnp.concatenate(pieces, axis=0)
+            for k in range(1, slots):
+                packed = lax.dynamic_update_slice_in_dim(packed, pieces[k], starts[k], axis=0)
+            return packed
 
         def own_rows(array):
-            pieces = array.reshape(rows // PIECE, count, PIECE // count, -1)
-            mine = lax.dynamic_index_in_dim(pieces, me, axis=1, keepdims=False)
+            split = array.reshape(rows // PIECE, count, PIECE // count, -1)
+            mine = lax.dynamic_index_in_dim(split, me, axis=1, keepdims=False)
             return mine.reshape(rows // count, -1)
 
-        valid = (jnp.arange(slot, dtype=jnp.int32)[None, :] < lengths[:, None]).reshape(rows, 1)
-        own = own_rows(hidden)
-        own_valid = own_rows(valid.astype(F32))
-        grad_feed = jnp.where(valid, cotangent, jnp.zeros((), BF16))
+        tokens = pack(enter(hidden))
+        grad_feed = jnp.where(valid[:, None], pack(enter(cotangent)), jnp.zeros((), BF16))
+        own = own_rows(tokens)
+        own_valid = own_rows(valid.astype(F32)[:, None])
         own_grad = own_rows(grad_feed)
-
-        normed, _ = norm_parts(hidden.astype(F32))
+        normed, _ = norm_parts(tokens.astype(F32))
         norm_in = (normed * vectors[0] + vectors[1]).astype(BF16)
-        seats = jnp.arange(rows, dtype=jnp.int32)
-        segment = seats // slot
-        places = lax.rem(seats, slot).astype(F32)
-        as_key = jnp.where(valid[:, 0], segment, -1)
-        as_query = jnp.where(valid[:, 0], segment, -2)
+        as_key = jnp.where(valid, segment, -1)
+        as_query = jnp.where(valid, segment, -2)
+        spots = places.astype(F32)
         segments = (
             as_query[:, None],
             as_key[None, :],
-            places[None, :],
+            spots[None, :],
             as_query[None, :],
             as_key[:, None],
-            places[:, None],
+            spots[:, None],
         )
         shift = jnp.concatenate([bias_pair[0], jnp.zeros_like(bias_pair[0]), bias_pair[1]])[None]
-        norm_mid, residual, sums_one, qkv, mixed, totals = front_call(
-            count, slopes, norm_in, first_full, shift, own, own_valid, segments, vectors
-        )
-        branch_grad, residual_grad, sums_two, unit_grad, feed_part, expand_grad, reduce_grad = (
-            feed_call(
+        unit_shift = expand_bias.astype(F32)[None]
+
+        def scatter(array, dim):
+            return lax.psum_scatter(array, "dp", scatter_dimension=dim, tiled=True)
+
+        def layer(variant, size):
+            expand_full = lax.all_gather(expand_weight, "dp", axis=0, tiled=True)
+            reduce_full = lax.all_gather(reduce_weight, "dp", axis=1, tiled=True)
+            norm_mid, residual, sums_one, qkv, mixed, totals = front_call(
+                count, size, variant, slopes, norm_in, first_full, shift, own, own_valid, segments, vectors
+            )
+            branch_grad, residual_grad, sums_two, unit_grad, feed_part, expand_grad, reduce_grad = feed_call(
                 count,
+                variant,
                 norm_mid,
                 expand_full,
                 reduce_full,
                 grad_feed,
                 residual,
                 own_grad,
-                expand_bias.astype(F32)[None],
+                unit_shift,
                 vectors,
             )
+            reduce_grad = scatter(reduce_grad, 1)
+            expand_grad = scatter(expand_grad, 0)
+            grad_triple, column_sums, output, sums_three, first_grad = back_call(
+                count,
+                rows,
+                variant,
+                slopes,
+                branch_grad,
+                first_full,
+                qkv,
+                mixed,
+                norm_in,
+                totals,
+                segments,
+                feed_part,
+                residual,
+                own_valid,
+                vectors,
+            )
+            hidden_grad, small, dp_small, first_grad = last_call(
+                groups,
+                count,
+                rows,
+                variant,
+                grad_triple,
+                first_full,
+                own,
+                residual_grad,
+                (sums_one, sums_two, sums_three),
+                own_valid,
+                column_sums,
+                unit_grad,
+                vectors,
+                first_grad,
+            )
+            return lax.optimization_barrier(
+                (output, hidden_grad, small, dp_small, reduce_grad, expand_grad, first_grad)
+            )
+
+        sizes = [size for size in SIZES if size < rows] + [rows]
+
+        def branch(variant, size):
+            def run():
+                return layer(variant, size)
+
+            return run
+
+        index = sum((needed > size).astype(jnp.int32) for size in sizes[:-1])
+        output, hidden_grad, small, dp_small, reduce_grad, expand_grad, first_grad = lax.switch(
+            index, [branch(k, size) for k, size in enumerate(sizes)]
         )
-
-        def scatter(array, dim):
-            return lax.psum_scatter(array, "dp", scatter_dimension=dim, tiled=True)
-
-        reduce_grad = scatter(reduce_grad, 1)
-        expand_grad = scatter(expand_grad, 0)
-        grad_triple, column_sums, output, sums_three, first_grad = back_call(
-            count,
-            slopes,
-            branch_grad,
-            first_full,
-            qkv,
-            mixed,
-            norm_in,
-            totals,
-            segments,
-            feed_part,
-            residual,
-            own_valid,
-            vectors,
-        )
-        first_grad = scatter(first_grad, 0)
-        hidden_grad, small, dp_small = last_call(
-            groups,
-            count,
-            grad_triple,
-            first_full,
-            own,
-            residual_grad,
-            (sums_one, sums_two, sums_three),
-            own_valid,
-            column_sums,
-            unit_grad,
-            vectors,
-        )
-        reduce_grad, expand_grad, triple_grad, merge_grad, output, hidden_grad = close_call(
-            reduce_grad, expand_grad, first_grad, output, hidden_grad
-        )
-        share = width // groups
+        at = sum(jnp.where(given == k, starts[k], 0) for k in range(slots))
+        swapped = [
+            trade(lax.dynamic_slice_in_dim(array, at, SLOT, axis=0)) for array in (output, hidden_grad)
+        ]
+        facts = jnp.stack([*starts, *[one.astype(jnp.int32) for one in changed], *lengths])
+        reduce_grad, expand_grad, triple_grad, merge_grad = close_call(reduce_grad, expand_grad, first_grad)
+        output, hidden_grad = unpack_call(facts, (output, hidden_grad), swapped)
         small = small.transpose(1, 0, 2).reshape(8, -1)
         totals = small[6, :4]
         if share < 128:
-            place = lax.rem(lax.axis_index("dp") * share, 128)
+            place = lax.rem(group * share, 128)
             small = lax.dynamic_slice_in_dim(small, place, share, axis=1)
         flat = dp_small.reshape(-1)
         triple_sums = flat[: 3 * head_cols]
@@ -1276,10 +1478,8 @@
 
 
 def solution(mesh):
-    local = make_local(mesh.shape["dp"], mesh.shape["mp"])
-
     return jax.shard_map(
-        local,
+        make_local(mesh.shape["dp"], mesh.shape["mp"]),
         mesh=mesh,
         in_specs=(
             P("dp", None),

time: 594 us -> 566 us (0.953)
  Pallas kernels: 506 us -> 450 us
  loops' own time: 0 us -> 21.9 us
  waiting for transfers between devices: 25.5 us -> 13.5 us
  local copies, waits for them, and re-layouts: 15 us -> 21.8 us
  between operations: 15.3 us -> 21.6 us
    another operation x0 -> x1, loops' own time: none -> 21.9 us  [local(): lax.switch(index, [branch(k, size) for k, size in enumerate(sizes)])]
    pallas_call x1, Pallas kernels: 120 us -> 101 us  [back_call(): pl.pallas_call(functools.partial(back_kernel, count, head_cols), name='ba...]
    pallas_call x1, Pallas kernels: 120 us -> 104 us  [last_call(): pl.pallas_call(functools.partial(last_kernel, groups, count), name='last_...]
    pallas_call x1, Pallas kernels: 135 us -> 120 us  [feed_call(): pl.pallas_call(functools.partial(feed_kernel, count, pieces), name='feed_...]
    all_gather x3, waiting for transfers between devices: 23.5 us -> 11.6 us  [the longest x1 11.5 us: local(): lax.all_gather(first, 'dp', axis=0, tiled=True)]
    dynamic_slice x1 -> x8, local copies, waits for them, and re-layouts: 1.56 us -> 11 us  [the longest x2 4.77 us: local(): lax.dynamic_slice_in_dim(array, at, SLOT, axis=0)]
    pallas_call x1, Pallas kernels: 121 us -> 113 us  [front_call(): pl.pallas_call(functools.partial(front_kernel, count, head_cols), name='f...]
    pallas_call x0 -> x1, Pallas kernels: none -> 7.06 us  [unpack_call(): pl.pallas_call(unpack_kernel, name='unpack', out_shape=(jax.ShapeDtypeStr...]
  transfers between devices with their start and end apart: 6 -> 9, of which waited for: 1 -> 1; matrix products, arithmetic and copies ran while one was open for 4% -> 5% of each run, Pallas kernels for 61% -> 58%
where the time goes in v4:
time: 566 us; the launch traced here: 560 us
  Pallas kernels  450 us (80%)
  loops' own time  21.9 us (4%)
  local copies, waits for them, and re-layouts  21.8 us (4%)
  between operations  21.6 us (4%)
  other arithmetic  19 us (3%)
  waiting for transfers between devices  13.5 us (2%)
  blocking collectives  10.6 us (2%)
    pallas_call x1, Pallas kernels, feed_call(): pl.pallas_call(functools.partial(feed_kernel, count, pieces), name='feed_...  120 us
    pallas_call x1, Pallas kernels, front_call(): pl.pallas_call(functools.partial(front_kernel, count, head_cols), name='f...  113 us
    pallas_call x1, Pallas kernels, last_call(): pl.pallas_call(functools.partial(last_kernel, groups, count), name='last_...  104 us
    pallas_call x1, Pallas kernels, back_call(): pl.pallas_call(functools.partial(back_kernel, count, head_cols), name='ba...  101 us
    another operation x1, loops' own time, local(): lax.switch(index, [branch(k, size) for k, size in enumerate(sizes)])  21.9 us
    all_gather x1, waiting for transfers between devices, local(): lax.all_gather(first, 'dp', axis=0, tiled=True)  11.5 us
  transfers between devices with their start and end apart: 9, of which 1 were waited for; matrix products, arithmetic and copies ran while one was open for 5% of the time, Pallas kernels for 58%

profile of v4, /device:TPU:0, one launch (start us, length us, event | category | flops | bytes accessed | tf_op | source)
XLA Modules:
  0.0 560.0 jit_solution(7893667629508072269)
XLA Ops:
  7.3 1.1 copy.36
  8.4 1.4 copy.35
  10.1 1.1 pad_maximum_fusion.2
  11.5 10.6 %all_gather.36 = bf16[7,2048]{1,0:T(8,128)(2,1)S(1)} all-gather(bf16[7,256]{1,0:T(8,128)(2,1)S(1)} %stack.79), channel_id=1, replica_groups=mesh['dp'=8,'mp'=4] {'dp'}, dimensions={1}, use_global_device_ids=true | all-gather | bytes 32256 | tf_op jit(solution)/shard_map/all_gather | solution.py:1279
  22.5 0.6 minimum_reduce_fusion
  23.3 0.7 iota_reduce_fusion
  24.7 1.9 constant_dynamic-slice_fusion.5
  26.6 0.4 collective-permute-start
  27.0 0.5 copy-done
  27.5 1.5 constant_dynamic-slice_fusion.3
  28.9 0.4 collective-permute-start.1
  29.9 0.6 dynamic_slice.30
  30.5 0.6 fusion.22
  36.6 0.6 fusion.12
  37.2 0.9 fusion.6
  38.1 1.0 convert_select_fusion
  39.1 6.4 %slice_select_fusion.1 = (bf16[512,2048]{1,0:T(8,128)(2,1)S(1)}, bf16[512,2048]{1,0:T(8,128)(2,1)S(1)}, bf16[512,2048]{1,0:T(8,128)(2,1)S(1)}, bf16[512,2048]{1,0:T(8,128)(2,1)S(1)}) fusion(bf16[512,2048]{1,0:T(8,128)(2,1)} %collective-permute-done.1, bf16[1024,2048]{1,0:T(8,128)(2,1)} %param.21, pred[]{:T(512)S(6)} %and.39, pred[]{:T(512)S(6)} %and.42, ...), kind=kLoop, calls=%fused_computation.12 | loop fusion | flops 4194304 | bytes 20971522 | tf_op jit(solution)/shard_map/jit(_where)/select_n | solution.py:1313
  45.5 0.6 pad_maximum_fusion
  46.4 0.6 convert_reduce_fusion
  47.0 1.2 fusion.2
  48.2 0.6 pad_maximum_fusion.1
  49.1 0.4 broadcast_select_fusion
  49.5 2.0 copy-done.1
  51.5 1.1 constant_dynamic-slice_fusion.2
  52.6 1.1 constant_dynamic-slice_fusion.4
  53.7 3.1 fusion.5
  56.8 11.5 %all-gather.32.cloned.1.call-done = bf16[2048,2048]{1,0:T(8,128)(2,1)} async-done(((bf16[256,2048]{1,0:T(8,128)(2,1)}), bf16[2048,2048]{1,0:T(8,128)(2,1)}) %all-gather.32.cloned.1.call-update) | async-done | bytes 8388624 | tf_op jit(solution)/shard_map/all_gather | solution.py:1273
  68.4 464.2 %conditional.1 = (bf16[1024,2048]{1,0:T(8,128)(2,1)}, bf16[1024,2048]{1,0:T(8,128)(2,1)}, f32[2,8,128]{2,1,0:T(8,128)S(1)}, f32[32,128]{1,0:T(8,128)S(1)}, bf16[...) conditional(s32[]{:T(128)} %clamp.3, (f32[8]{0:T(128)S(1)}, ...), branch_computations={%region_4.7_spmd, %region_7.10_spmd, %region_10.13_spmd, %region_1... | conditional | flops 485000019968 | bytes 117475600 | solution.py:1439
  76.8 0.7 all-gather.18.cloned.1.call-update
  77.5 0.7 all-gather.16.cloned.1.call-update
  78.3 0.8 copy.40.valid
  79.1 112.8 %front_line.6 = (bf16[832,2048]{1,0:T(8,128)(2,1)}, f32[208,2048]{1,0:T(8,128)}, f32[8,2048]{1,0:T(8,128)}, bf16[832,1536]{1,0:T(8,128)(2,1)}, bf16[832,512]{1,0:T(8,128)(2,1)}, /*index=5*/f32[8,832]{1,0:T(8,128)}) custom-call(f32[8]{0:T(128)S(1)} %get-tuple-element.220.slopes, bf16[1024,2048]{1,0:T(8,128)(2,1)} %get-tuple-element.221.norm_hbm, ...), custom_call_target="tpu_custom_call" | custom-call | flops 120000004096 | bytes 1048576 | tf_op jit(solution)/shard_map/cond/branch_1_fun/front_line/pallas_call | solution.py:439
  191.9 120.2 %feed_line.6 = (bf16[832,2048]{1,0:T(8,128)(2,1)}, f32[208,2048]{1,0:T(8,128)}, f32[8,2048]{1,0:T(8,128)}, f32[1,2048]{1,0:T(1,128)}, bf16[832,2048]{1,0:T(8,128...) custom-call(bf16[832,2048]{1,0:T(8,128)(2,1)} %get-tuple-element.230.middle_hbm, ...), custom_call_target="tpu_custom_call" | custom-call | flops 130000003072 | bytes 1048576 | tf_op jit(solution)/shard_map/cond/branch_1_fun/feed_line/pallas_call | solution.py:619
  312.2 0.5 reduce-scatter.17.cloned.1.call-update
  312.7 0.5 copy-done.4
  313.2 101.4 %back_line.6 = (bf16[832,1536]{1,0:T(8,128)(2,1)}, f32[1,1536]{1,0:T(1,128)}, bf16[1024,2048]{1,0:T(8,128)(2,1)}, f32[8,2048]{1,0:T(8,128)}, bf16[2048,2048]{1,0:T(8,128)(2,1)}) custom-call(f32[8]{0:T(128)S(1)} %get-tuple-element.220.slopes, bf16[832,2048]{1,0:T(8,128)(2,1)} %get-tuple-element.237.branch_hbm, ...), custom_call_target="tpu_custom_call" | custom-call | flops 120000004096 | bytes 1048576 | tf_op jit(solution)/shard_map/cond/branch_1_fun/back_line/pallas_call | solution.py:792
  414.7 104.5 %last_line.6 = (bf16[1024,2048]{1,0:T(8,128)(2,1)}, f32[2,8,128]{2,1,0:T(8,128)S(1)}, f32[32,128]{1,0:T(8,128)S(1)}, f32[256,2048]{1,0:T(8,128)}) custom-call(bf16[832,1536]{1,0:T(8,128)(2,1)} %get-tuple-element.246.triple_grad, bf16[2048,2048]{1,0:T(8,128)(2,1)} %get-tuple-element.222.weights_hbm.merge.triple_hbm, ...), custom_call_target="tpu_custom_call" | custom-call | flops 115000000512 | bytes 1048576 | tf_op jit(solution)/shard_map/cond/branch_1_fun/last_line/pallas_call | solution.py:1071
  532.6 3.3 constant_dynamic-slice_fusion.1
  535.9 1.5 constant_dynamic-slice_fusion
  537.4 0.5 collective-permute-start.2
  537.9 0.6 stack.86.facts
  538.5 0.6 slice.166
  539.7 0.6 pad_maximum_fusion.4
  540.3 0.5 fusion.17
  540.8 0.6 fusion.20
  541.4 0.6 slice_bitcast_fusion
  542.0 4.2 close.1
  546.2 7.1 %unpack.1 = (bf16[1024,2048]{1,0:T(8,128)(2,1)}, bf16[1024,2048]{1,0:T(8,128)(2,1)}) custom-call(s32[6]{0:T(128)} %stack.86.facts, bf16[1024,2048]{1,0:T(8,128)(2,1)} %get-tuple-element.410.rest_0_, bf16[1024,2048]{1,0:T(8,128)(2,1)} %get-tuple-element.411.rest_1_, bf16[512,2048]{1,0:T(8,128)(2,1)} %collective-permute-done.2.rest_2_, ...), custom_call_target="tpu_custom_call" | custom-call | flops 6000000000 | bytes 1048576 | tf_op jit(solution)/shard_map/unpack/pallas_call | solution.py:1220
  (86 shorter events, 2.2 us)
Async XLA Ops:
  7.2 4.1 copy-start.17
  7.2 4.1 copy-start.18
  7.2 4.1 copy-start.19
  7.2 4.1 copy-start.20
  7.2 4.1 copy-start.21
  7.2 4.1 copy-start.22
  7.2 4.1 copy-start.9
  7.3 61.1 %all-gather.32.cloned.1.call-start = ((), (), s32[]{:S(2)}) async-start(), calls=%async_computation.30 | async-start | bytes 9437184 | tf_op jit(solution)/shard_map/all_gather | solution.py:1273
  24.6 2.8 copy-start
  24.7 7.8 %copy-start.8 = (bf16[2,512]{1,0:T(2,128)(2,1)S(1)}, bf16[2,512]{1,0:T(2,128)(2,1)}, u32[]{:S(2)}) copy-start(bf16[2,512]{1,0:T(2,128)(2,1)} %param.26) | copy-start | bytes 6148
  24.7 7.9 %copy-start.11 = (bf16[2048]{0:T(1024)(128)(2,1)S(1)}, bf16[2048]{0:T(1024)(128)(2,1)}, u32[]{:S(2)}) copy-start(bf16[2048]{0:T(1024)(128)(2,1)} %param.32) | copy-start | bytes 12292
  26.6 12.5 %collective-permute-start = (bf16[512,2048]{1,0:T(8,128)(2,1)S(1)}, bf16[512,2048]{1,0:T(8,128)(2,1)}, u32[]{:S(2)}, u32[]{:S(2)}) collective-permute-start(bf16[512,2048]{1,0:T(8,128)(2,1)S(1)} %constant_dynamic-slice_fusion.5), channel_id=1, source_target_pairs={{0,4},{4,0},{8,12},{12,8},{16,20},{20,16},{24,28},{28,24},{1,5},{5... | collective-permute-start | bytes 6291464 | tf_op jit(solution)/shard_map/ppermute | solution.py:1303
  28.9 10.2 %collective-permute-start.1 = (bf16[512,2048]{1,0:T(8,128)(2,1)}, bf16[512,2048]{1,0:T(8,128)(2,1)}, u32[]{:S(2)}, u32[]{:S(2)}) collective-permute-start(bf16[512,2048]{1,0:T(8,128)(2,1)} %constant_dynamic-slice_fusion.3), channel_id=1, source_target_pairs={{0,4},{4,0},{8,12},{12,8},{16,20},{20,16},{24,28},{28,24},{1,5},{5... | collective-permute-start | bytes 6291464 | tf_op jit(solution)/shard_map/ppermute | solution.py:1303
  49.5 2.0 copy-start.1
  76.7 115.1 %all-gather.18.cloned.1.call-start = ((), (), s32[]{:S(2)}) async-start(), calls=%async_computation.15 | async-start | bytes 9437184 | tf_op jit(solution)/shard_map/cond/branch_1_fun/all_gather | solution.py:1375
  77.5 114.4 %all-gather.16.cloned.1.call-start = ((), (), s32[]{:S(2)}) async-start(), calls=%async_computation.14 | async-start | bytes 9437184 | tf_op jit(solution)/shard_map/cond/branch_1_fun/all_gather | solution.py:1374
  78.2 441.0 %reduce-scatter.15.cloned.1.call-start = ((), (), s32[]{:S(2)}) async-start(), calls=%async_computation.16 | async-start | bytes 9437184 | tf_op jit(solution)/shard_map/cond/branch_1_fun/reduce_scatter | solution.py:1371
  312.1 207.1 %reduce-scatter.17.cloned.1.call-start = ((), (), s32[]{:S(2)}) async-start(), calls=%async_computation.17 | async-start | bytes 9437184 | tf_op jit(solution)/shard_map/cond/branch_1_fun/reduce_scatter | solution.py:1371
  312.2 1.0 copy-start.4
  312.2 1.0 copy-start.13
  532.6 3.3 copy-start.2
  532.6 5.3 copy-start.10
  537.4 8.8 %collective-permute-start.3 = (bf16[512,2048]{1,0:T(8,128)(2,1)}, bf16[512,2048]{1,0:T(8,128)(2,1)}, u32[]{:S(2)}, u32[]{:S(2)}) collective-permute-start(bf16[512,2048]{1,0:T(8,128)(2,1)} %constant_dynamic-slice_fusion), channel_id=1, source_target_pairs={{0,4},{4,0},{8,12},{12,8},{16,20},{20,16},{24,28},{28,24},{1,5},{5... | collective-permute-start | bytes 6291464 | tf_op jit(solution)/shard_map/ppermute | solution.py:1303
  537.4 8.9 %collective-permute-start.2 = (bf16[512,2048]{1,0:T(8,128)(2,1)}, bf16[512,2048]{1,0:T(8,128)(2,1)}, u32[]{:S(2)}, u32[]{:S(2)}) collective-permute-start(bf16[512,2048]{1,0:T(8,128)(2,1)} %constant_dynamic-slice_fusion.1), channel_id=1, source_target_pairs={{0,4},{4,0},{8,12},{12,8},{16,20},{20,16},{24,28},{28,24},{1,5},{5... | collective-permute-start | bytes 6291464 | tf_op jit(solution)/shard_map/ppermute | solution.py:1303
Sparse Core Ops, SparseCore 0:
  11.3 56.9 all-gather.31
  79.4 55.8 all-gather.17
  137.3 54.3 all-gather.15
  312.3 69.5 reduce-scatter.14
  385.2 108.9 reduce-scatter.16

commit v5 on v4

--- a/solution.py
+++ b/solution.py
@@ -284,23 +284,46 @@
 
 def paced(line_tick, tiles, steps, later, drain):
     step = 0
-    plans = [spread(work, size // PIECE) for (_, size), work in zip(tiles, later)]
-    assert len(later) == len(tiles) and len(drain) == steps - sum(map(len, plans))
-    for shares in (*plans, drain):
-        span = len(shares)
+    spans = [size // PIECE for _, size in tiles]
+    plans = [work if callable(work) else spread(work, span) for work, span in zip(later, spans)]
+    spans.append(steps - sum(spans))
+    assert len(later) == len(tiles) and (callable(drain) or len(drain) == spans[-1])
+    for span, shares in zip(spans, (*plans, drain)):
 
         @pl.loop(0, span)
-        def _(k, step=step, shares=shares):
+        def _(k, step=step, span=span, shares=shares):
             line_tick(step + k)
-            for phase, share in enumerate(shares):
-                if share:
-
-                    @pl.when(k == phase)
-                    def _(share=share):
-                        for closure in share:
-                            closure()
+            if callable(shares):
+                shares(k, span)
+            else:
+                for phase, share in enumerate(shares):
+                    if share:
+
+                        @pl.when(k == phase)
+                        def _(share=share):
+                            for closure in share:
+                                closure()
 
         step += span
+
+
+def stepped(opening, each, amount, closing):
+    def work(k, span):
+        per = -(-amount // span)
+
+        @pl.when(k == 0)
+        def _():
+            for closure in opening:
+                closure()
+
+        pl.loop(jnp.minimum(k * per, amount), jnp.minimum((k + 1) * per, amount))(each)
+
+        @pl.when(k == span - 1)
+        def _():
+            for closure in closing:
+                closure()
+
+    return work
 
 
 def halves(values):
@@ -382,7 +405,7 @@
             total = jnp.sum(raised, axis=1, keepdims=True)
             out = out + dot32((raised * (1.0 / total)).astype(BF16), value[k])
             sums_log = jnp.where(lane == k, most + jnp.log(total), sums_log)
-        totals[2 * pair : 2 * pair + 2, start : start + size] = sums_log.T[:2, :]
+        totals[pair, :, start : start + size] = sums_log.T[:2, :]
         mixed[pl.ds(start, size), block(pair, PAIR)] = out.astype(BF16)
 
     def project_back(start, size):
@@ -398,13 +421,13 @@
 
     pairs = head_cols // PAIR
 
-    def work(start, size):
-        return [
-            functools.partial(project, start, size),
-            functools.partial(masks, start, size),
-            *[functools.partial(attend, start, size, pair) for pair in range(pairs)],
-            functools.partial(project_back, start, size),
-        ]
+    def work(start, size, *more):
+        return stepped(
+            [functools.partial(project, start, size), functools.partial(masks, start, size)],
+            functools.partial(attend, start, size),
+            pairs,
+            [functools.partial(project_back, start, size), *more],
+        )
 
     saves = (
         pltpu.make_async_copy(qkv, qkv_hbm, save_sem.at[0]),
@@ -415,8 +438,10 @@
         for copy in saves:
             copy.start()
 
-    for closure in work(*tiles[0]):
-        closure()
+    project(*tiles[0])
+    masks(*tiles[0])
+    pl.loop(0, pairs)(functools.partial(attend, *tiles[0]))
+    project_back(*tiles[0])
     later = [work(*tile) for tile in tiles[1:]] + [[save]]
     steps = ticks(count, line.pieces)
     drain = [[]] * (steps - line.pieces)
@@ -445,7 +470,7 @@
             jax.ShapeDtypeStruct((8, width), F32),
             jax.ShapeDtypeStruct((rows, 3 * head_cols), BF16),
             jax.ShapeDtypeStruct((rows, head_cols), BF16),
-            jax.ShapeDtypeStruct((head_cols // HEAD_DIM, rows), F32),
+            jax.ShapeDtypeStruct((head_cols // PAIR, 2, rows), F32),
         ),
         in_specs=[SMEM] + [ANY] * 2 + [VMEM] * 7,
         out_specs=(ANY, VMEM, VMEM, ANY, ANY, VMEM),
@@ -469,7 +494,7 @@
 def feed_kernel(
     count, pieces, middle_hbm, expand_hbm, reduce_hbm, grad_hbm, residual, own_grad, unit_shift, vectors,
     branch_grad, residual_grad, sums, unit_grad, feed_hbm, expand_grad, reduce_grad,
-    middle, expand, reduce, grad, active, pre_grad, part, acc, stage, load_sem, stage_sem, *rest,
+    middle, expand, reduce, grad, active, pre_grad, part, acc, stage, feed_stage, load_sem, stage_sem, feed_sem, *rest,
 ):
     line = Line(count, part, branch_grad, *rest)
     units = expand.shape[1]
@@ -517,92 +542,110 @@
         for k, values in enumerate((low.astype(F32), grad_mid * normed, grad_mid, grad_out)):
             sums[k : k + 1, :] += jnp.sum(values, axis=0, keepdims=True)
 
-    def forward(start, size, low_k, high_k):
-        rows = pl.ds(start, size)
-        if low_k == 0:
-            for copy in load_rows(start // TILE):
+    def forward(start, size, k):
+        rows, cols = pl.ds(start, size), block(k, BLOCK)
+        if start == 0:
+            for copy in load(k):
                 copy.wait()
-
-        @pl.loop(low_k, high_k)
-        def _(k):
-            cols = block(k, BLOCK)
-            if start == 0:
-                for copy in load(k):
-                    copy.wait()
-            pre = dot32(middle[rows, :], expand[:, cols]) + unit_shift[:, cols]
-            half = 0.5 + 0.5 * lax.erf(pre * 0.7071067811865476)
-            slope = half + pre * (0.3989422804014327 * jnp.exp(-0.5 * pre * pre))
-            active[rows, cols] = (pre * half).astype(BF16)
-            low = (dot_nt(grad[rows, :], reduce[cols, :]) * slope).astype(BF16)
-            pre_grad[rows, cols] = low
-            unit_grad[:, cols] += jnp.sum(low.astype(F32), axis=0, keepdims=True)
-
-    def backward(start, size, low_k, high_k):
-        rows = pl.ds(start, size)
-
-        @pl.loop(low_k, high_k)
-        def _(k):
-            cols = block(k, BLOCK)
-            part[rows, cols] = dot_nt(pre_grad[rows, :], expand[cols, :]).astype(BF16)
+        pre = dot32(middle[rows, :], expand[:, cols]) + unit_shift[:, cols]
+        half = 0.5 + 0.5 * lax.erf(pre * 0.7071067811865476)
+        slope = half + pre * (0.3989422804014327 * jnp.exp(-0.5 * pre * pre))
+        active[rows, cols] = (pre * half).astype(BF16)
+        low = (dot_nt(grad[rows, :], reduce[cols, :]) * slope).astype(BF16)
+        pre_grad[rows, cols] = low
+        unit_grad[:, cols] += jnp.sum(low.astype(F32), axis=0, keepdims=True)
+
+    def backward(start, size, k):
+        rows, cols = pl.ds(start, size), block(k, BLOCK)
+        part[rows, cols] = dot_nt(pre_grad[rows, :], expand[cols, :]).astype(BF16)
+
+    backs = width // BLOCK
+
+    def unit(start, size, k):
+        @pl.when(k < blocks)
+        def _():
+            forward(start, size, k)
+
+        @pl.when(k >= blocks)
+        def _():
+            backward(start, size, k - blocks)
 
     staged = {"rows": 0}
 
     def settle_slot(slot):
         rows = pl.ds(0, staged["rows"])
         pltpu.make_async_copy(
-            stage.at[slot, rows], feed_hbm.at[rows, pl.ds(0, BLOCK)], stage_sem.at[slot]
+            feed_stage.at[slot, rows], feed_hbm.at[rows, pl.ds(0, BLOCK)], feed_sem.at[slot]
         ).wait()
 
-    def emit(target, start, size, product):
+    def feed_product(start, size):
         before = staged["rows"]
-
-        @pl.loop(0, target.shape[1] // BLOCK)
+        rows = pl.ds(start, size)
+
+        @pl.loop(0, backs)
         def _(k):
-            slot = lax.rem(k, 4)
+            slot, cols = lax.rem(k, 4), block(k, BLOCK)
             if before:
                 settle_slot(slot)
-            stage[slot, :size, :] = product(block(k, BLOCK)).astype(BF16)
+            feed_stage[slot, :size, :] = dot32(active[rows, :], reduce[:, cols]).astype(BF16)
             pltpu.make_async_copy(
-                stage.at[slot, pl.ds(0, size)],
-                target.at[pl.ds(start, size), block(k, BLOCK)],
-                stage_sem.at[slot],
+                feed_stage.at[slot, pl.ds(0, size)], feed_hbm.at[rows, cols], feed_sem.at[slot]
             ).start()
 
         staged["rows"] = size
 
-    def feed_product(start, size):
-        emit(feed_hbm, start, size, lambda cols: dot32(active[pl.ds(start, size), :], reduce[:, cols]))
-
-    def reduce_product(start):
-        emit(reduce_grad, start, BLOCK, lambda cols: dot_tn(active[:, pl.ds(start, BLOCK)], grad[:, cols]))
-
-    def expand_product(start):
-        emit(expand_grad, start, BLOCK, lambda cols: dot_tn(middle[:, pl.ds(start, BLOCK)], pre_grad[:, cols]))
-
-    backs = width // BLOCK
+    def put(slot, target):
+        return pltpu.make_async_copy(stage.at[slot], target, stage_sem.at[slot])
+
+    def product(u):
+        def emit(target, start, columns, value):
+            @pl.loop(0, columns // BLOCK)
+            def _(k):
+                slot, cols = lax.rem(k, 4), block(k, BLOCK)
+
+                @pl.when(u > 0)
+                def _():
+                    put(slot, target.at[pl.ds(0, BLOCK), pl.ds(0, BLOCK)]).wait()
+
+                stage[slot] = value(cols).astype(BF16)
+                put(slot, target.at[start, cols]).start()
+
+        @pl.when(u < blocks)
+        def _():
+            rows = block(u, BLOCK)
+            emit(reduce_grad, rows, width, lambda cols: dot_tn(active[:, rows], grad[:, cols]))
+
+        @pl.when(u >= blocks)
+        def _():
+            rows = block(u - blocks, BLOCK)
+            emit(expand_grad, rows, units, lambda cols: dot_tn(middle[:, rows], pre_grad[:, cols]))
+
     assert backs == 4 and blocks == 4
 
-    def work(start, size):
-        return [
-            functools.partial(forward, start, size, 0, blocks // 2),
-            functools.partial(forward, start, size, blocks // 2, blocks),
-            functools.partial(backward, start, size, 0, backs // 2),
-            functools.partial(backward, start, size, backs // 2, backs),
-        ]
-
-    for closure in work(*tiles[0]):
-        closure()
+    def arrive(start):
+        for copy in load_rows(start // TILE):
+            copy.wait()
+
+    arrive(0)
+    pl.loop(0, blocks + backs)(functools.partial(unit, *tiles[0]))
     later = [
-        [*work(*after), functools.partial(feed_product, *tile)] for tile, after in zip(tiles, tiles[1:])
+        stepped(
+            [functools.partial(arrive, after[0])],
+            functools.partial(unit, *after),
+            blocks + backs,
+            [functools.partial(feed_product, *tile)],
+        )
+        for tile, after in zip(tiles, tiles[1:])
     ]
-    products = [functools.partial(reduce_product, r) for r in range(0, units, BLOCK)]
-    products += [functools.partial(expand_product, r) for r in range(0, width, BLOCK)]
     steps = ticks(count, pieces)
     beside = tiles[-1][1] // PIECE
-    taken = len(products) * beside // (steps - pieces + beside)
-    later.append([functools.partial(feed_product, *tiles[-1]), *products[:taken]])
-    drain = spread(products[taken:], steps - pieces)
+    amount = blocks + backs
+    taken = amount * beside // (steps - pieces + beside)
+    later.append(stepped([functools.partial(feed_product, *tiles[-1])], product, taken, []))
+    drain = stepped([], lambda u: product(u + taken), amount - taken, [])
     paced(lambda step: tick(line, step, finish), tiles, steps, later, drain)
+    for slot in range(4):
+        put(slot, expand_grad.at[pl.ds(0, BLOCK), pl.ds(0, BLOCK)]).wait()
     for slot in range(4):
         settle_slot(slot)
 
@@ -640,7 +683,9 @@
             pltpu.VMEM((rows, width), BF16),
             pltpu.VMEM((PIECE // count, width), F32),
             pltpu.VMEM((4, BLOCK, BLOCK), BF16),
+            pltpu.VMEM((4, TILE, BLOCK), BF16),
             pltpu.SemaphoreType.DMA((4, most)),
+            pltpu.SemaphoreType.DMA((4,)),
             pltpu.SemaphoreType.DMA((4,)),
             *Line.scratch(count, pieces, width),
         ],
@@ -718,7 +763,7 @@
         for k in range(2):
             scores = dot_nt(key, query[k]) + slopes[2 * pair + k] * place_col[:keys, :]
             scores = jnp.where(mask[:keys, :size] > 0.5, scores * 0.125, -1000000000.0)
-            soft = jnp.exp(scores - totals[2 * pair + k : 2 * pair + k + 1, rows])
+            soft = jnp.exp(scores - totals[pair, k : k + 1, rows])
             grad_probs = dot_nt(value, grad[k])
             row_terms = jnp.sum(soft * grad_probs, axis=0, keepdims=True)
             grad_scores = (soft * (grad_probs - row_terms)).astype(BF16)
@@ -752,12 +797,13 @@
 
     pairs = head_cols // PAIR
 
-    def work(start, size, first):
-        return [
-            functools.partial(open_tile, start, size),
-            *[functools.partial(back, start, size, first, pair) for pair in range(pairs)],
-            functools.partial(close_tile, start, size),
-        ]
+    def work(start, size, first, *more):
+        return stepped(
+            [functools.partial(open_tile, start, size)],
+            functools.partial(back, start, size, first),
+            pairs,
+            [functools.partial(close_tile, start, size), *more],
+        )
 
     products = [
         (branch_grad, mixed, r, c, 3 * head_cols)
@@ -769,10 +815,8 @@
         for c in range(0, 3 * head_cols, BLOCK)
     ]
     jobs = [functools.partial(job, k, *product) for k, product in enumerate(products)]
-    later = [work(*tile, k == 0) for k, tile in enumerate(reversed(tiles))]
-    for k in range(1, len(tiles)):
-        later[k - 1].append(lambda k=k: load_feed(k).wait())
-    later[-1].append(load_norm.wait)
+    waits = [load_feed(k).wait for k in range(1, len(tiles))] + [load_norm.wait]
+    later = [work(*tile, k == 0, wait) for k, (tile, wait) in enumerate(zip(reversed(tiles), waits))]
     steps = ticks(count, line.pieces)
     drain = spread(jobs, steps - line.pieces)
     paced(lambda step: tick(line, step, finish), tiles, steps, later, drain)

time: 566 us -> 559 us (0.988)
  Pallas kernels: 450 us -> 438 us
  waiting for transfers between devices: 13.5 us -> 21.6 us
    pallas_call x1, Pallas kernels: 113 us -> 104 us  [front_call(): pl.pallas_call(functools.partial(front_kernel, count, head_cols), name='f...]
    all_gather x1, waiting for transfers between devices: 0.02 us -> 8.56 us  [layer(): expand_full = lax.all_gather(expand_weight, 'dp', axis=0, tiled=True)]
  transfers between devices with their start and end apart: 9 -> 9, of which waited for: 1 -> 2; matrix products, arithmetic and copies ran while one was open for 5% -> 5% of each run, Pallas kernels for 58% -> 57%
where the time goes in v5:
time: 559 us; the launch traced here: 553 us
  Pallas kernels  438 us (78%)
  local copies, waits for them, and re-layouts  22.2 us (4%)
  between operations  21.7 us (4%)
  waiting for transfers between devices  21.6 us (4%)
  other arithmetic  19 us (3%)
  loops' own time  17 us (3%)
  blocking collectives  10.6 us (2%)
    pallas_call x1, Pallas kernels, feed_call(): pl.pallas_call(functools.partial(feed_kernel, count, pieces), name='feed_...  116 us
    pallas_call x1, Pallas kernels, last_call(): pl.pallas_call(functools.partial(last_kernel, groups, count), name='last_...  105 us
    pallas_call x1, Pallas kernels, front_call(): pl.pallas_call(functools.partial(front_kernel, count, head_cols), name='f...  104 us
    pallas_call x1, Pallas kernels, back_call(): pl.pallas_call(functools.partial(back_kernel, count, head_cols), name='ba...  102 us
    another operation x1, loops' own time, local(): lax.switch(index, [branch(k, size) for k, size in enumerate(sizes)])  17 us
    all_gather x1, waiting for transfers between devices, local(): lax.all_gather(first, 'dp', axis=0, tiled=True)  11.5 us
  transfers between devices with their start and end apart: 9, of which 2 were waited for; matrix products, arithmetic and copies ran while one was open for 5% of the time, Pallas kernels for 57%

profile of v5, /device:TPU:0, one launch (start us, length us, event | category | flops | bytes accessed | tf_op | source)
XLA Modules:
  0.0 552.5 jit_solution(15743502250854985660)
XLA Ops:
  7.3 1.1 copy.36
  8.4 1.4 copy.35
  10.1 1.1 pad_maximum_fusion.2
  11.5 10.6 %all_gather.36 = bf16[7,2048]{1,0:T(8,128)(2,1)S(1)} all-gather(bf16[7,256]{1,0:T(8,128)(2,1)S(1)} %stack.79), channel_id=1, replica_groups=mesh['dp'=8,'mp'=4] {'dp'}, dimensions={1}, use_global_device_ids=true | all-gather | bytes 32256 | tf_op jit(solution)/shard_map/all_gather | solution.py:1323
  22.5 0.6 minimum_reduce_fusion
  23.3 0.7 iota_reduce_fusion
  24.7 1.9 constant_dynamic-slice_fusion.5
  26.6 0.4 collective-permute-start
  27.0 0.5 copy-done
  27.5 1.5 constant_dynamic-slice_fusion.3
  29.9 0.6 dynamic_slice.30
  30.5 0.6 fusion.22
  36.6 0.6 fusion.12
  37.2 0.9 fusion.6
  38.1 1.0 convert_select_fusion
  39.1 6.4 %slice_select_fusion.1 = (bf16[512,2048]{1,0:T(8,128)(2,1)S(1)}, bf16[512,2048]{1,0:T(8,128)(2,1)S(1)}, bf16[512,2048]{1,0:T(8,128)(2,1)S(1)}, bf16[512,2048]{1,0:T(8,128)(2,1)S(1)}) fusion(bf16[512,2048]{1,0:T(8,128)(2,1)} %collective-permute-done.1, bf16[1024,2048]{1,0:T(8,128)(2,1)} %param.21, pred[]{:T(512)S(6)} %and.39, pred[]{:T(512)S(6)} %and.42, ...), kind=kLoop, calls=%fused_computation.12 | loop fusion | flops 4194304 | bytes 20971522 | tf_op jit(solution)/shard_map/jit(_where)/select_n | solution.py:1357
  45.5 0.6 pad_maximum_fusion
  46.4 0.6 convert_reduce_fusion
  47.0 1.2 fusion.2
  48.2 0.6 pad_maximum_fusion.1
  49.1 0.4 broadcast_select_fusion
  49.5 2.0 copy-done.1
  51.5 1.1 constant_dynamic-slice_fusion.2
  52.6 1.1 constant_dynamic-slice_fusion.4
  53.7 3.1 fusion.5
  56.8 11.5 %all-gather.32.cloned.1.call-done = bf16[2048,2048]{1,0:T(8,128)(2,1)} async-done(((bf16[256,2048]{1,0:T(8,128)(2,1)}), bf16[2048,2048]{1,0:T(8,128)(2,1)}) %all-gather.32.cloned.1.call-update) | async-done | bytes 8388624 | tf_op jit(solution)/shard_map/all_gather | solution.py:1317
  68.4 456.7 %conditional.1 = (bf16[1024,2048]{1,0:T(8,128)(2,1)}, bf16[1024,2048]{1,0:T(8,128)(2,1)}, f32[2,8,128]{2,1,0:T(8,128)S(1)}, f32[32,128]{1,0:T(8,128)S(1)}, bf16[...) conditional(s32[]{:T(128)} %clamp.3, (f32[8]{0:T(128)S(1)}, ...), branch_computations={%region_4.7_spmd, %region_7.10_spmd, %region_10.13_spmd, %region_1... | conditional | flops 485000019968 | bytes 117475600 | solution.py:1483
  74.8 0.7 all-gather.18.cloned.1.call-update
  75.5 0.7 all-gather.16.cloned.1.call-update
  76.2 0.8 copy.40.valid
  77.0 104.1 %front_line.6 = (bf16[832,2048]{1,0:T(8,128)(2,1)}, f32[208,2048]{1,0:T(8,128)}, f32[8,2048]{1,0:T(8,128)}, bf16[832,1536]{1,0:T(8,128)(2,1)}, bf16[832,512]{1,0:T(8,128)(2,1)}, /*index=5*/f32[4,2,832]{2,1,0:T(2,128)}) custom-call(f32[8]{0:T(128)S(1)} %get-tuple-element.220.slopes, bf16[1024,2048]{1,0:T(8,128)(2,1)} %get-tuple-element.221.norm_hbm, ...), custom_call_target="tpu_custom_call" | custom-call | flops 120000004096 | bytes 1048576 | tf_op jit(solution)/shard_map/cond/branch_1_fun/front_line/pallas_call | solution.py:464
  181.2 8.6 %all-gather.16.cloned.1.call-done.expand_hbm = bf16[2048,2048]{1,0:T(8,128)(2,1)} async-done(((bf16[256,2048]{1,0:T(8,128)(2,1)}), bf16[2048,2048]{1,0:T(8,128)(2,1)}) %all-gather.16.cloned.1.call-update) | async-done | bytes 8388624 | tf_op jit(solution)/shard_map/cond/branch_1_fun/all_gather | solution.py:1418
  189.7 116.1 %feed_line.6 = (bf16[832,2048]{1,0:T(8,128)(2,1)}, f32[208,2048]{1,0:T(8,128)}, f32[8,2048]{1,0:T(8,128)}, f32[1,2048]{1,0:T(1,128)}, bf16[832,2048]{1,0:T(8,128...) custom-call(bf16[832,2048]{1,0:T(8,128)(2,1)} %get-tuple-element.230.middle_hbm, ...), custom_call_target="tpu_custom_call" | custom-call | flops 130000003072 | bytes 1048576 | tf_op jit(solution)/shard_map/cond/branch_1_fun/feed_line/pallas_call | solution.py:662
  305.8 0.5 reduce-scatter.17.cloned.1.call-start
  306.4 1.0 copy-done.4
  307.4 102.2 %back_line.6 = (bf16[832,1536]{1,0:T(8,128)(2,1)}, f32[1,1536]{1,0:T(1,128)}, bf16[1024,2048]{1,0:T(8,128)(2,1)}, f32[8,2048]{1,0:T(8,128)}, bf16[2048,2048]{1,0:T(8,128)(2,1)}) custom-call(f32[8]{0:T(128)S(1)} %get-tuple-element.220.slopes, bf16[832,2048]{1,0:T(8,128)(2,1)} %get-tuple-element.237.branch_hbm, ...), custom_call_target="tpu_custom_call" | custom-call | flops 120000004096 | bytes 1048576 | tf_op jit(solution)/shard_map/cond/branch_1_fun/back_line/pallas_call | solution.py:836
  409.6 104.9 %last_line.6 = (bf16[1024,2048]{1,0:T(8,128)(2,1)}, f32[2,8,128]{2,1,0:T(8,128)S(1)}, f32[32,128]{1,0:T(8,128)S(1)}, f32[256,2048]{1,0:T(8,128)}) custom-call(bf16[832,1536]{1,0:T(8,128)(2,1)} %get-tuple-element.246.triple_grad, bf16[2048,2048]{1,0:T(8,128)(2,1)} %get-tuple-element.222.weights_hbm.merge.triple_hbm, ...), custom_call_target="tpu_custom_call" | custom-call | flops 115000000512 | bytes 1048576 | tf_op jit(solution)/shard_map/cond/branch_1_fun/last_line/pallas_call | solution.py:1115
  525.1 3.3 constant_dynamic-slice_fusion.1
  528.4 1.5 constant_dynamic-slice_fusion
  529.8 0.5 collective-permute-start.2
  530.4 0.6 stack.86.facts
  531.0 0.6 slice.166
  532.2 0.6 pad_maximum_fusion.4
  532.8 0.5 fusion.17
  533.3 0.6 fusion.20
  533.9 0.6 slice_bitcast_fusion
  534.5 4.2 close.1
  538.7 7.1 %unpack.1 = (bf16[1024,2048]{1,0:T(8,128)(2,1)}, bf16[1024,2048]{1,0:T(8,128)(2,1)}) custom-call(s32[6]{0:T(128)} %stack.86.facts, bf16[1024,2048]{1,0:T(8,128)(2,1)} %get-tuple-element.410.rest_0_, bf16[1024,2048]{1,0:T(8,128)(2,1)} %get-tuple-element.411.rest_1_, bf16[512,2048]{1,0:T(8,128)(2,1)} %collective-permute-done.2.rest_2_, ...), custom_call_target="tpu_custom_call" | custom-call | flops 6000000000 | bytes 1048576 | tf_op jit(solution)/shard_map/unpack/pallas_call | solution.py:1264
  (86 shorter events, 2.5 us)
Async XLA Ops:
  7.2 4.1 copy-start.17
  7.2 4.1 copy-start.18
  7.2 4.1 copy-start.19
  7.2 4.1 copy-start.20
  7.2 4.1 copy-start.21
  7.2 4.1 copy-start.22
  7.2 4.1 copy-start.9
  7.3 61.1 %all-gather.32.cloned.1.call-start = ((), (), s32[]{:S(2)}) async-start(), calls=%async_computation.30 | async-start | bytes 9437184 | tf_op jit(solution)/shard_map/all_gather | solution.py:1317
  24.6 2.8 copy-start
  24.7 7.8 %copy-start.8 = (bf16[2,512]{1,0:T(2,128)(2,1)S(1)}, bf16[2,512]{1,0:T(2,128)(2,1)}, u32[]{:S(2)}) copy-start(bf16[2,512]{1,0:T(2,128)(2,1)} %param.26) | copy-start | bytes 6148
  24.7 7.9 %copy-start.11 = (bf16[2048]{0:T(1024)(128)(2,1)S(1)}, bf16[2048]{0:T(1024)(128)(2,1)}, u32[]{:S(2)}) copy-start(bf16[2048]{0:T(1024)(128)(2,1)} %param.32) | copy-start | bytes 12292
  26.6 12.5 %collective-permute-start = (bf16[512,2048]{1,0:T(8,128)(2,1)S(1)}, bf16[512,2048]{1,0:T(8,128)(2,1)}, u32[]{:S(2)}, u32[]{:S(2)}) collective-permute-start(bf16[512,2048]{1,0:T(8,128)(2,1)S(1)} %constant_dynamic-slice_fusion.5), channel_id=1, source_target_pairs={{0,4},{4,0},{8,12},{12,8},{16,20},{20,16},{24,28},{28,24},{1,5},{5... | collective-permute-start | bytes 6291464 | tf_op jit(solution)/shard_map/ppermute | solution.py:1347
  28.9 10.2 %collective-permute-start.1 = (bf16[512,2048]{1,0:T(8,128)(2,1)}, bf16[512,2048]{1,0:T(8,128)(2,1)}, u32[]{:S(2)}, u32[]{:S(2)}) collective-permute-start(bf16[512,2048]{1,0:T(8,128)(2,1)} %constant_dynamic-slice_fusion.3), channel_id=1, source_target_pairs={{0,4},{4,0},{8,12},{12,8},{16,20},{20,16},{24,28},{28,24},{1,5},{5... | collective-permute-start | bytes 6291464 | tf_op jit(solution)/shard_map/ppermute | solution.py:1347
  49.5 2.0 copy-start.1
  74.7 106.4 %all-gather.18.cloned.1.call-start = ((), (), s32[]{:S(2)}) async-start(), calls=%async_computation.15 | async-start | bytes 9437184 | tf_op jit(solution)/shard_map/cond/branch_1_fun/all_gather | solution.py:1419
  75.5 114.3 %all-gather.16.cloned.1.call-start = ((), (), s32[]{:S(2)}) async-start(), calls=%async_computation.14 | async-start | bytes 9437184 | tf_op jit(solution)/shard_map/cond/branch_1_fun/all_gather | solution.py:1418
  76.2 438.3 %reduce-scatter.15.cloned.1.call-start = ((), (), s32[]{:S(2)}) async-start(), calls=%async_computation.16 | async-start | bytes 9437184 | tf_op jit(solution)/shard_map/cond/branch_1_fun/reduce_scatter | solution.py:1415
  305.8 208.7 %reduce-scatter.17.cloned.1.call-start = ((), (), s32[]{:S(2)}) async-start(), calls=%async_computation.17 | async-start | bytes 9437184 | tf_op jit(solution)/shard_map/cond/branch_1_fun/reduce_scatter | solution.py:1415
  306.4 1.0 copy-start.4
  306.4 1.0 copy-start.13
  525.0 3.3 copy-start.2
  525.1 5.3 copy-start.10
  529.8 8.8 %collective-permute-start.3 = (bf16[512,2048]{1,0:T(8,128)(2,1)}, bf16[512,2048]{1,0:T(8,128)(2,1)}, u32[]{:S(2)}, u32[]{:S(2)}) collective-permute-start(bf16[512,2048]{1,0:T(8,128)(2,1)} %constant_dynamic-slice_fusion), channel_id=1, source_target_pairs={{0,4},{4,0},{8,12},{12,8},{16,20},{20,16},{24,28},{28,24},{1,5},{5... | collective-permute-start | bytes 6291464 | tf_op jit(solution)/shard_map/ppermute | solution.py:1347
  529.8 8.9 %collective-permute-start.2 = (bf16[512,2048]{1,0:T(8,128)(2,1)}, bf16[512,2048]{1,0:T(8,128)(2,1)}, u32[]{:S(2)}, u32[]{:S(2)}) collective-permute-start(bf16[512,2048]{1,0:T(8,128)(2,1)} %constant_dynamic-slice_fusion.1), channel_id=1, source_target_pairs={{0,4},{4,0},{8,12},{12,8},{16,20},{20,16},{24,28},{28,24},{1,5},{5... | collective-permute-start | bytes 6291464 | tf_op jit(solution)/shard_map/ppermute | solution.py:1347
Sparse Core Ops, SparseCore 0:
  11.3 56.9 all-gather.31
  77.4 55.9 all-gather.17
  135.3 54.3 all-gather.15
  306.0 69.9 reduce-scatter.14
  379.3 109.0 reduce-scatter.16
